TPU v7x, 32 devices: a whole 2x2x4 slice. The times are simulated.
32 devices in a mesh: row: 8 (over y, x, core), depth: 4 (over z).
Axes of the slice: x: 2, y: 2, z: 4, core: 2. Of those that a mesh axis runs over, the one named last changes fastest.
Arguments:
- l_cores: float32 [16, 32, 384, 384], P('row', 'depth'), may hold values from -0.0546875 to 0.0546875
- l_bucket: int32 [16, 32], P('row', 'depth'), may hold values from 1 to 3
- present: int32 [16, 32], P('row', 'depth'), may hold values 0 or 1
- u_cores: float32 [32, 4, 384, 384], P('depth', None, 'row'), may hold values from -6 to 6
- u_bucket: int32 [32, 4], P('depth'), may hold values from 1 to 3
- diag_cores: float32 [16, 4, 384, 384], P('row', None, 'depth'), may hold values from -6 to 6
- pivot_inv: float32 [4, 384, 384], P(None, 'row'), may hold values from -0.3125 to 0.3125
- coupling: float32 [3, 384, 384], P(None, 'row'), may hold values from -0.21875 to 0.21875
Outputs:
- finished: float32 [16, 4, 384, 384], P('row', None, 'depth')
Inputs may be any that keep to these rules, and one draw needn't show every extreme that they name: A lower tile's core rank is l_bucket * 128. An upper tile's core rank is u_bucket * 128. `present`: 1 marks a nonzero lower tile.
All inputs are finite; a program needn't handle non-finite values. No bound on the sum of `present` on one device may be relied on, other than what follows from the above.
Results may differ from a plain program's by a relative error of at most 0.0003.
Values sent between devices are 32-bit elements; how exact they have to be, the bound alone decides.
No kernel may reach another device: no remote copies, remote signals or barrier semaphores. Data moves between devices by JAX's collectives and lax.ppermute only.
A program may use at most 128 MiB of HBM per device.

v0:
```python
import jax
import jax.numpy as jnp
from jax import lax
from jax.sharding import PartitionSpec as P

HIGH = lax.Precision.HIGHEST


def per_device(l_cores, l_bucket, present, u_cores, u_bucket, diag_cores, pivot_inv, coupling):
    width = l_cores.shape[-1]
    rank_step = width // 3
    share_rows = diag_cores.shape[2]
    pivots, links = (
        lax.all_gather(pivot_inv, "row", axis=1, tiled=True),
        lax.all_gather(coupling, "row", axis=1, tiled=True),
    )
    positions = jnp.arange(width, dtype=jnp.int32)
    col_keep = (
        (positions[None, None, :] < (l_bucket * rank_step)[:, :, None]) & (present[:, :, None] > 0)
    ).astype(jnp.float32)
    l_masked = l_cores * col_keep[:, :, None, :]
    u_limits = u_bucket * rank_step
    portion = lax.all_gather(u_cores, "row", axis=2, tiled=True)
    count_rows = portion.shape[2]
    row_ids = jnp.arange(count_rows, dtype=jnp.int32)
    row_mask = (row_ids[None, None, :] < u_limits[:, :, None]).astype(jnp.float32)
    u_masked = portion * row_mask[..., None]
    partial_update = jnp.einsum("ikar,kjrb->ijab", l_masked, u_masked, precision=HIGH)
    summed = lax.psum(partial_update, "depth")
    own_rows = lax.dynamic_slice_in_dim(summed, lax.axis_index("depth") * share_rows, share_rows, 2)
    reduced = diag_cores - own_rows
    previous = jnp.einsum("iab,bc->iac", reduced[:, 0], pivots[0], precision=HIGH)
    results = [previous]
    for column in range(1, reduced.shape[1]):
        linked = jnp.einsum("iab,bc->iac", previous, links[column - 1], precision=HIGH)
        previous = jnp.einsum(
            "iab,bc->iac", reduced[:, column] - linked, pivots[column], precision=HIGH
        )
        results.append(previous)
    return jnp.stack(results, axis=1)


def solution(mesh):
    in_specs = (
        P("row", "depth", None, None),
        P("row", "depth"),
        P("row", "depth"),
        P("depth", None, "row", None),
        P("depth", None),
        P("row", None, "depth", None),
        P(None, "row", None),
        P(None, "row", None),
    )
    out_specs = P("row", None, "depth", None)
    return jax.shard_map(
        per_device, mesh=mesh, in_specs=in_specs, out_specs=out_specs, check_vma=False
    )
```

profile of v0, /device:TPU:0, one launch (start us, length us, event | category | flops | bytes accessed | tf_op | source)
XLA Modules:
  0.0 453.8 jit_solution(7917406552698786464)
XLA Ops:
  6.5 0.0 copy-start.2
  6.5 0.0 copy-start.4
  6.5 0.0 copy-start.3
  6.5 0.0 all-gather.4.cloned.1.call-start
  6.5 0.7 all-gather.4.cloned.1.call-update
  7.3 0.0 all-reduce.2.cloned.1.call-start
  7.3 0.0 copy-done.2
  7.3 0.1 copy.9
  7.4 0.0 copy-done.4
  7.4 0.0 copy-done.3
  7.4 0.1 fusion.15
  7.5 0.1 fusion.13
  7.6 103.0 %all-gather.4.cloned.1.call-done = f32[8,4,384,384]{3,2,1,0:T(8,128)} async-done(((f32[8,4,48,384]{3,2,1,0:T(8,128)}), f32[8,4,384,384]{3,2,1,0:T(8,128)}) %all-gather.4.cloned.1.call-update) | async-done | bytes 18874384 | tf_op jit(solution)/shard_map/all_gather | solution.py:23
  110.6 94.9 %fusion.5 = f32[2,4,384,384]{2,3,0,1:T(8,128)} fusion(f32[2,8,384,384]{3,2,1,0:T(8,128)} %param.8, f32[2,8,384]{2,1,0:T(8,128)S(1)} %fusion.15, f32[8,4,384,384]{3,2,1,0:T(8,128)} %all-gather.4.cloned.1.call-done, f32[8,4,384]{2,1,0:T(4,128)S(1)} %fusion.13), kind=kOutput, calls=%fused_computation.6 | convolution fusion | flops 43493621760 | bytes 33103872 | tf_op jit(solution)/shard_map/ikar,kjrb->ijab/dot_general | solution.py:28
  205.5 0.0 copy-start.1
  205.5 0.0 all-reduce.2.cloned.1.call-update
  205.5 0.0 all-gather.6.cloned.1.call-start
  205.6 0.7 all-gather.6.cloned.1.call-update
  206.3 0.0 all-gather.8.cloned.1.call-start
  206.3 0.5 all-gather.8.cloned.1.call-update
  206.9 0.0 copy-done.1
  206.9 0.5 copy.11
  207.3 170.3 %all-reduce.2.cloned.1.call-done = f32[2,4,384,384]{2,3,0,1:T(8,128)} async-done(((f32[2,4,384,384]{2,3,0,1:T(8,128)}), f32[2,4,384,384]{2,3,0,1:T(8,128)}) %all-reduce.2.cloned.1.call-update) | async-done | bytes 4718608 | tf_op jit(solution)/shard_map/psum | solution.py:29
  377.6 2.4 dynamic-slice_subtract_fusion
  380.0 27.4 %all-gather.6.cloned.1.call-done = f32[4,384,384]{2,1,0:T(8,128)} async-done(((f32[4,48,384]{2,1,0:T(8,128)}), f32[4,384,384]{2,1,0:T(8,128)}) %all-gather.6.cloned.1.call-update) | async-done | bytes 2359312 | tf_op jit(solution)/shard_map/all_gather | solution.py:14
  407.4 1.9 fusion.12
  409.4 26.3 %all-gather.8.cloned.1.call-done = f32[3,384,384]{2,1,0:T(8,128)} async-done(((f32[3,48,384]{2,1,0:T(8,128)}), f32[3,384,384]{2,1,0:T(8,128)}) %all-gather.8.cloned.1.call-update) | async-done | bytes 1769488 | tf_op jit(solution)/shard_map/all_gather | solution.py:15
  435.6 0.0 copy-start
  435.6 2.3 convolution_subtract_fusion.2
  437.9 2.0 fusion.11
  439.9 2.2 convolution_subtract_fusion.1
  442.1 0.0 copy-done
  442.1 0.9 fusion.10
  443.0 2.2 convolution_subtract_fusion
  445.2 0.9 convolution_bitcast_fusion
  446.1 0.1 pad_maximum_fusion
  446.2 1.1 copy.16
  (3 shorter events, 0.0 us)
Async XLA Ops:
  6.5 0.8 copy-start.2
  6.5 0.9 copy-start.4
  6.5 0.9 copy-start.3
  6.5 104.1 %all-gather.4.cloned.1.call-start = ((), (), s32[]{:S(2)}) async-start(), calls=%async_computation | async-start | bytes 21233664 | tf_op jit(solution)/shard_map/all_gather | solution.py:23
  7.3 370.4 %all-reduce.2.cloned.1.call-start = ((), (), s32[]{:S(2)}) async-start(), calls=%async_computation.1 | async-start | bytes 9437184 | tf_op jit(solution)/shard_map/psum | solution.py:29
  205.5 1.3 copy-start.1
  205.5 201.9 %all-gather.6.cloned.1.call-start = ((), (), s32[]{:S(2)}) async-start(), calls=%async_computation.2 | async-start | bytes 2654208 | tf_op jit(solution)/shard_map/all_gather | solution.py:14
  206.3 229.3 %all-gather.8.cloned.1.call-start = ((), (), s32[]{:S(2)}) async-start(), calls=%async_computation.3 | async-start | bytes 1990656 | tf_op jit(solution)/shard_map/all_gather | solution.py:15
  435.6 6.5 %copy-start = (f32[4,384,384]{2,1,0:T(8,128)S(1)}, f32[4,384,384]{2,1,0:T(8,128)}, u32[]{:S(2)}) copy-start(f32[4,384,384]{2,1,0:T(8,128)} %all-gather.6.cloned.1.call-done) | copy-start | bytes 7077892
Sparse Core Ops, SparseCore 0:
  9.2 101.3 all-gather.3
  205.7 171.9 all-reduce.1
  379.5 27.8 all-gather.5
  409.2 26.3 all-gather.7
where the time goes:
time: 454 us
  waiting for transfers between devices  329 us (72%)
  matrix products  107 us (24%)
  between operations  13.3 us (3%)
    psum x1, waiting for transfers between devices, per_device(): summed = lax.psum(partial_update, 'depth')  170 us
    all_gather x1, waiting for transfers between devices, per_device(): portion = lax.all_gather(u_cores, 'row', axis=2, tiled=True)  103 us
    dot_general x1, matrix products, per_device(): jnp.einsum('ikar,kjrb->ijab', l_masked, u_masked, precision=HIGH)  94.9 us
    all_gather x1, waiting for transfers between devices, per_device(): lax.all_gather(pivot_inv, 'row', axis=1, tiled=True)  27.4 us
    all_gather x1, waiting for transfers between devices, per_device(): lax.all_gather(coupling, 'row', axis=1, tiled=True)  26.3 us
  transfers between devices with their start and end apart: 4, of which 4 were waited for; matrix products, arithmetic and copies ran while one was open for 1% of the time, Pallas kernels for 0%

commit v1 on v0

v1 whole, which is shorter than its diff:
```python
import functools

import jax
import jax.numpy as jnp
from jax import lax
from jax.experimental import pallas as pl
from jax.experimental.pallas import tpu as pltpu
from jax.sharding import PartitionSpec as P


HIGH = lax.Precision.HIGHEST
F32 = jnp.float32
BF16 = jnp.bfloat16


def plain_device(l_cores, l_bucket, present, u_cores, u_bucket, diag_cores, pivot_inv, coupling):
    width = l_cores.shape[-1]
    rank_step = width // 3
    pivots, links = (
        lax.all_gather(pivot_inv, "row", axis=1, tiled=True),
        lax.all_gather(coupling, "row", axis=1, tiled=True),
    )
    positions = jnp.arange(width, dtype=jnp.int32)
    col_keep = (
        (positions[None, None, :] < (l_bucket * rank_step)[:, :, None]) & (present[:, :, None] > 0)
    ).astype(F32)
    l_masked = l_cores * col_keep[:, :, None, :]
    portion = lax.all_gather(u_cores, "row", axis=2, tiled=True)
    row_mask = (positions[None, None, :] < (u_bucket * rank_step)[:, :, None]).astype(F32)
    u_masked = portion * row_mask[..., None]
    partial_update = jnp.einsum("ikar,kjrb->ijab", l_masked, u_masked, precision=HIGH)
    own_rows = lax.psum_scatter(partial_update, "depth", scatter_dimension=2, tiled=True)
    reduced = diag_cores - own_rows
    previous = jnp.einsum("iab,bc->iac", reduced[:, 0], pivots[0], precision=HIGH)
    results = [previous]
    for column in range(1, reduced.shape[1]):
        linked = jnp.einsum("iab,bc->iac", previous, links[column - 1], precision=HIGH)
        previous = jnp.einsum(
            "iab,bc->iac", reduced[:, column] - linked, pivots[column], precision=HIGH
        )
        results.append(previous)
    return jnp.stack(results, axis=1)


def halves(value):
    high = value.astype(BF16)
    return high, (value - high.astype(F32)).astype(BF16)


def dot3(left, right_high, right_low):
    high, low = left
    dot = functools.partial(jnp.dot, preferred_element_type=F32)
    return dot(high, right_high) + (dot(high, right_low) + dot(low, right_high))


def split_lower(l_cores, l_bucket, present):
    tiles, pivots, width, _ = l_cores.shape
    step = width // 3

    def body(bucket, flags, source, high, low):
        i = pl.program_id(1)
        lane = lax.broadcasted_iota(jnp.int32, (width, width), 1)
        for side in range(2):
            k = 2 * pl.program_id(0) + side
            limit = jnp.where(flags[i, k] > 0, bucket[i, k] * step, 0)
            a, b = halves(jnp.where(lane < limit, source[0, side], 0.0))
            high[0, :, side * width : (side + 1) * width] = a
            low[0, :, side * width : (side + 1) * width] = b

    out = jax.ShapeDtypeStruct((pivots // 2, tiles * width, 2 * width), BF16)
    block = pl.BlockSpec((1, width, 2 * width), lambda p, i, *_: (p, i, 0))
    return pl.pallas_call(
        body,
        grid_spec=pltpu.PrefetchScalarGridSpec(
            num_scalar_prefetch=2,
            grid=(pivots // 2, tiles),
            in_specs=[pl.BlockSpec((1, 2, width, width), lambda p, i, *_: (i, p, 0, 0))],
            out_specs=[block, block],
        ),
        out_shape=[out, out],
        name="split_lower",
    )(l_bucket, present, l_cores)


def pack(own, twin, place):
    pivots, columns, rows, width = own.shape
    half = pivots // 2

    def body(at, mine, other, *outs):
        core = at[0] % 2
        for column in range(columns):
            outs[column][core] = mine[:, column]
            outs[column][1 - core] = other[:, column]

    source = pl.BlockSpec((1, columns, rows, width), lambda k, at: (half * (at[0] % 2) + k, 0, 0, 0))
    return pl.pallas_call(
        body,
        grid_spec=pltpu.PrefetchScalarGridSpec(
            num_scalar_prefetch=1,
            grid=(half,),
            in_specs=[source, source],
            out_specs=[pl.BlockSpec((2, 1, rows, width), lambda k, at: (0, k, 0, 0))] * columns,
        ),
        out_shape=[jax.ShapeDtypeStruct((2, half, rows, width), F32)] * columns,
        name="pack",
    )(place, own, twin)


def sources(at, bundle):
    home = at[0] - at[0] % 2
    first = jnp.where(bundle == 0, home ^ 2, home ^ 4)
    second = jnp.where(bundle == 0, home ^ 4, home ^ 2)
    return first, second, home ^ 6


def gather_tile(at, bundle, own, twin, parts, store):
    store(at[0], own)
    store(at[0] ^ 1, twin)
    for chip, part in zip(sources(at, bundle), parts):
        for core in range(2):
            store(chip + core, part(core))


def multiply(j, place, u_bucket, lower, own, twin, mine, theirs):
    high, low = lower
    pairs, height, depth = high.shape
    rows, width = own.shape[-2:]
    tiles = height // width
    step = width // 3
    half = pairs // 2
    share = width // 4

    def body(at, bucket, lhs_high, lhs_low, own_ref, twin_ref, *rest):
        parts, others = rest[:3], rest[3:6]
        keep, send, rhs_high, rhs_low, total = rest[6:]
        p = pl.program_id(0)
        core = at[0] % 2
        row = lax.broadcasted_iota(jnp.int32, (rows, width), 0)

        def assemble(refs, bundle):
            for k in range(2):
                limit = bucket[2 * p + k, j] * step

                def store(device, value):
                    start = pl.multiple_of(device * rows, 16)
                    value = jnp.where(row < limit - start, value, 0.0)
                    a, b = halves(value)
                    rhs_high[pl.ds(k * width + start, rows)] = a
                    rhs_low[pl.ds(k * width + start, rows)] = b

                gather_tile(
                    at, bundle, own_ref[k, 0], twin_ref[k, 0],
                    [lambda s, r=r: r[s, k] for r in refs], store,
                )

        @pl.when(p // half == core)
        def _():
            assemble(parts, core)

        @pl.when(p // half != core)
        def _():
            assemble(others, 1 - core)

        left = lhs_high[0], lhs_low[0]
        product = jnp.dot(
            jnp.concatenate([left[0], left[1], left[0]], axis=1),
            jnp.concatenate([rhs_high[...], rhs_high[...], rhs_low[...]], axis=0),
            preferred_element_type=F32,
        )

        @pl.when(p == 0)
        def _():
            total[...] = product

        @pl.when(p > 0)
        def _():
            total[...] += product

        @pl.when(p == pairs - 1)
        def _():
            z = at[1]
            for slot, (target, block) in enumerate(((keep, z), (keep, z ^ 2), (send, z ^ 1), (send, z ^ 3))):
                for i in range(tiles):
                    start = pl.multiple_of(block * share, 8)
                    target[slot % 2, i] = total[pl.ds(i * width + start, share)]

    lhs = pl.BlockSpec((1, height, depth), lambda p, *_: (p, 0, 0))
    local = pl.BlockSpec((2, 1, rows, width), lambda p, *_: (p, j, 0, 0))
    piece = pl.BlockSpec((2, 2, rows, width), lambda p, *_: (0, p % half, 0, 0))
    out = pl.BlockSpec((2, tiles, share, width), lambda p, *_: (0, 0, 0, 0))
    shape = jax.ShapeDtypeStruct((2, tiles, share, width), F32)
    return pl.pallas_call(
        body,
        grid_spec=pltpu.PrefetchScalarGridSpec(
            num_scalar_prefetch=2,
            grid=(pairs,),
            in_specs=[lhs, lhs, local, local] + [piece] * 6,
            out_specs=[out, out],
            scratch_shapes=[
                pltpu.VMEM((depth, width), BF16),
                pltpu.VMEM((depth, width), BF16),
                pltpu.VMEM((height, width), F32),
            ],
        ),
        out_shape=[shape, shape],
    )(place, u_bucket, high, low, own, twin, *mine, *theirs)


def finish_early(place, columns, diag, sums, own, twin, mine, theirs):
    tiles, _, share, width = diag.shape
    rows = own.shape[-2]
    half = own.shape[0] // 2
    height = tiles * share

    def body(at, *refs):
        diag_ref = refs[0]
        parts = refs[1 : 1 + 3 * (columns - 1)]
        refs = refs[1 + 3 * (columns - 1) :]
        own_ref, twin_ref, refs = refs[0], refs[1], refs[2:]
        pieces, others, refs = refs[:3], refs[3:6], refs[6:]
        done, linked_ref, last_high, last_low, mat_high, mat_low = refs
        core = at[0] % 2

        def assemble(half_index, refs, bundle):
            for local in range(half):
                k = half_index * half + local
                if k >= 2 * columns - 1:
                    continue

                def store(device, value):
                    start = pl.multiple_of(device * rows, 16)
                    a, b = halves(value)
                    mat_high[k, pl.ds(start, rows)] = a
                    mat_low[k, pl.ds(start, rows)] = b

                gather_tile(
                    at, bundle, own_ref[k, 0], twin_ref[k, 0],
                    [lambda s, r=r: r[s, local] for r in refs], store,
                )

        for half_index in range(2):
            @pl.when(core == half_index)
            def _():
                assemble(half_index, pieces, core)
                assemble(1 - half_index, others, 1 - core)

        linked = None
        for column in range(columns - 1):
            keep, near, far = (parts[3 * column + n] for n in range(3))
            reduced = (diag_ref[:, column] - (keep[0] + near[0] + far[...])).reshape(height, width)
            if linked is not None:
                reduced = reduced - linked
            previous = dot3(halves(reduced), mat_high[column], mat_low[column])
            done[:, column] = previous.reshape(tiles, share, width)
            linked = dot3(halves(previous), mat_high[columns + column], mat_low[columns + column])
        linked_ref[...] = linked.reshape(tiles, share, width)
        last_high[...] = mat_high[columns - 1]
        last_low[...] = mat_low[columns - 1]

    operands = [diag]
    for keep, near, far in sums:
        operands += [keep, near, far]
    operands += [own, twin, *mine, *theirs]
    square = jax.ShapeDtypeStruct((width, width), BF16)
    vmem = pl.BlockSpec(memory_space=pltpu.VMEM)
    return pl.pallas_call(
        body,
        in_specs=[pl.BlockSpec(memory_space=pltpu.SMEM)] + [vmem] * len(operands),
        out_specs=[vmem] * 4,
        out_shape=[
            jax.ShapeDtypeStruct((tiles, columns - 1, share, width), F32),
            jax.ShapeDtypeStruct((tiles, share, width), F32),
            square,
            square,
        ],
        scratch_shapes=[pltpu.VMEM((2 * columns - 1, width, width), BF16)] * 2,
        name="finish_early",
    )(place, *operands)


def finish_last(columns, diag, done, linked, last_high, last_low, keep, near, far):
    tiles, _, share, width = diag.shape
    height = tiles * share

    def body(diag_ref, done_ref, linked_ref, high, low, keep_ref, near_ref, far_ref, out):
        for column in range(columns - 1):
            out[:, column] = done_ref[:, column]
        reduced = diag_ref[:, columns - 1] - (keep_ref[0] + near_ref[0] + far_ref[...]) - linked_ref[...]
        value = dot3(halves(reduced.reshape(height, width)), high[...], low[...])
        out[:, columns - 1] = value.reshape(tiles, share, width)

    return pl.pallas_call(
        body,
        in_specs=[pl.BlockSpec(memory_space=pltpu.VMEM)] * 8,
        out_specs=pl.BlockSpec(memory_space=pltpu.VMEM),
        out_shape=jax.ShapeDtypeStruct(diag.shape, F32),
        name="finish_last",
    )(diag, done, linked, last_high, last_low, keep, near, far)


def moves(size, first_of_core):
    return [(d, d ^ first_of_core[d % 2]) for d in range(size)]


def cube_device(l_cores, l_bucket, present, u_cores, u_bucket, diag_cores, pivot_inv, coupling):
    columns = u_cores.shape[1]
    size = lax.axis_size("row")
    first = functools.partial(lax.ppermute, axis_name="row", perm=moves(size, (2, 4)))
    second = functools.partial(lax.ppermute, axis_name="row", perm=moves(size, (4, 2)))
    twin_of = functools.partial(lax.ppermute, axis_name="row", perm=moves(size, (1, 1)))
    deep = lax.axis_size("depth")
    near_of = functools.partial(lax.ppermute, axis_name="depth", perm=[(z, z ^ 1) for z in range(deep)])
    far_of = functools.partial(lax.ppermute, axis_name="depth", perm=[(z, z ^ 2) for z in range(deep)])
    place = jnp.stack([lax.axis_index("row"), lax.axis_index("depth")]).astype(jnp.int32)

    u_twin = twin_of(u_cores)
    small = jnp.concatenate([pivot_inv, coupling, pivot_inv[:1]], axis=0)[:, None]
    small_twin = twin_of(small)
    bundles = pack(u_cores, u_twin, place)
    lower = split_lower(l_cores, l_bucket, present)
    bundles += pack(small, small_twin, place)

    gathered = []
    for bundle in bundles:
        a = first(bundle)
        b = second(bundle)
        c = second(a)
        twins = tuple(twin_of(v) for v in (a, b, c))
        gathered.append(((a, b, c), twins))

    sums = []
    for j in range(columns):
        keep, send = multiply(j, place, u_bucket, lower, u_cores, u_twin, *gathered[j])
        near = near_of(send)
        far = far_of(keep[1] + near[1])
        sums.append((keep, near, far))
    done, linked, last_high, last_low = finish_early(
        place, columns, diag_cores, sums[:-1], small, small_twin, *gathered[columns],
    )
    return finish_last(columns, diag_cores, done, linked, last_high, last_low, *sums[-1])


def solution(mesh):
    in_specs = (
        P("row", "depth", None, None),
        P("row", "depth"),
        P("row", "depth"),
        P("depth", None, "row", None),
        P("depth", None),
        P("row", None, "depth", None),
        P(None, "row", None),
        P(None, "row", None),
    )
    out_specs = P("row", None, "depth", None)

    cube = mesh.shape["row"] == 8 and mesh.shape["depth"] == 4
    return jax.shard_map(
        cube_device if cube else plain_device,
        mesh=mesh, in_specs=in_specs, out_specs=out_specs, check_vma=False,
    )
```

time: 454 us -> 236 us (0.52)
  waiting for transfers between devices: 329 us -> 107 us
  matrix products: 107 us -> 0 us
  Pallas kernels: 0 us -> 86.8 us
  starting transfers between devices: 0.12 us -> 31.8 us
  between operations: 13.3 us -> 0.35 us
  local copies, waits for them, and re-layouts: 1.65 us -> 6.23 us
    psum x1 -> x0, waiting for transfers between devices: 170 us -> none  [per_device(): summed = lax.psum(partial_update, 'depth')]
    all_gather x3 -> x0, waiting for transfers between devices: 157 us -> none  [the longest x1 103 us: per_device(): portion = lax.all_gather(u_cores, 'row', axis=2, tiled=True)]
    dot_general x8 -> x0, matrix products: 107 us -> none  [the longest x1 94.9 us: per_device(): jnp.einsum('ikar,kjrb->ijab', l_masked, u_masked, precision=HIGH)]
    ppermute x0 -> x40, waiting for transfers between devices: none -> 107 us  [the longest x5 45.5 us: cube_device(): a = first(bundle)]
    pallas_call x0 -> x9, Pallas kernels: none -> 86.8 us  [the longest x4 55.6 us: multiply(): pl.pallas_call(body, grid_spec=pltpu.PrefetchScalarGridSpec(num_scalar_pr...]
    ppermute x0 -> x40, starting transfers between devices: none -> 31.8 us  [the longest x5 6.73 us: cube_device(): b = second(bundle)]
    unnamed x11 -> x67, local copies, waits for them, and re-layouts: 0.48 us -> 5.34 us
  transfers between devices with their start and end apart: 4 -> 40, of which waited for: 4 -> 12; matrix products, arithmetic and copies ran while one was open for 1% -> 2% of each run, Pallas kernels for 0% -> 35%
where the time goes in v1:
time: 236 us; the launch traced here: 235 us
  waiting for transfers between devices  107 us (45%)
  Pallas kernels  86.8 us (37%)
  starting transfers between devices  31.8 us (13%)
  local copies, waits for them, and re-layouts  6.23 us (3%)
  other arithmetic  2.93 us (1%)
    pallas_call x4, Pallas kernels, multiply(): pl.pallas_call(body, grid_spec=pltpu.PrefetchScalarGridSpec(num_scalar_pr...  55.6 us
    ppermute x5, waiting for transfers between devices, cube_device(): a = first(bundle)  45.5 us
    ppermute x4, waiting for transfers between devices, cube_device(): near = near_of(send)  23.3 us
    ppermute x5, waiting for transfers between devices, cube_device(): c = second(a)  18.1 us
    ppermute x4, waiting for transfers between devices, cube_device(): far = far_of(keep[1] + near[1])  17.5 us
    pallas_call x1, Pallas kernels, split_lower(): pl.pallas_call(body, grid_spec=pltpu.PrefetchScalarGridSpec(num_scalar_pr...  10.7 us
    pallas_call x1, Pallas kernels, finish_early(): pl.pallas_call(body, in_specs=[pl.BlockSpec(memory_space=pltpu.SMEM)] + [...  8.44 us
    pallas_call x2, Pallas kernels, pack(): pl.pallas_call(body, grid_spec=pltpu.PrefetchScalarGridSpec(num_scalar_pr...  8.41 us
  transfers between devices with their start and end apart: 40, of which 12 were waited for; matrix products, arithmetic and copies ran while one was open for 2% of the time, Pallas kernels for 35%

profile of v1, /device:TPU:0, one launch (start us, length us, event | category | flops | bytes accessed | tf_op | source)
XLA Modules:
  0.0 235.0 jit_solution(6761725797611822939)
XLA Ops:
  0.0 0.5 collective-permute-start
  0.5 0.9 slice.33
  1.4 1.1 maximum_bitcast_fusion.mine.refs_10_
  2.5 0.1 collective-permute-start.25
  2.6 0.7 pad_add_fusion.at
  3.3 2.4 %collective-permute-done.25.other.refs_11_ = f32[8,1,48,384]{3,2,1,0:T(8,128)S(1)} collective-permute-done((f32[8,1,48,384]{3,2,1,0:T(8,128)S(1)}, f32[8,1,48,384]{3,2,1,0:T(8,128)S(1)}, u32[]{:S(2)}, u32[]{:S(2)}) %collective-permute-start.25) | collective-permute-done | bytes 589856 | tf_op jit(solution)/shard_map/ppermute | solution.py:318
  5.7 0.8 copy-done.2
  6.5 3.9 %pack.3 = f32[2,4,48,384]{3,2,1,0:T(8,128)} custom-call(s32[2]{0:T(128)} %pad_add_fusion.at, f32[8,1,48,384]{3,2,1,0:T(8,128)} %copy-done.1, f32[8,1,48,384]{3,2,1,0:T(8,128)} %copy-done.2), custom_call_target="tpu_custom_call" | custom-call | tf_op jit(solution)/shard_map/pack/pallas_call | solution.py:96
  10.4 2.8 %collective-permute-start.26 = (f32[2,4,48,384]{3,2,1,0:T(8,128)}, f32[2,4,48,384]{3,2,1,0:T(8,128)}, u32[]{:S(2)}, u32[]{:S(2)}) collective-permute-start(f32[2,4,48,384]{3,2,1,0:T(8,128)} %pack.3), channel_id=1, source_target_pairs={{0,8},{4,20},{8,0},{12,28},{16,24},{20,4},{24,16},{28,12},{1,9},{5... | collective-permute-start | bytes 1769480 | tf_op jit(solution)/shard_map/ppermute | solution.py:325
  13.3 1.4 copy-done
  14.7 4.5 %pack.2 = (f32[2,4,48,384]{3,2,1,0:T(8,128)}, f32[2,4,48,384]{3,2,1,0:T(8,128)}, f32[2,4,48,384]{3,2,1,0:T(8,128)}, f32[2,4,48,384]{3,2,1,0:T(8,128)}) custom-call(s32[2]{0:T(128)} %pad_add_fusion.at, f32[8,4,48,384]{3,2,1,0:T(8,128)} %own_ref.7, f32[8,4,48,384]{3,2,1,0:T(8,128)} %copy-done), custom_call_target="tpu_custom_call" | custom-call | tf_op jit(solution)/shard_map/pack/pallas_call | solution.py:96
  19.2 2.0 collective-permute-start.33
  21.3 1.5 collective-permute-start.17
  22.8 0.5 collective-permute-start.18
  23.3 0.2 collective-permute-start.9
  23.5 12.2 %collective-permute-done.32.rest_0_ = f32[2,4,48,384]{3,2,1,0:T(8,128)S(1)} collective-permute-done((f32[2,4,48,384]{3,2,1,0:T(8,128)}, f32[2,4,48,384]{3,2,1,0:T(8,128)S(1)}, u32[]{:S(2)}, u32[]{:S(2)}) %collective-permute-start.32) | collective-permute-done | bytes 589856 | tf_op jit(solution)/shard_map/ppermute | solution.py:325
  35.6 1.5 collective-permute-start.10
  37.2 0.5 collective-permute-start.1
  37.7 10.6 %collective-permute-done.17.rest_0_ = f32[2,4,48,384]{3,2,1,0:T(8,128)S(1)} collective-permute-done((f32[2,4,48,384]{3,2,1,0:T(8,128)}, f32[2,4,48,384]{3,2,1,0:T(8,128)S(1)}, u32[]{:S(2)}, u32[]{:S(2)}) %collective-permute-start.17) | collective-permute-done | bytes 589856 | tf_op jit(solution)/shard_map/ppermute | solution.py:325
  48.3 1.5 collective-permute-start.2
  49.8 0.5 collective-permute-start.34
  50.3 10.6 %collective-permute-done.9.rest_0_ = f32[2,4,48,384]{3,2,1,0:T(8,128)S(1)} collective-permute-done((f32[2,4,48,384]{3,2,1,0:T(8,128)}, f32[2,4,48,384]{3,2,1,0:T(8,128)S(1)}, u32[]{:S(2)}, u32[]{:S(2)}) %collective-permute-start.9) | collective-permute-done | bytes 589856 | tf_op jit(solution)/shard_map/ppermute | solution.py:325
  61.0 0.5 collective-permute-start.36
  61.4 12.1 %collective-permute-done.1.rest_0_ = f32[2,4,48,384]{3,2,1,0:T(8,128)S(1)} collective-permute-done((f32[2,4,48,384]{3,2,1,0:T(8,128)}, f32[2,4,48,384]{3,2,1,0:T(8,128)S(1)}, u32[]{:S(2)}, u32[]{:S(2)}) %collective-permute-start.1) | collective-permute-done | bytes 589856 | tf_op jit(solution)/shard_map/ppermute | solution.py:325
  73.6 1.5 collective-permute-start.19
  75.1 3.7 %collective-permute-done.34.rest_2_ = f32[2,4,48,384]{3,2,1,0:T(8,128)S(1)} collective-permute-done((f32[2,4,48,384]{3,2,1,0:T(8,128)S(1)}, f32[2,4,48,384]{3,2,1,0:T(8,128)S(1)}, u32[]{:S(2)}, u32[]{:S(2)}) %collective-permute-start.34) | collective-permute-done | bytes 589856 | tf_op jit(solution)/shard_map/ppermute | solution.py:327
  78.8 0.2 collective-permute-start.21
  79.0 1.7 collective-permute-start.11
  80.7 4.4 %collective-permute-done.19.rest_2_ = f32[2,4,48,384]{3,2,1,0:T(8,128)S(1)} collective-permute-done((f32[2,4,48,384]{3,2,1,0:T(8,128)S(1)}, f32[2,4,48,384]{3,2,1,0:T(8,128)S(1)}, u32[]{:S(2)}, u32[]{:S(2)}) %collective-permute-start.19) | collective-permute-done | bytes 589856 | tf_op jit(solution)/shard_map/ppermute | solution.py:327
  85.1 0.3 collective-permute-start.13
  85.4 1.7 collective-permute-start.3
  87.1 4.4 %collective-permute-done.11.rest_2_ = f32[2,4,48,384]{3,2,1,0:T(8,128)} collective-permute-done((f32[2,4,48,384]{3,2,1,0:T(8,128)S(1)}, f32[2,4,48,384]{3,2,1,0:T(8,128)}, u32[]{:S(2)}, u32[]{:S(2)}) %collective-permute-start.11) | collective-permute-done | bytes 589856 | tf_op jit(solution)/shard_map/ppermute | solution.py:327
  91.5 0.2 collective-permute-start.4
  91.7 0.3 collective-permute-start.14
  92.1 0.2 collective-permute-start.5
  92.2 5.6 %collective-permute-done.3.rest_2_ = f32[2,4,48,384]{3,2,1,0:T(8,128)} collective-permute-done((f32[2,4,48,384]{3,2,1,0:T(8,128)S(1)}, f32[2,4,48,384]{3,2,1,0:T(8,128)}, u32[]{:S(2)}, u32[]{:S(2)}) %collective-permute-start.3) | collective-permute-done | bytes 589856 | tf_op jit(solution)/shard_map/ppermute | solution.py:327
  97.9 0.1 collective-permute-start.6
  98.1 0.9 copy-done.26
  98.9 0.4 collective-permute-start.37
  99.3 0.7 copy.9.bucket
  100.0 10.7 %split_lower.1 = (bf16[4,768,768]{2,1,0:T(8,128)(2,1)}, bf16[4,768,768]{2,1,0:T(8,128)(2,1)}) custom-call(s32[2,8]{1,0:T(2,128)} %bucket.5, s32[2,8]{1,0:T(2,128)} %flags.1, f32[2,8,384,384]{3,2,1,0:T(8,128)} %source.1), custom_call_target="tpu_custom_call" | custom-call | tf_op jit(solution)/shard_map/split_lower/pallas_call | solution.py:72
  110.7 13.9 %shard_map.84 = (f32[2,2,96,384]{3,2,1,0:T(8,128)}, f32[2,2,96,384]{3,2,1,0:T(8,128)}) custom-call(s32[2]{0:T(128)} %pad_add_fusion.at, s32[8,4]{1,0:T(8,128)} %copy.9.bucket, bf16[4,768,768]{2,1,0:T(8,128)(2,1)} %get-tuple-element.23.lhs_high, bf16[4,768,768]{2,1,0:T(8,128)(2,1)} %get-tuple-element.24.lhs_low, f32[8,4,48,384]{3,2,1,0:T(8,128)} %own_ref.7, ...), custom_call_target="tpu_custom_call" | custom-call | tf_op jit(solution)/shard_map/pallas_call | solution.py:192
  124.6 1.1 collective-permute-start.27
  125.7 1.6 collective-permute-start.23
  127.3 13.9 %shard_map.83 = (f32[2,2,96,384]{3,2,1,0:T(8,128)}, f32[2,2,96,384]{3,2,1,0:T(8,128)}) custom-call(s32[2]{0:T(128)} %pad_add_fusion.at, s32[8,4]{1,0:T(8,128)} %copy.9.bucket, bf16[4,768,768]{2,1,0:T(8,128)(2,1)} %get-tuple-element.23.lhs_high, bf16[4,768,768]{2,1,0:T(8,128)(2,1)} %get-tuple-element.24.lhs_low, f32[8,4,48,384]{3,2,1,0:T(8,128)} %own_ref.7, ...), custom_call_target="tpu_custom_call" | custom-call | tf_op jit(solution)/shard_map/pallas_call | solution.py:192
  141.2 1.0 collective-permute-start.28
  142.3 0.4 collective-permute-start.15
  142.7 13.9 %shard_map.82 = (f32[2,2,96,384]{3,2,1,0:T(8,128)}, f32[2,2,96,384]{3,2,1,0:T(8,128)}) custom-call(s32[2]{0:T(128)} %pad_add_fusion.at, s32[8,4]{1,0:T(8,128)} %copy.9.bucket, bf16[4,768,768]{2,1,0:T(8,128)(2,1)} %get-tuple-element.23.lhs_high, bf16[4,768,768]{2,1,0:T(8,128)(2,1)} %get-tuple-element.24.lhs_low, f32[8,4,48,384]{3,2,1,0:T(8,128)} %own_ref.7, ...), custom_call_target="tpu_custom_call" | custom-call | tf_op jit(solution)/shard_map/pallas_call | solution.py:192
  156.6 1.6 collective-permute-start.7
  158.3 13.9 %shard_map.85 = (f32[2,2,96,384]{3,2,1,0:T(8,128)}, f32[2,2,96,384]{3,2,1,0:T(8,128)}) custom-call(s32[2]{0:T(128)} %pad_add_fusion.at, s32[8,4]{1,0:T(8,128)} %copy.9.bucket, bf16[4,768,768]{2,1,0:T(8,128)(2,1)} %get-tuple-element.23.lhs_high, bf16[4,768,768]{2,1,0:T(8,128)(2,1)} %get-tuple-element.24.lhs_low, f32[8,4,48,384]{3,2,1,0:T(8,128)} %own_ref.7, ...), custom_call_target="tpu_custom_call" | custom-call | tf_op jit(solution)/shard_map/pallas_call | solution.py:192
  172.2 0.1 collective-permute-start.29
  172.3 0.5 collective-permute-start.38
  172.9 0.2 collective-permute-start.30
  173.1 0.4 collective-permute-start.31
  173.5 2.7 %collective-permute-start.24 = (f32[2,96,384]{2,1,0:T(8,128)S(1)}, f32[2,96,384]{2,1,0:T(8,128)S(1)}, u32[]{:S(2)}, u32[]{:S(2)}) collective-permute-start(f32[2,96,384]{2,1,0:T(8,128)S(1)} %fusion.1), channel_id=1, source_target_pairs={{0,2},{1,3},{2,0},{3,1},{4,6},{5,7},{6,4},{7,5},{8,10},{9,11},{10,... | collective-permute-start | bytes 884744 | tf_op jit(solution)/shard_map/ppermute | solution.py:335
  176.1 1.0 fusion.3
  177.2 0.4 collective-permute-start.16
  177.6 23.3 %collective-permute-done.38.near_ref = f32[2,2,96,384]{3,2,1,0:T(8,128)S(1)} collective-permute-done((f32[2,2,96,384]{3,2,1,0:T(8,128)}, f32[2,2,96,384]{3,2,1,0:T(8,128)S(1)}, u32[]{:S(2)}, u32[]{:S(2)}) %collective-permute-start.38) | collective-permute-done | bytes 589856 | tf_op jit(solution)/shard_map/ppermute | solution.py:334
  200.9 3.0 %collective-permute-start.39 = (f32[2,96,384]{2,1,0:T(8,128)S(1)}, f32[2,96,384]{2,1,0:T(8,128)S(1)}, u32[]{:S(2)}, u32[]{:S(2)}) collective-permute-start(f32[2,96,384]{2,1,0:T(8,128)S(1)} %fusion), channel_id=1, source_target_pairs={{0,2},{1,3},{2,0},{3,1},{4,6},{5,7},{6,4},{7,5},{8,10},{9,11},{10,... | collective-permute-start | bytes 884744 | tf_op jit(solution)/shard_map/ppermute | solution.py:335
  203.9 0.8 copy-done.31
  204.7 17.4 %collective-permute-done.8.refs_3_ = f32[2,96,384]{2,1,0:T(8,128)} collective-permute-done((f32[2,96,384]{2,1,0:T(8,128)S(1)}, f32[2,96,384]{2,1,0:T(8,128)}, u32[]{:S(2)}, u32[]{:S(2)}) %collective-permute-start.8) | collective-permute-done | bytes 294944 | tf_op jit(solution)/shard_map/ppermute | solution.py:335
  222.2 8.4 %finish_early.1 = (f32[2,3,96,384]{3,2,1,0:T(8,128)}, f32[2,96,384]{2,1,0:T(8,128)}, bf16[384,384]{1,0:T(8,128)(2,1)}, bf16[384,384]{1,0:T(8,128)(2,1)}) custom-call(s32[2]{0:T(128)} %pad_add_fusion.at, f32[2,4,96,384]{3,2,1,0:T(8,128)} %diag_ref.1, f32[2,2,96,384]{3,2,1,0:T(8,128)} %get-tuple-element.26.refs_1_, ...), custom_call_target="tpu_custom_call" | custom-call | tf_op jit(solution)/shard_map/finish_early/pallas_call | solution.py:266
  230.6 0.7 copy-done.29
  231.3 3.7 %finish_last.1 = f32[2,4,96,384]{3,2,1,0:T(8,128)} custom-call(f32[2,4,96,384]{3,2,1,0:T(8,128)} %diag_ref.1, f32[2,3,96,384]{3,2,1,0:T(8,128)} %get-tuple-element.34.done_ref, f32[2,96,384]{2,1,0:T(8,128)} %get-tuple-element.35.linked_ref, bf16[384,384]{1,0:T(8,128)(2,1)} %get-tuple-element.36.high, bf16[384,384]{1,0:T(8,128)(2,1)} %get-tuple-element.37.low, ...), custom_call_target="tpu_custom_call" | custom-call | tf_op jit(solution)/shard_map/finish_last/pallas_call | solution.py:292
  (99 shorter events, 0.4 us)
Async XLA Ops:
  0.0 13.3 %collective-permute-start = (f32[8,4,48,384]{3,2,1,0:T(8,128)}, f32[8,4,48,384]{3,2,1,0:T(8,128)S(1)}, u32[]{:S(2)}, u32[]{:S(2)}) collective-permute-start(f32[8,4,48,384]{3,2,1,0:T(8,128)} %own_ref.7), channel_id=1, source_target_pairs={{0,4},{4,0},{8,12},{12,8},{16,20},{20,16},{24,28},{28,24},{1,5},{5... | collective-permute-start | bytes 7077896 | tf_op jit(solution)/shard_map/ppermute | solution.py:316
  2.5 3.2 %collective-permute-start.25 = (f32[8,1,48,384]{3,2,1,0:T(8,128)S(1)}, f32[8,1,48,384]{3,2,1,0:T(8,128)S(1)}, u32[]{:S(2)}, u32[]{:S(2)}) collective-permute-start(f32[8,1,48,384]{3,2,1,0:T(8,128)S(1)} %maximum_bitcast_fusion.mine.refs_10_), channel_id=1, source_target_pairs={{0,4},{4,0},{8,12},{12,8},{16,20},{20,16},{24,28},{28,24},{1,5},{5... | collective-permute-start | bytes 1769480 | tf_op jit(solution)/shard_map/ppermute | solution.py:318
  10.4 88.9 %copy-start.32 = (s32[8,4]{0,1:T(4,128)S(1)}, s32[8,4]{0,1:T(4,128)}, u32[]{:S(2)}) copy-start(s32[8,4]{0,1:T(4,128)} %param.12) | copy-start | bytes 388
  10.4 12.9 %collective-permute-start.26 = (f32[2,4,48,384]{3,2,1,0:T(8,128)}, f32[2,4,48,384]{3,2,1,0:T(8,128)}, u32[]{:S(2)}, u32[]{:S(2)}) collective-permute-start(f32[2,4,48,384]{3,2,1,0:T(8,128)} %pack.3), channel_id=1, source_target_pairs={{0,8},{4,20},{8,0},{12,28},{16,24},{20,4},{24,16},{28,12},{1,9},{5... | collective-permute-start | bytes 1769480 | tf_op jit(solution)/shard_map/ppermute | solution.py:325
  19.2 16.4 %collective-permute-start.32 = (f32[2,4,48,384]{3,2,1,0:T(8,128)}, f32[2,4,48,384]{3,2,1,0:T(8,128)S(1)}, u32[]{:S(2)}, u32[]{:S(2)}) collective-permute-start(f32[2,4,48,384]{3,2,1,0:T(8,128)} %get-tuple-element.38), channel_id=1, source_target_pairs={{0,8},{4,20},{8,0},{12,28},{16,24},{20,4},{24,16},{28,12},{1,9},{5... | collective-permute-start | bytes 1769480 | tf_op jit(solution)/shard_map/ppermute | solution.py:325
  19.2 17.9 %collective-permute-start.33 = (f32[2,4,48,384]{3,2,1,0:T(8,128)}, f32[2,4,48,384]{3,2,1,0:T(8,128)S(1)}, u32[]{:S(2)}, u32[]{:S(2)}) collective-permute-start(f32[2,4,48,384]{3,2,1,0:T(8,128)} %get-tuple-element.38), channel_id=1, source_target_pairs={{0,16},{4,12},{8,24},{12,4},{16,0},{20,28},{24,8},{28,20},{1,17},{... | collective-permute-start | bytes 1769480 | tf_op jit(solution)/shard_map/ppermute | solution.py:326
  21.3 27.0 %collective-permute-start.17 = (f32[2,4,48,384]{3,2,1,0:T(8,128)}, f32[2,4,48,384]{3,2,1,0:T(8,128)S(1)}, u32[]{:S(2)}, u32[]{:S(2)}) collective-permute-start(f32[2,4,48,384]{3,2,1,0:T(8,128)} %get-tuple-element.31), channel_id=1, source_target_pairs={{0,8},{4,20},{8,0},{12,28},{16,24},{20,4},{24,16},{28,12},{1,9},{5... | collective-permute-start | bytes 1769480 | tf_op jit(solution)/shard_map/ppermute | solution.py:325
  22.8 27.0 %collective-permute-start.18 = (f32[2,4,48,384]{3,2,1,0:T(8,128)}, f32[2,4,48,384]{3,2,1,0:T(8,128)S(1)}, u32[]{:S(2)}, u32[]{:S(2)}) collective-permute-start(f32[2,4,48,384]{3,2,1,0:T(8,128)} %get-tuple-element.31), channel_id=1, source_target_pairs={{0,16},{4,12},{8,24},{12,4},{16,0},{20,28},{24,8},{28,20},{1,17},{... | collective-permute-start | bytes 1769480 | tf_op jit(solution)/shard_map/ppermute | solution.py:326
  23.3 37.6 %collective-permute-start.9 = (f32[2,4,48,384]{3,2,1,0:T(8,128)}, f32[2,4,48,384]{3,2,1,0:T(8,128)S(1)}, u32[]{:S(2)}, u32[]{:S(2)}) collective-permute-start(f32[2,4,48,384]{3,2,1,0:T(8,128)} %get-tuple-element.28), channel_id=1, source_target_pairs={{0,8},{4,20},{8,0},{12,28},{16,24},{20,4},{24,16},{28,12},{1,9},{5... | collective-permute-start | bytes 1769480 | tf_op jit(solution)/shard_map/ppermute | solution.py:325
  35.6 75.0 %copy-start.10 = (f32[2,4,48,384]{3,2,1,0:T(8,128)}, f32[2,4,48,384]{3,2,1,0:T(8,128)S(1)}, u32[]{:S(2)}) copy-start(f32[2,4,48,384]{3,2,1,0:T(8,128)S(1)} %collective-permute-done.32.rest_0_) | copy-start | bytes 1769476
  35.6 25.3 %collective-permute-start.10 = (f32[2,4,48,384]{3,2,1,0:T(8,128)}, f32[2,4,48,384]{3,2,1,0:T(8,128)S(1)}, u32[]{:S(2)}, u32[]{:S(2)}) collective-permute-start(f32[2,4,48,384]{3,2,1,0:T(8,128)} %get-tuple-element.28), channel_id=1, source_target_pairs={{0,16},{4,12},{8,24},{12,4},{16,0},{20,28},{24,8},{28,20},{1,17},{... | collective-permute-start | bytes 1769480 | tf_op jit(solution)/shard_map/ppermute | solution.py:326
  37.2 41.8 %copy-start.11 = (f32[2,4,48,384]{3,2,1,0:T(8,128)}, f32[2,4,48,384]{3,2,1,0:T(8,128)S(1)}, u32[]{:S(2)}) copy-start(f32[2,4,48,384]{3,2,1,0:T(8,128)S(1)} %collective-permute-done.33.rest_1_) | copy-start | bytes 1769476
  37.2 36.4 %collective-permute-start.1 = (f32[2,4,48,384]{3,2,1,0:T(8,128)}, f32[2,4,48,384]{3,2,1,0:T(8,128)S(1)}, u32[]{:S(2)}, u32[]{:S(2)}) collective-permute-start(f32[2,4,48,384]{3,2,1,0:T(8,128)} %get-tuple-element.25), channel_id=1, source_target_pairs={{0,8},{4,20},{8,0},{12,28},{16,24},{20,4},{24,16},{28,12},{1,9},{5... | collective-permute-start | bytes 1769480 | tf_op jit(solution)/shard_map/ppermute | solution.py:325
  48.3 62.4 %copy-start.19 = (f32[2,4,48,384]{3,2,1,0:T(8,128)}, f32[2,4,48,384]{3,2,1,0:T(8,128)S(1)}, u32[]{:S(2)}) copy-start(f32[2,4,48,384]{3,2,1,0:T(8,128)S(1)} %collective-permute-done.17.rest_0_) | copy-start | bytes 1769476
  48.3 26.8 %collective-permute-start.2 = (f32[2,4,48,384]{3,2,1,0:T(8,128)}, f32[2,4,48,384]{3,2,1,0:T(8,128)S(1)}, u32[]{:S(2)}, u32[]{:S(2)}) collective-permute-start(f32[2,4,48,384]{3,2,1,0:T(8,128)} %get-tuple-element.25), channel_id=1, source_target_pairs={{0,16},{4,12},{8,24},{12,4},{16,0},{20,28},{24,8},{28,20},{1,17},{... | collective-permute-start | bytes 1769480 | tf_op jit(solution)/shard_map/ppermute | solution.py:326
  49.8 48.2 %copy-start.20 = (f32[2,4,48,384]{3,2,1,0:T(8,128)}, f32[2,4,48,384]{3,2,1,0:T(8,128)S(1)}, u32[]{:S(2)}) copy-start(f32[2,4,48,384]{3,2,1,0:T(8,128)S(1)} %collective-permute-done.18.rest_1_) | copy-start | bytes 1769476
  49.8 29.0 %collective-permute-start.34 = (f32[2,4,48,384]{3,2,1,0:T(8,128)S(1)}, f32[2,4,48,384]{3,2,1,0:T(8,128)S(1)}, u32[]{:S(2)}, u32[]{:S(2)}) collective-permute-start(f32[2,4,48,384]{3,2,1,0:T(8,128)S(1)} %collective-permute-done.32.rest_0_), channel_id=1, source_target_pairs={{0,16},{4,12},{8,24},{12,4},{16,0},{20,28},{24,8},{28,20},{1,17},{... | collective-permute-start | bytes 1769480 | tf_op jit(solution)/shard_map/ppermute | solution.py:327
  60.9 63.7 %copy-start.16 = (f32[2,4,48,384]{3,2,1,0:T(8,128)}, f32[2,4,48,384]{3,2,1,0:T(8,128)S(1)}, u32[]{:S(2)}) copy-start(f32[2,4,48,384]{3,2,1,0:T(8,128)S(1)} %collective-permute-done.9.rest_0_) | copy-start | bytes 1769476
  60.9 18.1 %collective-permute-start.35 = (f32[2,4,48,384]{3,2,1,0:T(8,128)S(1)}, f32[2,4,48,384]{3,2,1,0:T(8,128)S(1)}, u32[]{:S(2)}, u32[]{:S(2)}) collective-permute-start(f32[2,4,48,384]{3,2,1,0:T(8,128)S(1)} %collective-permute-done.32.rest_0_), channel_id=1, source_target_pairs={{0,4},{4,0},{8,12},{12,8},{16,20},{20,16},{24,28},{28,24},{1,5},{5... | collective-permute-start | bytes 1769480 | tf_op jit(solution)/shard_map/ppermute | solution.py:328
  61.0 37.0 %copy-start.18 = (f32[2,4,48,384]{3,2,1,0:T(8,128)}, f32[2,4,48,384]{3,2,1,0:T(8,128)S(1)}, u32[]{:S(2)}) copy-start(f32[2,4,48,384]{3,2,1,0:T(8,128)S(1)} %collective-permute-done.10.rest_1_) | copy-start | bytes 1769476
  61.0 19.7 %collective-permute-start.36 = (f32[2,4,48,384]{3,2,1,0:T(8,128)S(1)}, f32[2,4,48,384]{3,2,1,0:T(8,128)S(1)}, u32[]{:S(2)}, u32[]{:S(2)}) collective-permute-start(f32[2,4,48,384]{3,2,1,0:T(8,128)S(1)} %collective-permute-done.33.rest_1_), channel_id=1, source_target_pairs={{0,4},{4,0},{8,12},{12,8},{16,20},{20,16},{24,28},{28,24},{1,5},{5... | collective-permute-start | bytes 1769480 | tf_op jit(solution)/shard_map/ppermute | solution.py:328
  73.5 37.1 %copy-start.13 = (f32[2,4,48,384]{3,2,1,0:T(8,128)}, f32[2,4,48,384]{3,2,1,0:T(8,128)S(1)}, u32[]{:S(2)}) copy-start(f32[2,4,48,384]{3,2,1,0:T(8,128)S(1)} %collective-permute-done.1.rest_0_) | copy-start | bytes 1769476
  73.6 11.6 %collective-permute-start.19 = (f32[2,4,48,384]{3,2,1,0:T(8,128)S(1)}, f32[2,4,48,384]{3,2,1,0:T(8,128)S(1)}, u32[]{:S(2)}, u32[]{:S(2)}) collective-permute-start(f32[2,4,48,384]{3,2,1,0:T(8,128)S(1)} %collective-permute-done.17.rest_0_), channel_id=1, source_target_pairs={{0,16},{4,12},{8,24},{12,4},{16,0},{20,28},{24,8},{28,20},{1,17},{... | collective-permute-start | bytes 1769480 | tf_op jit(solution)/shard_map/ppermute | solution.py:327
  75.1 49.5 %copy-start.15 = (f32[2,4,48,384]{3,2,1,0:T(8,128)}, f32[2,4,48,384]{3,2,1,0:T(8,128)S(1)}, u32[]{:S(2)}) copy-start(f32[2,4,48,384]{3,2,1,0:T(8,128)S(1)} %collective-permute-done.2.rest_1_) | copy-start | bytes 1769476
  75.1 10.3 %collective-permute-start.20 = (f32[2,4,48,384]{3,2,1,0:T(8,128)S(1)}, f32[2,4,48,384]{3,2,1,0:T(8,128)S(1)}, u32[]{:S(2)}, u32[]{:S(2)}) collective-permute-start(f32[2,4,48,384]{3,2,1,0:T(8,128)S(1)} %collective-permute-done.17.rest_0_), channel_id=1, source_target_pairs={{0,4},{4,0},{8,12},{12,8},{16,20},{20,16},{24,28},{28,24},{1,5},{5... | collective-permute-start | bytes 1769480 | tf_op jit(solution)/shard_map/ppermute | solution.py:328
  78.8 31.9 %copy-start.12 = (f32[2,4,48,384]{3,2,1,0:T(8,128)}, f32[2,4,48,384]{3,2,1,0:T(8,128)S(1)}, u32[]{:S(2)}) copy-start(f32[2,4,48,384]{3,2,1,0:T(8,128)S(1)} %collective-permute-done.34.rest_2_) | copy-start | bytes 1769476
  78.8 8.3 %collective-permute-start.21 = (f32[2,4,48,384]{3,2,1,0:T(8,128)S(1)}, f32[2,4,48,384]{3,2,1,0:T(8,128)S(1)}, u32[]{:S(2)}, u32[]{:S(2)}) collective-permute-start(f32[2,4,48,384]{3,2,1,0:T(8,128)S(1)} %collective-permute-done.18.rest_1_), channel_id=1, source_target_pairs={{0,4},{4,0},{8,12},{12,8},{16,20},{20,16},{24,28},{28,24},{1,5},{5... | collective-permute-start | bytes 1769480 | tf_op jit(solution)/shard_map/ppermute | solution.py:328
  79.0 19.0 %copy-start.14 = (f32[2,4,48,384]{3,2,1,0:T(8,128)}, f32[2,4,48,384]{3,2,1,0:T(8,128)S(1)}, u32[]{:S(2)}) copy-start(f32[2,4,48,384]{3,2,1,0:T(8,128)S(1)} %collective-permute-done.35.rest_3_) | copy-start | bytes 1769476
  79.0 12.6 %collective-permute-start.11 = (f32[2,4,48,384]{3,2,1,0:T(8,128)S(1)}, f32[2,4,48,384]{3,2,1,0:T(8,128)}, u32[]{:S(2)}, u32[]{:S(2)}) collective-permute-start(f32[2,4,48,384]{3,2,1,0:T(8,128)S(1)} %collective-permute-done.9.rest_0_), channel_id=1, source_target_pairs={{0,16},{4,12},{8,24},{12,4},{16,0},{20,28},{24,8},{28,20},{1,17},{... | collective-permute-start | bytes 1769480 | tf_op jit(solution)/shard_map/ppermute | solution.py:327
  80.7 17.3 %copy-start.17 = (f32[2,4,48,384]{3,2,1,0:T(8,128)}, f32[2,4,48,384]{3,2,1,0:T(8,128)S(1)}, u32[]{:S(2)}) copy-start(f32[2,4,48,384]{3,2,1,0:T(8,128)S(1)} %collective-permute-done.36.rest_4_) | copy-start | bytes 1769476
  80.7 11.0 %collective-permute-start.12 = (f32[2,4,48,384]{3,2,1,0:T(8,128)S(1)}, f32[2,4,48,384]{3,2,1,0:T(8,128)S(1)}, u32[]{:S(2)}, u32[]{:S(2)}) collective-permute-start(f32[2,4,48,384]{3,2,1,0:T(8,128)S(1)} %collective-permute-done.9.rest_0_), channel_id=1, source_target_pairs={{0,4},{4,0},{8,12},{12,8},{16,20},{20,16},{24,28},{28,24},{1,5},{5... | collective-permute-start | bytes 1769480 | tf_op jit(solution)/shard_map/ppermute | solution.py:328
  85.1 12.9 %copy-start.21 = (f32[2,4,48,384]{3,2,1,0:T(8,128)}, f32[2,4,48,384]{3,2,1,0:T(8,128)S(1)}, u32[]{:S(2)}) copy-start(f32[2,4,48,384]{3,2,1,0:T(8,128)S(1)} %collective-permute-done.19.rest_2_) | copy-start | bytes 1769476
  85.1 6.9 %collective-permute-start.13 = (f32[2,4,48,384]{3,2,1,0:T(8,128)S(1)}, f32[2,4,48,384]{3,2,1,0:T(8,128)S(1)}, u32[]{:S(2)}, u32[]{:S(2)}) collective-permute-start(f32[2,4,48,384]{3,2,1,0:T(8,128)S(1)} %collective-permute-done.10.rest_1_), channel_id=1, source_target_pairs={{0,4},{4,0},{8,12},{12,8},{16,20},{20,16},{24,28},{28,24},{1,5},{5... | collective-permute-start | bytes 1769480 | tf_op jit(solution)/shard_map/ppermute | solution.py:328
  85.4 12.6 %copy-start.23 = (f32[2,4,48,384]{3,2,1,0:T(8,128)}, f32[2,4,48,384]{3,2,1,0:T(8,128)S(1)}, u32[]{:S(2)}) copy-start(f32[2,4,48,384]{3,2,1,0:T(8,128)S(1)} %collective-permute-done.20.rest_3_) | copy-start | bytes 1769476
  85.4 12.5 %collective-permute-start.3 = (f32[2,4,48,384]{3,2,1,0:T(8,128)S(1)}, f32[2,4,48,384]{3,2,1,0:T(8,128)}, u32[]{:S(2)}, u32[]{:S(2)}) collective-permute-start(f32[2,4,48,384]{3,2,1,0:T(8,128)S(1)} %collective-permute-done.1.rest_0_), channel_id=1, source_target_pairs={{0,16},{4,12},{8,24},{12,4},{16,0},{20,28},{24,8},{28,20},{1,17},{... | collective-permute-start | bytes 1769480 | tf_op jit(solution)/shard_map/ppermute | solution.py:327
  87.1 10.9 %collective-permute-start.22 = (f32[2,4,48,384]{3,2,1,0:T(8,128)S(1)}, f32[2,4,48,384]{3,2,1,0:T(8,128)S(1)}, u32[]{:S(2)}, u32[]{:S(2)}) collective-permute-start(f32[2,4,48,384]{3,2,1,0:T(8,128)S(1)} %collective-permute-done.19.rest_2_), channel_id=1, source_target_pairs={{0,4},{4,0},{8,12},{12,8},{16,20},{20,16},{24,28},{28,24},{1,5},{5... | collective-permute-start | bytes 1769480 | tf_op jit(solution)/shard_map/ppermute | solution.py:328
  91.5 33.1 %collective-permute-start.4 = (f32[2,4,48,384]{3,2,1,0:T(8,128)S(1)}, f32[2,4,48,384]{3,2,1,0:T(8,128)}, u32[]{:S(2)}, u32[]{:S(2)}) collective-permute-start(f32[2,4,48,384]{3,2,1,0:T(8,128)S(1)} %collective-permute-done.1.rest_0_), channel_id=1, source_target_pairs={{0,4},{4,0},{8,12},{12,8},{16,20},{20,16},{24,28},{28,24},{1,5},{5... | collective-permute-start | bytes 1769480 | tf_op jit(solution)/shard_map/ppermute | solution.py:328
  91.7 34.0 %collective-permute-start.14 = (f32[2,4,48,384]{3,2,1,0:T(8,128)}, f32[2,4,48,384]{3,2,1,0:T(8,128)}, u32[]{:S(2)}, u32[]{:S(2)}) collective-permute-start(f32[2,4,48,384]{3,2,1,0:T(8,128)} %collective-permute-done.11.rest_2_), channel_id=1, source_target_pairs={{0,4},{4,0},{8,12},{12,8},{16,20},{20,16},{24,28},{28,24},{1,5},{5... | collective-permute-start | bytes 1769480 | tf_op jit(solution)/shard_map/ppermute | solution.py:328
  92.1 49.2 %collective-permute-start.5 = (f32[2,4,48,384]{3,2,1,0:T(8,128)S(1)}, f32[2,4,48,384]{3,2,1,0:T(8,128)}, u32[]{:S(2)}, u32[]{:S(2)}) collective-permute-start(f32[2,4,48,384]{3,2,1,0:T(8,128)S(1)} %collective-permute-done.2.rest_1_), channel_id=1, source_target_pairs={{0,4},{4,0},{8,12},{12,8},{16,20},{20,16},{24,28},{28,24},{1,5},{5... | collective-permute-start | bytes 1769480 | tf_op jit(solution)/shard_map/ppermute | solution.py:328
  97.9 44.4 %collective-permute-start.6 = (f32[2,4,48,384]{3,2,1,0:T(8,128)}, f32[2,4,48,384]{3,2,1,0:T(8,128)}, u32[]{:S(2)}, u32[]{:S(2)}) collective-permute-start(f32[2,4,48,384]{3,2,1,0:T(8,128)} %collective-permute-done.3.rest_2_), channel_id=1, source_target_pairs={{0,4},{4,0},{8,12},{12,8},{16,20},{20,16},{24,28},{28,24},{1,5},{5... | collective-permute-start | bytes 1769480 | tf_op jit(solution)/shard_map/ppermute | solution.py:328
  98.9 57.7 %collective-permute-start.37 = (f32[2,4,48,384]{3,2,1,0:T(8,128)S(1)}, f32[2,4,48,384]{3,2,1,0:T(8,128)}, u32[]{:S(2)}, u32[]{:S(2)}) collective-permute-start(f32[2,4,48,384]{3,2,1,0:T(8,128)S(1)} %collective-permute-done.34.rest_2_), channel_id=1, source_target_pairs={{0,4},{4,0},{8,12},{12,8},{16,20},{20,16},{24,28},{28,24},{1,5},{5... | collective-permute-start | bytes 1769480 | tf_op jit(solution)/shard_map/ppermute | solution.py:328
  124.6 47.6 %collective-permute-start.27 = (f32[2,4,48,384]{3,2,1,0:T(8,128)}, f32[2,4,48,384]{3,2,1,0:T(8,128)}, u32[]{:S(2)}, u32[]{:S(2)}) collective-permute-start(f32[2,4,48,384]{3,2,1,0:T(8,128)} %pack.3), channel_id=1, source_target_pairs={{0,16},{4,12},{8,24},{12,4},{16,0},{20,28},{24,8},{28,20},{1,17},{... | collective-permute-start | bytes 1769480 | tf_op jit(solution)/shard_map/ppermute | solution.py:326
  125.7 46.5 %collective-permute-start.23 = (f32[2,2,96,384]{3,2,1,0:T(8,128)}, f32[2,2,96,384]{3,2,1,0:T(8,128)S(1)}, u32[]{:S(2)}, u32[]{:S(2)}) collective-permute-start(f32[2,2,96,384]{3,2,1,0:T(8,128)} %get-tuple-element.33), channel_id=1, source_target_pairs={{0,1},{1,0},{2,3},{3,2},{4,5},{5,4},{6,7},{7,6},{8,9},{9,8},{10,11... | collective-permute-start | bytes 1769480 | tf_op jit(solution)/shard_map/ppermute | solution.py:334
  141.2 31.6 %collective-permute-start.28 = (f32[2,4,48,384]{3,2,1,0:T(8,128)}, f32[2,4,48,384]{3,2,1,0:T(8,128)}, u32[]{:S(2)}, u32[]{:S(2)}) collective-permute-start(f32[2,4,48,384]{3,2,1,0:T(8,128)} %collective-permute-done.26.refs_12_), channel_id=1, source_target_pairs={{0,16},{4,12},{8,24},{12,4},{16,0},{20,28},{24,8},{28,20},{1,17},{... | collective-permute-start | bytes 1769480 | tf_op jit(solution)/shard_map/ppermute | solution.py:327
  142.3 30.8 %collective-permute-start.15 = (f32[2,2,96,384]{3,2,1,0:T(8,128)}, f32[2,2,96,384]{3,2,1,0:T(8,128)S(1)}, u32[]{:S(2)}, u32[]{:S(2)}) collective-permute-start(f32[2,2,96,384]{3,2,1,0:T(8,128)} %get-tuple-element.30), channel_id=1, source_target_pairs={{0,1},{1,0},{2,3},{3,2},{4,5},{5,4},{6,7},{7,6},{8,9},{9,8},{10,11... | collective-permute-start | bytes 1769480 | tf_op jit(solution)/shard_map/ppermute | solution.py:334
  156.6 16.2 %copy-start.5 = (f32[2,2,96,384]{3,2,1,0:T(8,128)S(1)}, f32[2,2,96,384]{3,2,1,0:T(8,128)}, u32[]{:S(2)}) copy-start(f32[2,2,96,384]{3,2,1,0:T(8,128)} %get-tuple-element.32.refs_7_) | copy-start | bytes 1769476
  156.6 16.8 %copy-start.7 = (f32[2,2,96,384]{3,2,1,0:T(8,128)S(1)}, f32[2,2,96,384]{3,2,1,0:T(8,128)}, u32[]{:S(2)}) copy-start(f32[2,2,96,384]{3,2,1,0:T(8,128)} %get-tuple-element.29.refs_4_) | copy-start | bytes 1769476
  156.6 19.5 %copy-start.9 = (f32[2,2,96,384]{3,2,1,0:T(8,128)S(1)}, f32[2,2,96,384]{3,2,1,0:T(8,128)}, u32[]{:S(2)}) copy-start(f32[2,2,96,384]{3,2,1,0:T(8,128)} %get-tuple-element.26.refs_1_) | copy-start | bytes 1769476
  156.6 16.8 %collective-permute-start.7 = (f32[2,2,96,384]{3,2,1,0:T(8,128)}, f32[2,2,96,384]{3,2,1,0:T(8,128)}, u32[]{:S(2)}, u32[]{:S(2)}) collective-permute-start(f32[2,2,96,384]{3,2,1,0:T(8,128)} %get-tuple-element.27), channel_id=1, source_target_pairs={{0,1},{1,0},{2,3},{3,2},{4,5},{5,4},{6,7},{7,6},{8,9},{9,8},{10,11... | collective-permute-start | bytes 1769480 | tf_op jit(solution)/shard_map/ppermute | solution.py:334
  172.2 28.7 %copy-start.3 = (f32[2,2,96,384]{3,2,1,0:T(8,128)S(1)}, f32[2,2,96,384]{3,2,1,0:T(8,128)}, u32[]{:S(2)}) copy-start(f32[2,2,96,384]{3,2,1,0:T(8,128)} %get-tuple-element.39.keep_ref) | copy-start | bytes 1769476
  172.2 5.0 %collective-permute-start.29 = (f32[2,4,48,384]{3,2,1,0:T(8,128)}, f32[2,4,48,384]{3,2,1,0:T(8,128)S(1)}, u32[]{:S(2)}, u32[]{:S(2)}) collective-permute-start(f32[2,4,48,384]{3,2,1,0:T(8,128)} %collective-permute-done.26.refs_12_), channel_id=1, source_target_pairs={{0,4},{4,0},{8,12},{12,8},{16,20},{20,16},{24,28},{28,24},{1,5},{5... | collective-permute-start | bytes 1769480 | tf_op jit(solution)/shard_map/ppermute | solution.py:328
  172.3 49.9 %copy-start.6 = (f32[2,2,96,384]{3,2,1,0:T(8,128)}, f32[2,2,96,384]{3,2,1,0:T(8,128)S(1)}, u32[]{:S(2)}) copy-start(f32[2,2,96,384]{3,2,1,0:T(8,128)S(1)} %collective-permute-done.23.refs_8_) | copy-start | bytes 1769476
  172.3 28.6 %collective-permute-start.38 = (f32[2,2,96,384]{3,2,1,0:T(8,128)}, f32[2,2,96,384]{3,2,1,0:T(8,128)S(1)}, u32[]{:S(2)}, u32[]{:S(2)}) collective-permute-start(f32[2,2,96,384]{3,2,1,0:T(8,128)} %get-tuple-element.40), channel_id=1, source_target_pairs={{0,1},{1,0},{2,3},{3,2},{4,5},{5,4},{6,7},{7,6},{8,9},{9,8},{10,11... | collective-permute-start | bytes 1769480 | tf_op jit(solution)/shard_map/ppermute | solution.py:334
  172.9 28.1 %collective-permute-start.30 = (f32[2,4,48,384]{3,2,1,0:T(8,128)}, f32[2,4,48,384]{3,2,1,0:T(8,128)S(1)}, u32[]{:S(2)}, u32[]{:S(2)}) collective-permute-start(f32[2,4,48,384]{3,2,1,0:T(8,128)} %collective-permute-done.27.refs_13_), channel_id=1, source_target_pairs={{0,4},{4,0},{8,12},{12,8},{16,20},{20,16},{24,28},{28,24},{1,5},{5... | collective-permute-start | bytes 1769480 | tf_op jit(solution)/shard_map/ppermute | solution.py:328
  173.1 49.1 %copy-start.8 = (f32[2,2,96,384]{3,2,1,0:T(8,128)}, f32[2,2,96,384]{3,2,1,0:T(8,128)S(1)}, u32[]{:S(2)}) copy-start(f32[2,2,96,384]{3,2,1,0:T(8,128)S(1)} %collective-permute-done.15.refs_5_) | copy-start | bytes 1769476
  173.1 30.9 %collective-permute-start.31 = (f32[2,4,48,384]{3,2,1,0:T(8,128)}, f32[2,4,48,384]{3,2,1,0:T(8,128)}, u32[]{:S(2)}, u32[]{:S(2)}) collective-permute-start(f32[2,4,48,384]{3,2,1,0:T(8,128)} %collective-permute-done.28.refs_14_), channel_id=1, source_target_pairs={{0,4},{4,0},{8,12},{12,8},{16,20},{20,16},{24,28},{28,24},{1,5},{5... | collective-permute-start | bytes 1769480 | tf_op jit(solution)/shard_map/ppermute | solution.py:328
  173.5 30.4 %collective-permute-start.24 = (f32[2,96,384]{2,1,0:T(8,128)S(1)}, f32[2,96,384]{2,1,0:T(8,128)S(1)}, u32[]{:S(2)}, u32[]{:S(2)}) collective-permute-start(f32[2,96,384]{2,1,0:T(8,128)S(1)} %fusion.1), channel_id=1, source_target_pairs={{0,2},{1,3},{2,0},{3,1},{4,6},{5,7},{6,4},{7,5},{8,10},{9,11},{10,... | collective-permute-start | bytes 884744 | tf_op jit(solution)/shard_map/ppermute | solution.py:335
  177.2 23.8 %copy-start.27 = (f32[2,4,48,384]{3,2,1,0:T(8,128)}, f32[2,4,48,384]{3,2,1,0:T(8,128)S(1)}, u32[]{:S(2)}) copy-start(f32[2,4,48,384]{3,2,1,0:T(8,128)S(1)} %collective-permute-done.29.refs_15_) | copy-start | bytes 1769476
  177.2 26.8 %collective-permute-start.16 = (f32[2,96,384]{2,1,0:T(8,128)S(1)}, f32[2,96,384]{2,1,0:T(8,128)S(1)}, u32[]{:S(2)}, u32[]{:S(2)}) collective-permute-start(f32[2,96,384]{2,1,0:T(8,128)S(1)} %fusion.2), channel_id=1, source_target_pairs={{0,2},{1,3},{2,0},{3,1},{4,6},{5,7},{6,4},{7,5},{8,10},{9,11},{10,... | collective-permute-start | bytes 884744 | tf_op jit(solution)/shard_map/ppermute | solution.py:335
  200.8 29.8 %copy-start.4 = (f32[2,2,96,384]{3,2,1,0:T(8,128)}, f32[2,2,96,384]{3,2,1,0:T(8,128)S(1)}, u32[]{:S(2)}) copy-start(f32[2,2,96,384]{3,2,1,0:T(8,128)S(1)} %collective-permute-done.38.near_ref) | copy-start | bytes 1769476
  200.9 21.3 %collective-permute-start.8 = (f32[2,96,384]{2,1,0:T(8,128)S(1)}, f32[2,96,384]{2,1,0:T(8,128)}, u32[]{:S(2)}, u32[]{:S(2)}) collective-permute-start(f32[2,96,384]{2,1,0:T(8,128)S(1)} %fusion.3), channel_id=1, source_target_pairs={{0,2},{1,3},{2,0},{3,1},{4,6},{5,7},{6,4},{7,5},{8,10},{9,11},{10,... | collective-permute-start | bytes 884744 | tf_op jit(solution)/shard_map/ppermute | solution.py:335
  200.9 21.2 %copy-start.28 = (f32[2,4,48,384]{3,2,1,0:T(8,128)}, f32[2,4,48,384]{3,2,1,0:T(8,128)S(1)}, u32[]{:S(2)}) copy-start(f32[2,4,48,384]{3,2,1,0:T(8,128)S(1)} %collective-permute-done.30.refs_16_) | copy-start | bytes 1769476
  200.9 29.7 %collective-permute-start.39 = (f32[2,96,384]{2,1,0:T(8,128)S(1)}, f32[2,96,384]{2,1,0:T(8,128)S(1)}, u32[]{:S(2)}, u32[]{:S(2)}) collective-permute-start(f32[2,96,384]{2,1,0:T(8,128)S(1)} %fusion), channel_id=1, source_target_pairs={{0,2},{1,3},{2,0},{3,1},{4,6},{5,7},{6,4},{7,5},{8,10},{9,11},{10,... | collective-permute-start | bytes 884744 | tf_op jit(solution)/shard_map/ppermute | solution.py:335
  203.9 18.2 %copy-start.30 = (f32[2,96,384]{2,1,0:T(8,128)}, f32[2,96,384]{2,1,0:T(8,128)S(1)}, u32[]{:S(2)}) copy-start(f32[2,96,384]{2,1,0:T(8,128)S(1)} %collective-permute-done.24.refs_9_) | copy-start | bytes 884740
  (9 other events, 31.0 us)

commit v2 on v1

--- a/solution.py
+++ b/solution.py
@@ -11,6 +11,7 @@
 HIGH = lax.Precision.HIGHEST
 F32 = jnp.float32
 BF16 = jnp.bfloat16
+LIMIT = 16 * 2**20
 
 
 def plain_device(l_cores, l_bucket, present, u_cores, u_bucket, diag_cores, pivot_inv, coupling):
@@ -78,6 +79,7 @@
             out_specs=[block, block],
         ),
         out_shape=[out, out],
+        compiler_params=pltpu.CompilerParams(vmem_limit_bytes=LIMIT),
         name="split_lower",
     )(l_bucket, present, l_cores)
 
@@ -102,6 +104,7 @@
             out_specs=[pl.BlockSpec((2, 1, rows, width), lambda k, at: (0, k, 0, 0))] * columns,
         ),
         out_shape=[jax.ShapeDtypeStruct((2, half, rows, width), F32)] * columns,
+        compiler_params=pltpu.CompilerParams(vmem_limit_bytes=LIMIT),
         name="pack",
     )(place, own, twin)
 
@@ -121,7 +124,7 @@
             store(chip + core, part(core))
 
 
-def multiply(j, place, u_bucket, lower, own, twin, mine, theirs):
+def multiply(j, pieces, place, u_bucket, lower, own, twin, mine, theirs):
     high, low = lower
     pairs, height, depth = high.shape
     rows, width = own.shape[-2:]
@@ -129,80 +132,60 @@
     step = width // 3
     half = pairs // 2
     share = width // 4
+    each = tiles // pieces
 
     def body(at, bucket, lhs_high, lhs_low, own_ref, twin_ref, *rest):
         parts, others = rest[:3], rest[3:6]
-        keep, send, rhs_high, rhs_low, total = rest[6:]
-        p = pl.program_id(0)
-        core = at[0] % 2
+        keep, send = rest[6 : 6 + pieces], rest[6 + pieces : 6 + 2 * pieces]
+        rhs_high, rhs_low, total = rest[6 + 2 * pieces :]
+        core, z = at[0] % 2, at[1]
         row = lax.broadcasted_iota(jnp.int32, (rows, width), 0)
-
-        def assemble(refs, bundle):
-            for k in range(2):
-                limit = bucket[2 * p + k, j] * step
-
-                def store(device, value):
-                    start = pl.multiple_of(device * rows, 16)
-                    value = jnp.where(row < limit - start, value, 0.0)
-                    a, b = halves(value)
-                    rhs_high[pl.ds(k * width + start, rows)] = a
-                    rhs_low[pl.ds(k * width + start, rows)] = b
-
-                gather_tile(
-                    at, bundle, own_ref[k, 0], twin_ref[k, 0],
-                    [lambda s, r=r: r[s, k] for r in refs], store,
+        for turn, (bundle, refs) in enumerate(((core, parts), (1 - core, others))):
+            for local in range(half):
+                slot = turn * half + local
+                p = bundle * half + local
+                for k in range(2):
+                    limit = bucket[j, 2 * p + k] * step
+
+                    def store(device, value):
+                        start = pl.multiple_of(device * rows, 16)
+                        a, b = halves(jnp.where(row < limit - start, value, 0.0))
+                        rhs_high[slot, pl.ds(k * width + start, rows)] = a
+                        rhs_low[slot, pl.ds(k * width + start, rows)] = b
+
+                    gather_tile(
+                        at, bundle, own_ref[2 * p + k, j], twin_ref[2 * p + k, j],
+                        [lambda s, r=r: r[s, 2 * local + k] for r in refs], store,
+                    )
+                a, b = lhs_high[p], lhs_low[p]
+                product = jnp.dot(
+                    jnp.concatenate([a, b, a], axis=1),
+                    jnp.concatenate([rhs_high[slot], rhs_high[slot], rhs_low[slot]], axis=0),
+                    preferred_element_type=F32,
                 )
-
-        @pl.when(p // half == core)
-        def _():
-            assemble(parts, core)
-
-        @pl.when(p // half != core)
-        def _():
-            assemble(others, 1 - core)
-
-        left = lhs_high[0], lhs_low[0]
-        product = jnp.dot(
-            jnp.concatenate([left[0], left[1], left[0]], axis=1),
-            jnp.concatenate([rhs_high[...], rhs_high[...], rhs_low[...]], axis=0),
-            preferred_element_type=F32,
-        )
-
-        @pl.when(p == 0)
-        def _():
-            total[...] = product
-
-        @pl.when(p > 0)
-        def _():
-            total[...] += product
-
-        @pl.when(p == pairs - 1)
-        def _():
-            z = at[1]
-            for slot, (target, block) in enumerate(((keep, z), (keep, z ^ 2), (send, z ^ 1), (send, z ^ 3))):
-                for i in range(tiles):
-                    start = pl.multiple_of(block * share, 8)
-                    target[slot % 2, i] = total[pl.ds(i * width + start, share)]
-
-    lhs = pl.BlockSpec((1, height, depth), lambda p, *_: (p, 0, 0))
-    local = pl.BlockSpec((2, 1, rows, width), lambda p, *_: (p, j, 0, 0))
-    piece = pl.BlockSpec((2, 2, rows, width), lambda p, *_: (0, p % half, 0, 0))
-    out = pl.BlockSpec((2, tiles, share, width), lambda p, *_: (0, 0, 0, 0))
-    shape = jax.ShapeDtypeStruct((2, tiles, share, width), F32)
-    return pl.pallas_call(
-        body,
-        grid_spec=pltpu.PrefetchScalarGridSpec(
-            num_scalar_prefetch=2,
-            grid=(pairs,),
-            in_specs=[lhs, lhs, local, local] + [piece] * 6,
-            out_specs=[out, out],
-            scratch_shapes=[
-                pltpu.VMEM((depth, width), BF16),
-                pltpu.VMEM((depth, width), BF16),
-                pltpu.VMEM((height, width), F32),
-            ],
-        ),
-        out_shape=[shape, shape],
+                if slot == 0:
+                    total[...] = product
+                else:
+                    total[...] += product
+        for slot, (target, block) in enumerate(((keep, z), (keep, z ^ 2), (send, z ^ 1), (send, z ^ 3))):
+            for i in range(tiles):
+                start = pl.multiple_of(block * share, 8)
+                target[i // each][slot % 2, i % each] = total[pl.ds(i * width + start, share)]
+
+    shape = jax.ShapeDtypeStruct((2, each, share, width), F32)
+    vmem = pl.BlockSpec(memory_space=pltpu.VMEM)
+    smem = pl.BlockSpec(memory_space=pltpu.SMEM)
+    return pl.pallas_call(
+        body,
+        in_specs=[smem, smem] + [vmem] * 10,
+        out_specs=[vmem] * (2 * pieces),
+        scratch_shapes=[
+            pltpu.VMEM((pairs, depth, width), BF16),
+            pltpu.VMEM((pairs, depth, width), BF16),
+            pltpu.VMEM((height, width), F32),
+        ],
+        out_shape=[shape] * (2 * pieces),
+        compiler_params=pltpu.CompilerParams(vmem_limit_bytes=LIMIT),
     )(place, u_bucket, high, low, own, twin, *mine, *theirs)
 
 
@@ -274,28 +257,36 @@
             square,
         ],
         scratch_shapes=[pltpu.VMEM((2 * columns - 1, width, width), BF16)] * 2,
+        compiler_params=pltpu.CompilerParams(vmem_limit_bytes=LIMIT),
         name="finish_early",
     )(place, *operands)
 
 
-def finish_last(columns, diag, done, linked, last_high, last_low, keep, near, far):
+def finish_last(columns, diag, done, linked, last_high, last_low, parts):
     tiles, _, share, width = diag.shape
-    height = tiles * share
-
-    def body(diag_ref, done_ref, linked_ref, high, low, keep_ref, near_ref, far_ref, out):
+    each = tiles // len(parts)
+    height = each * share
+
+    def body(diag_ref, done_ref, linked_ref, high, low, *rest):
+        out = rest[-1]
         for column in range(columns - 1):
             out[:, column] = done_ref[:, column]
-        reduced = diag_ref[:, columns - 1] - (keep_ref[0] + near_ref[0] + far_ref[...]) - linked_ref[...]
-        value = dot3(halves(reduced.reshape(height, width)), high[...], low[...])
-        out[:, columns - 1] = value.reshape(tiles, share, width)
-
-    return pl.pallas_call(
-        body,
-        in_specs=[pl.BlockSpec(memory_space=pltpu.VMEM)] * 8,
+        for n in range(len(parts)):
+            keep, near, far = rest[3 * n : 3 * n + 3]
+            span = slice(n * each, (n + 1) * each)
+            update = keep[0] + near[0] + far[...]
+            reduced = diag_ref[span, columns - 1] - update - linked_ref[span]
+            value = dot3(halves(reduced.reshape(height, width)), high[...], low[...])
+            out[span, columns - 1] = value.reshape(each, share, width)
+
+    return pl.pallas_call(
+        body,
+        in_specs=[pl.BlockSpec(memory_space=pltpu.VMEM)] * (5 + 3 * len(parts)),
         out_specs=pl.BlockSpec(memory_space=pltpu.VMEM),
         out_shape=jax.ShapeDtypeStruct(diag.shape, F32),
+        compiler_params=pltpu.CompilerParams(vmem_limit_bytes=LIMIT),
         name="finish_last",
-    )(diag, done, linked, last_high, last_low, keep, near, far)
+    )(diag, done, linked, last_high, last_low, *[v for part in parts for v in part])
 
 
 def moves(size, first_of_core):
@@ -303,7 +294,7 @@
 
 
 def cube_device(l_cores, l_bucket, present, u_cores, u_bucket, diag_cores, pivot_inv, coupling):
-    columns = u_cores.shape[1]
+    columns, tiles = u_cores.shape[1], l_cores.shape[0]
     size = lax.axis_size("row")
     first = functools.partial(lax.ppermute, axis_name="row", perm=moves(size, (2, 4)))
     second = functools.partial(lax.ppermute, axis_name="row", perm=moves(size, (4, 2)))
@@ -329,15 +320,21 @@
         gathered.append(((a, b, c), twins))
 
     sums = []
+    bucket = u_bucket.T
     for j in range(columns):
-        keep, send = multiply(j, place, u_bucket, lower, u_cores, u_twin, *gathered[j])
-        near = near_of(send)
-        far = far_of(keep[1] + near[1])
-        sums.append((keep, near, far))
+        pieces = tiles if j == columns - 1 else 1
+        outs = multiply(j, pieces, place, bucket, lower, u_cores, u_twin, *gathered[j])
+        parts = []
+        for n in range(pieces):
+            keep, send = outs[n], outs[pieces + n]
+            near = near_of(send)
+            far = far_of(keep[1] + near[1])
+            parts.append((keep, near, far))
+        sums.append(parts)
     done, linked, last_high, last_low = finish_early(
-        place, columns, diag_cores, sums[:-1], small, small_twin, *gathered[columns],
+        place, columns, diag_cores, [p[0] for p in sums[:-1]], small, small_twin, *gathered[columns],
     )
-    return finish_last(columns, diag_cores, done, linked, last_high, last_low, *sums[-1])
+    return finish_last(columns, diag_cores, done, linked, last_high, last_low, sums[-1])
 
 
 def solution(mesh):

time: 236 us -> 218 us (0.924)
  Pallas kernels: 86.8 us -> 52.1 us
  waiting for transfers between devices: 107 us -> 118 us
  starting transfers between devices: 31.8 us -> 40.7 us
    pallas_call x5, Pallas kernels: 59.2 us -> 41.4 us  [the longest x4 39.9 us: multiply(): pl.pallas_call(body, in_specs=[smem, smem] + [vmem] * 10, out_specs=[vmem...]
    ppermute x4 -> x5, waiting for transfers between devices: 17.5 us -> 34.2 us  [cube_device(): far = far_of(keep[1] + near[1])]
    pallas_call x1, Pallas kernels: 10.7 us -> 2.84 us  [split_lower(): pl.pallas_call(body, grid_spec=pltpu.PrefetchScalarGridSpec(num_scalar_pr...]
    pallas_call x2, Pallas kernels: 8.41 us -> 3.58 us  [pack(): pl.pallas_call(body, grid_spec=pltpu.PrefetchScalarGridSpec(num_scalar_pr...]
    pallas_call x1, Pallas kernels: 8.44 us -> 4.23 us  [finish_early(): pl.pallas_call(body, in_specs=[pl.BlockSpec(memory_space=pltpu.SMEM)] + [...]
    ppermute x5, starting transfers between devices: 5.03 us -> 8.39 us  [cube_device(): a = first(bundle)]
    ppermute x5, waiting for transfers between devices: 18.1 us -> 15.3 us  [cube_device(): c = second(a)]
    ppermute x5, starting transfers between devices: 6.73 us -> 9.47 us  [cube_device(): b = second(bundle)]
  transfers between devices with their start and end apart: 40 -> 42, of which waited for: 12 -> 16; matrix products, arithmetic and copies ran while one was open for 2% -> 1% of each run, Pallas kernels for 35% -> 23%
where the time goes in v2:
time: 218 us; the launch traced here: 217 us
  waiting for transfers between devices  118 us (54%)
  Pallas kernels  52.1 us (24%)
  starting transfers between devices  40.7 us (19%)
  local copies, waits for them, and re-layouts  4.81 us (2%)
    ppermute x5, waiting for transfers between devices, cube_device(): a = first(bundle)  44.5 us
    pallas_call x4, Pallas kernels, multiply(): pl.pallas_call(body, in_specs=[smem, smem] + [vmem] * 10, out_specs=[vmem...  39.9 us
    ppermute x5, waiting for transfers between devices, cube_device(): far = far_of(keep[1] + near[1])  34.2 us
    ppermute x5, waiting for transfers between devices, cube_device(): near = near_of(send)  21.3 us
    ppermute x5, waiting for transfers between devices, cube_device(): c = second(a)  15.3 us
    ppermute x5, starting transfers between devices, cube_device(): b = second(bundle)  9.47 us
    ppermute x5, starting transfers between devices, cube_device(): a = first(bundle)  8.39 us
    ppermute x5, starting transfers between devices, cube_device(): near = near_of(send)  6.72 us
  transfers between devices with their start and end apart: 42, of which 16 were waited for; matrix products, arithmetic and copies ran while one was open for 1% of the time, Pallas kernels for 23%

profile of v2, /device:TPU:0, one launch (start us, length us, event | category | flops | bytes accessed | tf_op | source)
XLA Modules:
  0.0 217.3 jit_solution(2214789104392311931)
XLA Ops:
  0.0 0.5 collective-permute-start
  0.5 1.1 slice.39
  1.6 1.1 maximum_bitcast_fusion.mine.refs_10_
  2.9 2.8 %collective-permute-done.25.other.refs_11_ = f32[8,1,48,384]{3,2,1,0:T(8,128)S(1)} collective-permute-done((f32[8,1,48,384]{3,2,1,0:T(8,128)S(1)}, f32[8,1,48,384]{3,2,1,0:T(8,128)S(1)}, u32[]{:S(2)}, u32[]{:S(2)}) %collective-permute-start.25) | collective-permute-done | bytes 589856 | tf_op jit(solution)/shard_map/ppermute | solution.py:309
  5.7 0.7 pack.3
  6.5 2.9 %collective-permute-start.26 = (f32[2,4,48,384]{3,2,1,0:T(8,128)S(1)}, f32[2,4,48,384]{3,2,1,0:T(8,128)S(1)}, u32[]{:S(2)}, u32[]{:S(2)}) collective-permute-start(f32[2,4,48,384]{3,2,1,0:T(8,128)S(1)} %pack.3), channel_id=1, source_target_pairs={{0,8},{4,20},{8,0},{12,28},{16,24},{20,4},{24,16},{28,12},{1,9},{5... | collective-permute-start | bytes 1769480 | tf_op jit(solution)/shard_map/ppermute | solution.py:316
  9.4 2.8 %pack.2 = (f32[2,4,48,384]{3,2,1,0:T(8,128)S(1)}, f32[2,4,48,384]{3,2,1,0:T(8,128)S(1)}, f32[2,4,48,384]{3,2,1,0:T(8,128)S(1)}, f32[2,4,48,384]{3,2,1,0:T(8,128)S(1)}) custom-call(s32[2]{0:T(128)S(1)} %pad_add_fusion.at, f32[8,4,48,384]{3,2,1,0:T(8,128)S(1)} %copy-done, f32[8,4,48,384]{3,2,1,0:T(8,128)} %collective-permute-done.other.twin_ref), custom_call_target="tpu_custom_call" | custom-call | tf_op jit(solution)/shard_map/pack/pallas_call | solution.py:98
  12.2 0.1 collective-permute-start.32
  12.3 2.0 collective-permute-start.33
  14.4 1.5 collective-permute-start.17
  15.9 0.5 collective-permute-start.18
  16.4 3.3 %collective-permute-done.26.refs_12_ = f32[2,4,48,384]{3,2,1,0:T(8,128)S(1)} collective-permute-done((f32[2,4,48,384]{3,2,1,0:T(8,128)S(1)}, f32[2,4,48,384]{3,2,1,0:T(8,128)S(1)}, u32[]{:S(2)}, u32[]{:S(2)}) %collective-permute-start.26) | collective-permute-done | bytes 589856 | tf_op jit(solution)/shard_map/ppermute | solution.py:316
  19.6 2.4 %collective-permute-start.9 = (f32[2,4,48,384]{3,2,1,0:T(8,128)S(1)}, f32[2,4,48,384]{3,2,1,0:T(8,128)S(1)}, u32[]{:S(2)}, u32[]{:S(2)}) collective-permute-start(f32[2,4,48,384]{3,2,1,0:T(8,128)S(1)} %get-tuple-element.30), channel_id=1, source_target_pairs={{0,8},{4,20},{8,0},{12,28},{16,24},{20,4},{24,16},{28,12},{1,9},{5... | collective-permute-start | bytes 1769480 | tf_op jit(solution)/shard_map/ppermute | solution.py:316
  22.0 10.2 %collective-permute-done.32.rest_0_ = f32[2,4,48,384]{3,2,1,0:T(8,128)S(1)} collective-permute-done((f32[2,4,48,384]{3,2,1,0:T(8,128)S(1)}, f32[2,4,48,384]{3,2,1,0:T(8,128)S(1)}, u32[]{:S(2)}, u32[]{:S(2)}) %collective-permute-start.32) | collective-permute-done | bytes 589856 | tf_op jit(solution)/shard_map/ppermute | solution.py:316
  32.3 2.4 %collective-permute-start.10 = (f32[2,4,48,384]{3,2,1,0:T(8,128)S(1)}, f32[2,4,48,384]{3,2,1,0:T(8,128)S(1)}, u32[]{:S(2)}, u32[]{:S(2)}) collective-permute-start(f32[2,4,48,384]{3,2,1,0:T(8,128)S(1)} %get-tuple-element.30), channel_id=1, source_target_pairs={{0,16},{4,12},{8,24},{12,4},{16,0},{20,28},{24,8},{28,20},{1,17},{... | collective-permute-start | bytes 1769480 | tf_op jit(solution)/shard_map/ppermute | solution.py:317
  34.7 1.5 collective-permute-start.1
  36.2 8.7 %collective-permute-done.17.rest_0_ = f32[2,4,48,384]{3,2,1,0:T(8,128)S(1)} collective-permute-done((f32[2,4,48,384]{3,2,1,0:T(8,128)S(1)}, f32[2,4,48,384]{3,2,1,0:T(8,128)S(1)}, u32[]{:S(2)}, u32[]{:S(2)}) %collective-permute-start.17) | collective-permute-done | bytes 589856 | tf_op jit(solution)/shard_map/ppermute | solution.py:316
  44.9 2.4 %collective-permute-start.2 = (f32[2,4,48,384]{3,2,1,0:T(8,128)S(1)}, f32[2,4,48,384]{3,2,1,0:T(8,128)S(1)}, u32[]{:S(2)}, u32[]{:S(2)}) collective-permute-start(f32[2,4,48,384]{3,2,1,0:T(8,128)S(1)} %get-tuple-element.27), channel_id=1, source_target_pairs={{0,16},{4,12},{8,24},{12,4},{16,0},{20,28},{24,8},{28,20},{1,17},{... | collective-permute-start | bytes 1769480 | tf_op jit(solution)/shard_map/ppermute | solution.py:317
  47.4 10.2 %collective-permute-done.9.rest_0_ = f32[2,4,48,384]{3,2,1,0:T(8,128)S(1)} collective-permute-done((f32[2,4,48,384]{3,2,1,0:T(8,128)S(1)}, f32[2,4,48,384]{3,2,1,0:T(8,128)S(1)}, u32[]{:S(2)}, u32[]{:S(2)}) %collective-permute-start.9) | collective-permute-done | bytes 589856 | tf_op jit(solution)/shard_map/ppermute | solution.py:316
  57.6 0.5 collective-permute-start.36
  58.1 12.1 %collective-permute-done.1.rest_0_ = f32[2,4,48,384]{3,2,1,0:T(8,128)S(1)} collective-permute-done((f32[2,4,48,384]{3,2,1,0:T(8,128)S(1)}, f32[2,4,48,384]{3,2,1,0:T(8,128)S(1)}, u32[]{:S(2)}, u32[]{:S(2)}) %collective-permute-start.1) | collective-permute-done | bytes 589856 | tf_op jit(solution)/shard_map/ppermute | solution.py:316
  70.2 2.4 %collective-permute-start.19 = (f32[2,4,48,384]{3,2,1,0:T(8,128)S(1)}, f32[2,4,48,384]{3,2,1,0:T(8,128)S(1)}, u32[]{:S(2)}, u32[]{:S(2)}) collective-permute-start(f32[2,4,48,384]{3,2,1,0:T(8,128)S(1)} %collective-permute-done.17.rest_0_), channel_id=1, source_target_pairs={{0,16},{4,12},{8,24},{12,4},{16,0},{20,28},{24,8},{28,20},{1,17},{... | collective-permute-start | bytes 1769480 | tf_op jit(solution)/shard_map/ppermute | solution.py:318
  72.6 1.0 collective-permute-done.34.rest_2_
  73.6 0.3 collective-permute-start.21
  74.0 2.0 collective-permute-start.11
  76.0 4.5 %collective-permute-done.19.rest_2_ = f32[2,4,48,384]{3,2,1,0:T(8,128)S(1)} collective-permute-done((f32[2,4,48,384]{3,2,1,0:T(8,128)S(1)}, f32[2,4,48,384]{3,2,1,0:T(8,128)S(1)}, u32[]{:S(2)}, u32[]{:S(2)}) %collective-permute-start.19) | collective-permute-done | bytes 589856 | tf_op jit(solution)/shard_map/ppermute | solution.py:318
  80.5 0.1 collective-permute-start.13
  80.6 2.0 collective-permute-start.3
  82.6 0.1 collective-permute-start.22
  82.7 4.1 %collective-permute-done.11.rest_2_ = f32[2,4,48,384]{3,2,1,0:T(8,128)S(1)} collective-permute-done((f32[2,4,48,384]{3,2,1,0:T(8,128)S(1)}, f32[2,4,48,384]{3,2,1,0:T(8,128)S(1)}, u32[]{:S(2)}, u32[]{:S(2)}) %collective-permute-start.11) | collective-permute-done | bytes 589856 | tf_op jit(solution)/shard_map/ppermute | solution.py:318
  86.8 0.1 collective-permute-start.4
  86.9 0.4 collective-permute-start.5
  87.3 0.1 collective-permute-start.37
  87.4 5.7 %collective-permute-done.3.rest_2_ = f32[2,4,48,384]{3,2,1,0:T(8,128)S(1)} collective-permute-done((f32[2,4,48,384]{3,2,1,0:T(8,128)S(1)}, f32[2,4,48,384]{3,2,1,0:T(8,128)S(1)}, u32[]{:S(2)}, u32[]{:S(2)}) %collective-permute-start.3) | collective-permute-done | bytes 589856 | tf_op jit(solution)/shard_map/ppermute | solution.py:318
  93.1 0.1 collective-permute-start.14
  93.2 0.4 collective-permute-start.6
  93.6 3.7 %copy-done.1 = f32[2,8,384,384]{3,2,1,0:T(8,128)S(1)} copy-done((f32[2,8,384,384]{3,2,1,0:T(8,128)S(1)}, f32[2,8,384,384]{3,2,1,0:T(8,128)}, u32[]{:S(2)}) %copy-start.1) | copy-done | bytes 9437208
  97.3 2.8 %split_lower.1 = (bf16[4,768,768]{2,1,0:T(8,128)(2,1)S(1)}, bf16[4,768,768]{2,1,0:T(8,128)(2,1)S(1)}) custom-call(s32[2,8]{1,0:T(2,128)S(1)} %copy-done.4, s32[2,8]{1,0:T(2,128)S(1)} %copy-done.5, f32[2,8,384,384]{3,2,1,0:T(8,128)S(1)} %copy-done.1), custom_call_target="tpu_custom_call" | custom-call | tf_op jit(solution)/shard_map/split_lower/pallas_call | solution.py:73
  100.2 9.9 %shard_map.84 = (f32[2,2,96,384]{3,2,1,0:T(8,128)S(1)}, f32[2,2,96,384]{3,2,1,0:T(8,128)S(1)}) custom-call(s32[2]{0:T(128)S(1)} %pad_add_fusion.at, s32[4,8]{1,0:T(4,128)S(1)} %bitcast.15, bf16[4,768,768]{2,1,0:T(8,128)(2,1)S(1)} %get-tuple-element.25.lhs_high, bf16[4,768,768]{2,1,0:T(8,128)(2,1)S(1)} %get-tuple-element.26.lhs_low, ...), custom_call_target="tpu_custom_call" | custom-call | tf_op jit(solution)/shard_map/pallas_call | solution.py:178
  110.1 2.1 collective-permute-start.27
  112.2 0.1 collective-permute-start.28
  112.3 2.0 collective-permute-start.23
  114.3 9.9 %shard_map.85 = (f32[2,1,96,384]{3,2,1,0:T(8,128)S(1)}, f32[2,1,96,384]{3,2,1,0:T(8,128)S(1)}, f32[2,1,96,384]{3,2,1,0:T(8,128)S(1)}, f32[2,1,96,384]{3,2,1,0:T(8,128)S(1)}) custom-call(s32[2]{0:T(128)S(1)} %pad_add_fusion.at, s32[4,8]{1,0:T(4,128)S(1)} %bitcast.16, bf16[4,768,768]{2,1,0:T(8,128)(2,1)S(1)} %get-tuple-element.25.lhs_high, ...), custom_call_target="tpu_custom_call" | custom-call | tf_op jit(solution)/shard_map/pallas_call | solution.py:178
  124.2 0.1 collective-permute-start.40
  124.3 10.1 %shard_map.83 = (f32[2,2,96,384]{3,2,1,0:T(8,128)S(1)}, f32[2,2,96,384]{3,2,1,0:T(8,128)S(1)}) custom-call(s32[2]{0:T(128)S(1)} %pad_add_fusion.at, s32[4,8]{1,0:T(4,128)S(1)} %bitcast.17, bf16[4,768,768]{2,1,0:T(8,128)(2,1)S(1)} %get-tuple-element.25.lhs_high, bf16[4,768,768]{2,1,0:T(8,128)(2,1)S(1)} %get-tuple-element.26.lhs_low, ...), custom_call_target="tpu_custom_call" | custom-call | tf_op jit(solution)/shard_map/pallas_call | solution.py:178
  134.5 2.1 collective-permute-start.15
  136.6 9.9 %shard_map.82 = (f32[2,2,96,384]{3,2,1,0:T(8,128)S(1)}, f32[2,2,96,384]{3,2,1,0:T(8,128)S(1)}) custom-call(s32[2]{0:T(128)S(1)} %pad_add_fusion.at, s32[4,8]{1,0:T(4,128)S(1)} %bitcast.18, bf16[4,768,768]{2,1,0:T(8,128)(2,1)S(1)} %get-tuple-element.25.lhs_high, bf16[4,768,768]{2,1,0:T(8,128)(2,1)S(1)} %get-tuple-element.26.lhs_low, ...), custom_call_target="tpu_custom_call" | custom-call | tf_op jit(solution)/shard_map/pallas_call | solution.py:178
  146.5 0.1 collective-permute-start.7
  146.7 0.5 collective-permute-start.30
  147.2 0.1 collective-permute-start.31
  147.3 2.9 %collective-permute-done.15.refs_5_ = f32[2,2,96,384]{3,2,1,0:T(8,128)S(1)} collective-permute-done((f32[2,2,96,384]{3,2,1,0:T(8,128)S(1)}, f32[2,2,96,384]{3,2,1,0:T(8,128)S(1)}, u32[]{:S(2)}, u32[]{:S(2)}) %collective-permute-start.15) | collective-permute-done | bytes 589856 | tf_op jit(solution)/shard_map/ppermute | solution.py:330
  150.3 2.5 %collective-permute-start.38 = (f32[2,1,96,384]{3,2,1,0:T(8,128)S(1)}, f32[2,1,96,384]{3,2,1,0:T(8,128)S(1)}, u32[]{:S(2)}, u32[]{:S(2)}) collective-permute-start(f32[2,1,96,384]{3,2,1,0:T(8,128)S(1)} %get-tuple-element.42), channel_id=1, source_target_pairs={{0,1},{1,0},{2,3},{3,2},{4,5},{5,4},{6,7},{7,6},{8,9},{9,8},{10,11... | collective-permute-start | bytes 884744 | tf_op jit(solution)/shard_map/ppermute | solution.py:330
  152.8 10.1 %collective-permute-done.7.refs_2_ = f32[2,2,96,384]{3,2,1,0:T(8,128)S(1)} collective-permute-done((f32[2,2,96,384]{3,2,1,0:T(8,128)S(1)}, f32[2,2,96,384]{3,2,1,0:T(8,128)S(1)}, u32[]{:S(2)}, u32[]{:S(2)}) %collective-permute-start.7) | collective-permute-done | bytes 589856 | tf_op jit(solution)/shard_map/ppermute | solution.py:330
  162.9 2.9 %collective-permute-start.24 = (f32[2,96,384]{2,1,0:T(8,128)S(1)}, f32[2,96,384]{2,1,0:T(8,128)S(1)}, u32[]{:S(2)}, u32[]{:S(2)}) collective-permute-start(f32[2,96,384]{2,1,0:T(8,128)S(1)} %fusion), channel_id=1, source_target_pairs={{0,2},{1,3},{2,0},{3,1},{4,6},{5,7},{6,4},{7,5},{8,10},{9,11},{10,... | collective-permute-start | bytes 884744 | tf_op jit(solution)/shard_map/ppermute | solution.py:331
  165.8 0.1 collective-permute-start.16
  166.0 8.2 %collective-permute-done.38.rest_1_ = f32[2,1,96,384]{3,2,1,0:T(8,128)S(1)} collective-permute-done((f32[2,1,96,384]{3,2,1,0:T(8,128)S(1)}, f32[2,1,96,384]{3,2,1,0:T(8,128)S(1)}, u32[]{:S(2)}, u32[]{:S(2)}) %collective-permute-start.38) | collective-permute-done | bytes 294944 | tf_op jit(solution)/shard_map/ppermute | solution.py:330
  174.2 0.2 collective-permute-start.8
  174.4 2.8 %collective-permute-start.41 = (f32[1,96,384]{2,1,0:T(8,128)S(1)}, f32[1,96,384]{2,1,0:T(8,128)S(1)}, u32[]{:S(2)}, u32[]{:S(2)}) collective-permute-start(f32[1,96,384]{2,1,0:T(8,128)S(1)} %fusion.3), channel_id=1, source_target_pairs={{0,2},{1,3},{2,0},{3,1},{4,6},{5,7},{6,4},{7,5},{8,10},{9,11},{10,... | collective-permute-start | bytes 442376 | tf_op jit(solution)/shard_map/ppermute | solution.py:331
  177.2 0.2 collective-permute-start.39
  177.4 21.6 %collective-permute-done.24.refs_9_ = f32[2,96,384]{2,1,0:T(8,128)S(1)} collective-permute-done((f32[2,96,384]{2,1,0:T(8,128)S(1)}, f32[2,96,384]{2,1,0:T(8,128)S(1)}, u32[]{:S(2)}, u32[]{:S(2)}) %collective-permute-start.24) | collective-permute-done | bytes 294944 | tf_op jit(solution)/shard_map/ppermute | solution.py:331
  199.0 6.3 %collective-permute-done.16.refs_6_ = f32[2,96,384]{2,1,0:T(8,128)S(1)} collective-permute-done((f32[2,96,384]{2,1,0:T(8,128)S(1)}, f32[2,96,384]{2,1,0:T(8,128)S(1)}, u32[]{:S(2)}, u32[]{:S(2)}) %collective-permute-start.16) | collective-permute-done | bytes 294944 | tf_op jit(solution)/shard_map/ppermute | solution.py:331
  205.3 6.3 %collective-permute-done.8.refs_3_ = f32[2,96,384]{2,1,0:T(8,128)S(1)} collective-permute-done((f32[2,96,384]{2,1,0:T(8,128)S(1)}, f32[2,96,384]{2,1,0:T(8,128)S(1)}, u32[]{:S(2)}, u32[]{:S(2)}) %collective-permute-start.8) | collective-permute-done | bytes 294944 | tf_op jit(solution)/shard_map/ppermute | solution.py:331
  211.6 4.2 %finish_early.1 = (f32[2,3,96,384]{3,2,1,0:T(8,128)S(1)}, f32[2,96,384]{2,1,0:T(8,128)S(1)}, bf16[384,384]{1,0:T(8,128)(2,1)S(1)}, bf16[384,384]{1,0:T(8,128)(2,1)S(1)}) custom-call(s32[2]{0:T(128)S(1)} %pad_add_fusion.at, f32[2,4,96,384]{3,2,1,0:T(8,128)S(1)} %copy-done.2, f32[2,2,96,384]{3,2,1,0:T(8,128)S(1)} %get-tuple-element.28.refs_1_, ...), custom_call_target="tpu_custom_call" | custom-call | tf_op jit(solution)/shard_map/finish_early/pallas_call | solution.py:249
  215.8 1.5 finish_last.1
  (49 shorter events, 0.5 us)
Async XLA Ops:
  0.0 9.4 %copy-start = (f32[8,4,48,384]{3,2,1,0:T(8,128)S(1)}, f32[8,4,48,384]{3,2,1,0:T(8,128)}, u32[]{:S(2)}) copy-start(f32[8,4,48,384]{3,2,1,0:T(8,128)} %own_ref.7) | copy-start | bytes 7077892
  0.0 9.4 %collective-permute-start = (f32[8,4,48,384]{3,2,1,0:T(8,128)}, f32[8,4,48,384]{3,2,1,0:T(8,128)}, u32[]{:S(2)}, u32[]{:S(2)}) collective-permute-start(f32[8,4,48,384]{3,2,1,0:T(8,128)} %own_ref.7), channel_id=1, source_target_pairs={{0,4},{4,0},{8,12},{12,8},{16,20},{20,16},{24,28},{28,24},{1,5},{5... | collective-permute-start | bytes 7077896 | tf_op jit(solution)/shard_map/ppermute | solution.py:307
  2.7 3.0 %collective-permute-start.25 = (f32[8,1,48,384]{3,2,1,0:T(8,128)S(1)}, f32[8,1,48,384]{3,2,1,0:T(8,128)S(1)}, u32[]{:S(2)}, u32[]{:S(2)}) collective-permute-start(f32[8,1,48,384]{3,2,1,0:T(8,128)S(1)} %maximum_bitcast_fusion.mine.refs_10_), channel_id=1, source_target_pairs={{0,4},{4,0},{8,12},{12,8},{16,20},{20,16},{24,28},{28,24},{1,5},{5... | collective-permute-start | bytes 1769480 | tf_op jit(solution)/shard_map/ppermute | solution.py:309
  6.5 87.2 %copy-start.4 = (s32[2,8]{1,0:T(2,128)S(1)}, s32[2,8]{1,0:T(2,128)}, u32[]{:S(2)}) copy-start(s32[2,8]{1,0:T(2,128)} %bucket.1) | copy-start | bytes 196
  6.5 87.2 %copy-start.5 = (s32[2,8]{1,0:T(2,128)S(1)}, s32[2,8]{1,0:T(2,128)}, u32[]{:S(2)}) copy-start(s32[2,8]{1,0:T(2,128)} %flags.1) | copy-start | bytes 196
  6.5 13.2 %collective-permute-start.26 = (f32[2,4,48,384]{3,2,1,0:T(8,128)S(1)}, f32[2,4,48,384]{3,2,1,0:T(8,128)S(1)}, u32[]{:S(2)}, u32[]{:S(2)}) collective-permute-start(f32[2,4,48,384]{3,2,1,0:T(8,128)S(1)} %pack.3), channel_id=1, source_target_pairs={{0,8},{4,20},{8,0},{12,28},{16,24},{20,4},{24,16},{28,12},{1,9},{5... | collective-permute-start | bytes 1769480 | tf_op jit(solution)/shard_map/ppermute | solution.py:316
  12.2 20.0 %collective-permute-start.32 = (f32[2,4,48,384]{3,2,1,0:T(8,128)S(1)}, f32[2,4,48,384]{3,2,1,0:T(8,128)S(1)}, u32[]{:S(2)}, u32[]{:S(2)}) collective-permute-start(f32[2,4,48,384]{3,2,1,0:T(8,128)S(1)} %get-tuple-element.40), channel_id=1, source_target_pairs={{0,8},{4,20},{8,0},{12,28},{16,24},{20,4},{24,16},{28,12},{1,9},{5... | collective-permute-start | bytes 1769480 | tf_op jit(solution)/shard_map/ppermute | solution.py:316
  12.3 22.4 %collective-permute-start.33 = (f32[2,4,48,384]{3,2,1,0:T(8,128)S(1)}, f32[2,4,48,384]{3,2,1,0:T(8,128)S(1)}, u32[]{:S(2)}, u32[]{:S(2)}) collective-permute-start(f32[2,4,48,384]{3,2,1,0:T(8,128)S(1)} %get-tuple-element.40), channel_id=1, source_target_pairs={{0,16},{4,12},{8,24},{12,4},{16,0},{20,28},{24,8},{28,20},{1,17},{... | collective-permute-start | bytes 1769480 | tf_op jit(solution)/shard_map/ppermute | solution.py:317
  14.4 30.5 %collective-permute-start.17 = (f32[2,4,48,384]{3,2,1,0:T(8,128)S(1)}, f32[2,4,48,384]{3,2,1,0:T(8,128)S(1)}, u32[]{:S(2)}, u32[]{:S(2)}) collective-permute-start(f32[2,4,48,384]{3,2,1,0:T(8,128)S(1)} %get-tuple-element.33), channel_id=1, source_target_pairs={{0,8},{4,20},{8,0},{12,28},{16,24},{20,4},{24,16},{28,12},{1,9},{5... | collective-permute-start | bytes 1769480 | tf_op jit(solution)/shard_map/ppermute | solution.py:316
  15.9 31.5 %collective-permute-start.18 = (f32[2,4,48,384]{3,2,1,0:T(8,128)S(1)}, f32[2,4,48,384]{3,2,1,0:T(8,128)S(1)}, u32[]{:S(2)}, u32[]{:S(2)}) collective-permute-start(f32[2,4,48,384]{3,2,1,0:T(8,128)S(1)} %get-tuple-element.33), channel_id=1, source_target_pairs={{0,16},{4,12},{8,24},{12,4},{16,0},{20,28},{24,8},{28,20},{1,17},{... | collective-permute-start | bytes 1769480 | tf_op jit(solution)/shard_map/ppermute | solution.py:317
  19.6 80.5 %copy-start.3 = (s32[8,4]{0,1:T(4,128)S(1)}, s32[8,4]{0,1:T(4,128)}, u32[]{:S(2)}) copy-start(s32[8,4]{0,1:T(4,128)} %param.12) | copy-start | bytes 388
  19.6 37.9 %collective-permute-start.9 = (f32[2,4,48,384]{3,2,1,0:T(8,128)S(1)}, f32[2,4,48,384]{3,2,1,0:T(8,128)S(1)}, u32[]{:S(2)}, u32[]{:S(2)}) collective-permute-start(f32[2,4,48,384]{3,2,1,0:T(8,128)S(1)} %get-tuple-element.30), channel_id=1, source_target_pairs={{0,8},{4,20},{8,0},{12,28},{16,24},{20,4},{24,16},{28,12},{1,9},{5... | collective-permute-start | bytes 1769480 | tf_op jit(solution)/shard_map/ppermute | solution.py:316
  32.3 25.3 %collective-permute-start.10 = (f32[2,4,48,384]{3,2,1,0:T(8,128)S(1)}, f32[2,4,48,384]{3,2,1,0:T(8,128)S(1)}, u32[]{:S(2)}, u32[]{:S(2)}) collective-permute-start(f32[2,4,48,384]{3,2,1,0:T(8,128)S(1)} %get-tuple-element.30), channel_id=1, source_target_pairs={{0,16},{4,12},{8,24},{12,4},{16,0},{20,28},{24,8},{28,20},{1,17},{... | collective-permute-start | bytes 1769480 | tf_op jit(solution)/shard_map/ppermute | solution.py:317
  34.7 35.5 %collective-permute-start.1 = (f32[2,4,48,384]{3,2,1,0:T(8,128)S(1)}, f32[2,4,48,384]{3,2,1,0:T(8,128)S(1)}, u32[]{:S(2)}, u32[]{:S(2)}) collective-permute-start(f32[2,4,48,384]{3,2,1,0:T(8,128)S(1)} %get-tuple-element.27), channel_id=1, source_target_pairs={{0,8},{4,20},{8,0},{12,28},{16,24},{20,4},{24,16},{28,12},{1,9},{5... | collective-permute-start | bytes 1769480 | tf_op jit(solution)/shard_map/ppermute | solution.py:316
  44.9 27.7 %collective-permute-start.2 = (f32[2,4,48,384]{3,2,1,0:T(8,128)S(1)}, f32[2,4,48,384]{3,2,1,0:T(8,128)S(1)}, u32[]{:S(2)}, u32[]{:S(2)}) collective-permute-start(f32[2,4,48,384]{3,2,1,0:T(8,128)S(1)} %get-tuple-element.27), channel_id=1, source_target_pairs={{0,16},{4,12},{8,24},{12,4},{16,0},{20,28},{24,8},{28,20},{1,17},{... | collective-permute-start | bytes 1769480 | tf_op jit(solution)/shard_map/ppermute | solution.py:317
  47.3 26.3 %collective-permute-start.34 = (f32[2,4,48,384]{3,2,1,0:T(8,128)S(1)}, f32[2,4,48,384]{3,2,1,0:T(8,128)S(1)}, u32[]{:S(2)}, u32[]{:S(2)}) collective-permute-start(f32[2,4,48,384]{3,2,1,0:T(8,128)S(1)} %collective-permute-done.32.rest_0_), channel_id=1, source_target_pairs={{0,16},{4,12},{8,24},{12,4},{16,0},{20,28},{24,8},{28,20},{1,17},{... | collective-permute-start | bytes 1769480 | tf_op jit(solution)/shard_map/ppermute | solution.py:318
  57.6 16.4 %collective-permute-start.35 = (f32[2,4,48,384]{3,2,1,0:T(8,128)S(1)}, f32[2,4,48,384]{3,2,1,0:T(8,128)S(1)}, u32[]{:S(2)}, u32[]{:S(2)}) collective-permute-start(f32[2,4,48,384]{3,2,1,0:T(8,128)S(1)} %collective-permute-done.32.rest_0_), channel_id=1, source_target_pairs={{0,4},{4,0},{8,12},{12,8},{16,20},{20,16},{24,28},{28,24},{1,5},{5... | collective-permute-start | bytes 1769480 | tf_op jit(solution)/shard_map/ppermute | solution.py:319
  57.6 18.4 %collective-permute-start.36 = (f32[2,4,48,384]{3,2,1,0:T(8,128)S(1)}, f32[2,4,48,384]{3,2,1,0:T(8,128)S(1)}, u32[]{:S(2)}, u32[]{:S(2)}) collective-permute-start(f32[2,4,48,384]{3,2,1,0:T(8,128)S(1)} %collective-permute-done.33.rest_1_), channel_id=1, source_target_pairs={{0,4},{4,0},{8,12},{12,8},{16,20},{20,16},{24,28},{28,24},{1,5},{5... | collective-permute-start | bytes 1769480 | tf_op jit(solution)/shard_map/ppermute | solution.py:319
  70.2 10.3 %collective-permute-start.19 = (f32[2,4,48,384]{3,2,1,0:T(8,128)S(1)}, f32[2,4,48,384]{3,2,1,0:T(8,128)S(1)}, u32[]{:S(2)}, u32[]{:S(2)}) collective-permute-start(f32[2,4,48,384]{3,2,1,0:T(8,128)S(1)} %collective-permute-done.17.rest_0_), channel_id=1, source_target_pairs={{0,16},{4,12},{8,24},{12,4},{16,0},{20,28},{24,8},{28,20},{1,17},{... | collective-permute-start | bytes 1769480 | tf_op jit(solution)/shard_map/ppermute | solution.py:318
  72.6 7.9 %collective-permute-start.20 = (f32[2,4,48,384]{3,2,1,0:T(8,128)S(1)}, f32[2,4,48,384]{3,2,1,0:T(8,128)S(1)}, u32[]{:S(2)}, u32[]{:S(2)}) collective-permute-start(f32[2,4,48,384]{3,2,1,0:T(8,128)S(1)} %collective-permute-done.17.rest_0_), channel_id=1, source_target_pairs={{0,4},{4,0},{8,12},{12,8},{16,20},{20,16},{24,28},{28,24},{1,5},{5... | collective-permute-start | bytes 1769480 | tf_op jit(solution)/shard_map/ppermute | solution.py:319
  73.6 9.0 %collective-permute-start.21 = (f32[2,4,48,384]{3,2,1,0:T(8,128)S(1)}, f32[2,4,48,384]{3,2,1,0:T(8,128)S(1)}, u32[]{:S(2)}, u32[]{:S(2)}) collective-permute-start(f32[2,4,48,384]{3,2,1,0:T(8,128)S(1)} %collective-permute-done.18.rest_1_), channel_id=1, source_target_pairs={{0,4},{4,0},{8,12},{12,8},{16,20},{20,16},{24,28},{28,24},{1,5},{5... | collective-permute-start | bytes 1769480 | tf_op jit(solution)/shard_map/ppermute | solution.py:319
  74.0 12.8 %collective-permute-start.11 = (f32[2,4,48,384]{3,2,1,0:T(8,128)S(1)}, f32[2,4,48,384]{3,2,1,0:T(8,128)S(1)}, u32[]{:S(2)}, u32[]{:S(2)}) collective-permute-start(f32[2,4,48,384]{3,2,1,0:T(8,128)S(1)} %collective-permute-done.9.rest_0_), channel_id=1, source_target_pairs={{0,16},{4,12},{8,24},{12,4},{16,0},{20,28},{24,8},{28,20},{1,17},{... | collective-permute-start | bytes 1769480 | tf_op jit(solution)/shard_map/ppermute | solution.py:318
  76.0 10.9 %collective-permute-start.12 = (f32[2,4,48,384]{3,2,1,0:T(8,128)S(1)}, f32[2,4,48,384]{3,2,1,0:T(8,128)S(1)}, u32[]{:S(2)}, u32[]{:S(2)}) collective-permute-start(f32[2,4,48,384]{3,2,1,0:T(8,128)S(1)} %collective-permute-done.9.rest_0_), channel_id=1, source_target_pairs={{0,4},{4,0},{8,12},{12,8},{16,20},{20,16},{24,28},{28,24},{1,5},{5... | collective-permute-start | bytes 1769480 | tf_op jit(solution)/shard_map/ppermute | solution.py:319
  80.5 6.8 %collective-permute-start.13 = (f32[2,4,48,384]{3,2,1,0:T(8,128)S(1)}, f32[2,4,48,384]{3,2,1,0:T(8,128)S(1)}, u32[]{:S(2)}, u32[]{:S(2)}) collective-permute-start(f32[2,4,48,384]{3,2,1,0:T(8,128)S(1)} %collective-permute-done.10.rest_1_), channel_id=1, source_target_pairs={{0,4},{4,0},{8,12},{12,8},{16,20},{20,16},{24,28},{28,24},{1,5},{5... | collective-permute-start | bytes 1769480 | tf_op jit(solution)/shard_map/ppermute | solution.py:319
  80.6 12.5 %collective-permute-start.3 = (f32[2,4,48,384]{3,2,1,0:T(8,128)S(1)}, f32[2,4,48,384]{3,2,1,0:T(8,128)S(1)}, u32[]{:S(2)}, u32[]{:S(2)}) collective-permute-start(f32[2,4,48,384]{3,2,1,0:T(8,128)S(1)} %collective-permute-done.1.rest_0_), channel_id=1, source_target_pairs={{0,16},{4,12},{8,24},{12,4},{16,0},{20,28},{24,8},{28,20},{1,17},{... | collective-permute-start | bytes 1769480 | tf_op jit(solution)/shard_map/ppermute | solution.py:318
  82.6 10.6 %collective-permute-start.22 = (f32[2,4,48,384]{3,2,1,0:T(8,128)S(1)}, f32[2,4,48,384]{3,2,1,0:T(8,128)S(1)}, u32[]{:S(2)}, u32[]{:S(2)}) collective-permute-start(f32[2,4,48,384]{3,2,1,0:T(8,128)S(1)} %collective-permute-done.19.rest_2_), channel_id=1, source_target_pairs={{0,4},{4,0},{8,12},{12,8},{16,20},{20,16},{24,28},{28,24},{1,5},{5... | collective-permute-start | bytes 1769480 | tf_op jit(solution)/shard_map/ppermute | solution.py:319
  86.8 23.3 %collective-permute-start.4 = (f32[2,4,48,384]{3,2,1,0:T(8,128)S(1)}, f32[2,4,48,384]{3,2,1,0:T(8,128)S(1)}, u32[]{:S(2)}, u32[]{:S(2)}) collective-permute-start(f32[2,4,48,384]{3,2,1,0:T(8,128)S(1)} %collective-permute-done.1.rest_0_), channel_id=1, source_target_pairs={{0,4},{4,0},{8,12},{12,8},{16,20},{20,16},{24,28},{28,24},{1,5},{5... | collective-permute-start | bytes 1769480 | tf_op jit(solution)/shard_map/ppermute | solution.py:319
  86.9 25.3 %collective-permute-start.5 = (f32[2,4,48,384]{3,2,1,0:T(8,128)S(1)}, f32[2,4,48,384]{3,2,1,0:T(8,128)S(1)}, u32[]{:S(2)}, u32[]{:S(2)}) collective-permute-start(f32[2,4,48,384]{3,2,1,0:T(8,128)S(1)} %collective-permute-done.2.rest_1_), channel_id=1, source_target_pairs={{0,4},{4,0},{8,12},{12,8},{16,20},{20,16},{24,28},{28,24},{1,5},{5... | collective-permute-start | bytes 1769480 | tf_op jit(solution)/shard_map/ppermute | solution.py:319
  87.3 25.0 %collective-permute-start.37 = (f32[2,4,48,384]{3,2,1,0:T(8,128)S(1)}, f32[2,4,48,384]{3,2,1,0:T(8,128)S(1)}, u32[]{:S(2)}, u32[]{:S(2)}) collective-permute-start(f32[2,4,48,384]{3,2,1,0:T(8,128)S(1)} %collective-permute-done.34.rest_2_), channel_id=1, source_target_pairs={{0,4},{4,0},{8,12},{12,8},{16,20},{20,16},{24,28},{28,24},{1,5},{5... | collective-permute-start | bytes 1769480 | tf_op jit(solution)/shard_map/ppermute | solution.py:319
  93.1 31.1 %collective-permute-start.14 = (f32[2,4,48,384]{3,2,1,0:T(8,128)S(1)}, f32[2,4,48,384]{3,2,1,0:T(8,128)S(1)}, u32[]{:S(2)}, u32[]{:S(2)}) collective-permute-start(f32[2,4,48,384]{3,2,1,0:T(8,128)S(1)} %collective-permute-done.11.rest_2_), channel_id=1, source_target_pairs={{0,4},{4,0},{8,12},{12,8},{16,20},{20,16},{24,28},{28,24},{1,5},{5... | collective-permute-start | bytes 1769480 | tf_op jit(solution)/shard_map/ppermute | solution.py:319
  93.2 41.3 %collective-permute-start.6 = (f32[2,4,48,384]{3,2,1,0:T(8,128)S(1)}, f32[2,4,48,384]{3,2,1,0:T(8,128)S(1)}, u32[]{:S(2)}, u32[]{:S(2)}) collective-permute-start(f32[2,4,48,384]{3,2,1,0:T(8,128)S(1)} %collective-permute-done.3.rest_2_), channel_id=1, source_target_pairs={{0,4},{4,0},{8,12},{12,8},{16,20},{20,16},{24,28},{28,24},{1,5},{5... | collective-permute-start | bytes 1769480 | tf_op jit(solution)/shard_map/ppermute | solution.py:319
  93.6 3.7 %copy-start.1 = (f32[2,8,384,384]{3,2,1,0:T(8,128)S(1)}, f32[2,8,384,384]{3,2,1,0:T(8,128)}, u32[]{:S(2)}) copy-start(f32[2,8,384,384]{3,2,1,0:T(8,128)} %source.1) | copy-start | bytes 28311556
  110.1 36.5 %collective-permute-start.27 = (f32[2,4,48,384]{3,2,1,0:T(8,128)S(1)}, f32[2,4,48,384]{3,2,1,0:T(8,128)S(1)}, u32[]{:S(2)}, u32[]{:S(2)}) collective-permute-start(f32[2,4,48,384]{3,2,1,0:T(8,128)S(1)} %pack.3), channel_id=1, source_target_pairs={{0,16},{4,12},{8,24},{12,4},{16,0},{20,28},{24,8},{28,20},{1,17},{... | collective-permute-start | bytes 1769480 | tf_op jit(solution)/shard_map/ppermute | solution.py:317
  112.2 34.5 %collective-permute-start.28 = (f32[2,4,48,384]{3,2,1,0:T(8,128)S(1)}, f32[2,4,48,384]{3,2,1,0:T(8,128)S(1)}, u32[]{:S(2)}, u32[]{:S(2)}) collective-permute-start(f32[2,4,48,384]{3,2,1,0:T(8,128)S(1)} %collective-permute-done.26.refs_12_), channel_id=1, source_target_pairs={{0,16},{4,12},{8,24},{12,4},{16,0},{20,28},{24,8},{28,20},{1,17},{... | collective-permute-start | bytes 1769480 | tf_op jit(solution)/shard_map/ppermute | solution.py:318
  112.3 34.9 %collective-permute-start.23 = (f32[2,2,96,384]{3,2,1,0:T(8,128)S(1)}, f32[2,2,96,384]{3,2,1,0:T(8,128)S(1)}, u32[]{:S(2)}, u32[]{:S(2)}) collective-permute-start(f32[2,2,96,384]{3,2,1,0:T(8,128)S(1)} %get-tuple-element.35), channel_id=1, source_target_pairs={{0,1},{1,0},{2,3},{3,2},{4,5},{5,4},{6,7},{7,6},{8,9},{9,8},{10,11... | collective-permute-start | bytes 1769480 | tf_op jit(solution)/shard_map/ppermute | solution.py:330
  124.2 22.3 %collective-permute-start.40 = (f32[2,1,96,384]{3,2,1,0:T(8,128)S(1)}, f32[2,1,96,384]{3,2,1,0:T(8,128)S(1)}, u32[]{:S(2)}, u32[]{:S(2)}) collective-permute-start(f32[2,1,96,384]{3,2,1,0:T(8,128)S(1)} %get-tuple-element.44), channel_id=1, source_target_pairs={{0,1},{1,0},{2,3},{3,2},{4,5},{5,4},{6,7},{7,6},{8,9},{9,8},{10,11... | collective-permute-start | bytes 884744 | tf_op jit(solution)/shard_map/ppermute | solution.py:330
  134.5 15.8 %collective-permute-start.15 = (f32[2,2,96,384]{3,2,1,0:T(8,128)S(1)}, f32[2,2,96,384]{3,2,1,0:T(8,128)S(1)}, u32[]{:S(2)}, u32[]{:S(2)}) collective-permute-start(f32[2,2,96,384]{3,2,1,0:T(8,128)S(1)} %get-tuple-element.32), channel_id=1, source_target_pairs={{0,1},{1,0},{2,3},{3,2},{4,5},{5,4},{6,7},{7,6},{8,9},{9,8},{10,11... | collective-permute-start | bytes 1769480 | tf_op jit(solution)/shard_map/ppermute | solution.py:330
  146.5 65.1 %copy-start.2 = (f32[2,4,96,384]{3,2,1,0:T(8,128)S(1)}, f32[2,4,96,384]{3,2,1,0:T(8,128)}, u32[]{:S(2)}) copy-start(f32[2,4,96,384]{3,2,1,0:T(8,128)} %diag_ref.1) | copy-start | bytes 3538948
  146.5 16.4 %collective-permute-start.7 = (f32[2,2,96,384]{3,2,1,0:T(8,128)S(1)}, f32[2,2,96,384]{3,2,1,0:T(8,128)S(1)}, u32[]{:S(2)}, u32[]{:S(2)}) collective-permute-start(f32[2,2,96,384]{3,2,1,0:T(8,128)S(1)} %get-tuple-element.29), channel_id=1, source_target_pairs={{0,1},{1,0},{2,3},{3,2},{4,5},{5,4},{6,7},{7,6},{8,9},{9,8},{10,11... | collective-permute-start | bytes 1769480 | tf_op jit(solution)/shard_map/ppermute | solution.py:330
  146.6 19.2 %collective-permute-start.29 = (f32[2,4,48,384]{3,2,1,0:T(8,128)S(1)}, f32[2,4,48,384]{3,2,1,0:T(8,128)S(1)}, u32[]{:S(2)}, u32[]{:S(2)}) collective-permute-start(f32[2,4,48,384]{3,2,1,0:T(8,128)S(1)} %collective-permute-done.26.refs_12_), channel_id=1, source_target_pairs={{0,4},{4,0},{8,12},{12,8},{16,20},{20,16},{24,28},{28,24},{1,5},{5... | collective-permute-start | bytes 1769480 | tf_op jit(solution)/shard_map/ppermute | solution.py:319
  146.7 27.7 %collective-permute-start.30 = (f32[2,4,48,384]{3,2,1,0:T(8,128)S(1)}, f32[2,4,48,384]{3,2,1,0:T(8,128)S(1)}, u32[]{:S(2)}, u32[]{:S(2)}) collective-permute-start(f32[2,4,48,384]{3,2,1,0:T(8,128)S(1)} %collective-permute-done.27.refs_13_), channel_id=1, source_target_pairs={{0,4},{4,0},{8,12},{12,8},{16,20},{20,16},{24,28},{28,24},{1,5},{5... | collective-permute-start | bytes 1769480 | tf_op jit(solution)/shard_map/ppermute | solution.py:319
  147.2 30.0 %collective-permute-start.31 = (f32[2,4,48,384]{3,2,1,0:T(8,128)S(1)}, f32[2,4,48,384]{3,2,1,0:T(8,128)S(1)}, u32[]{:S(2)}, u32[]{:S(2)}) collective-permute-start(f32[2,4,48,384]{3,2,1,0:T(8,128)S(1)} %collective-permute-done.28.refs_14_), channel_id=1, source_target_pairs={{0,4},{4,0},{8,12},{12,8},{16,20},{20,16},{24,28},{28,24},{1,5},{5... | collective-permute-start | bytes 1769480 | tf_op jit(solution)/shard_map/ppermute | solution.py:319
  150.3 23.9 %collective-permute-start.38 = (f32[2,1,96,384]{3,2,1,0:T(8,128)S(1)}, f32[2,1,96,384]{3,2,1,0:T(8,128)S(1)}, u32[]{:S(2)}, u32[]{:S(2)}) collective-permute-start(f32[2,1,96,384]{3,2,1,0:T(8,128)S(1)} %get-tuple-element.42), channel_id=1, source_target_pairs={{0,1},{1,0},{2,3},{3,2},{4,5},{5,4},{6,7},{7,6},{8,9},{9,8},{10,11... | collective-permute-start | bytes 884744 | tf_op jit(solution)/shard_map/ppermute | solution.py:330
  162.9 36.1 %collective-permute-start.24 = (f32[2,96,384]{2,1,0:T(8,128)S(1)}, f32[2,96,384]{2,1,0:T(8,128)S(1)}, u32[]{:S(2)}, u32[]{:S(2)}) collective-permute-start(f32[2,96,384]{2,1,0:T(8,128)S(1)} %fusion), channel_id=1, source_target_pairs={{0,2},{1,3},{2,0},{3,1},{4,6},{5,7},{6,4},{7,5},{8,10},{9,11},{10,... | collective-permute-start | bytes 884744 | tf_op jit(solution)/shard_map/ppermute | solution.py:331
  165.8 39.5 %collective-permute-start.16 = (f32[2,96,384]{2,1,0:T(8,128)S(1)}, f32[2,96,384]{2,1,0:T(8,128)S(1)}, u32[]{:S(2)}, u32[]{:S(2)}) collective-permute-start(f32[2,96,384]{2,1,0:T(8,128)S(1)} %fusion.1), channel_id=1, source_target_pairs={{0,2},{1,3},{2,0},{3,1},{4,6},{5,7},{6,4},{7,5},{8,10},{9,11},{10,... | collective-permute-start | bytes 884744 | tf_op jit(solution)/shard_map/ppermute | solution.py:331
  174.2 37.4 %collective-permute-start.8 = (f32[2,96,384]{2,1,0:T(8,128)S(1)}, f32[2,96,384]{2,1,0:T(8,128)S(1)}, u32[]{:S(2)}, u32[]{:S(2)}) collective-permute-start(f32[2,96,384]{2,1,0:T(8,128)S(1)} %fusion.2), channel_id=1, source_target_pairs={{0,2},{1,3},{2,0},{3,1},{4,6},{5,7},{6,4},{7,5},{8,10},{9,11},{10,... | collective-permute-start | bytes 884744 | tf_op jit(solution)/shard_map/ppermute | solution.py:331
  174.4 41.4 %collective-permute-start.41 = (f32[1,96,384]{2,1,0:T(8,128)S(1)}, f32[1,96,384]{2,1,0:T(8,128)S(1)}, u32[]{:S(2)}, u32[]{:S(2)}) collective-permute-start(f32[1,96,384]{2,1,0:T(8,128)S(1)} %fusion.3), channel_id=1, source_target_pairs={{0,2},{1,3},{2,0},{3,1},{4,6},{5,7},{6,4},{7,5},{8,10},{9,11},{10,... | collective-permute-start | bytes 442376 | tf_op jit(solution)/shard_map/ppermute | solution.py:331
  177.2 38.6 %collective-permute-start.39 = (f32[1,96,384]{2,1,0:T(8,128)S(1)}, f32[1,96,384]{2,1,0:T(8,128)S(1)}, u32[]{:S(2)}, u32[]{:S(2)}) collective-permute-start(f32[1,96,384]{2,1,0:T(8,128)S(1)} %fusion.4), channel_id=1, source_target_pairs={{0,2},{1,3},{2,0},{3,1},{4,6},{5,7},{6,4},{7,5},{8,10},{9,11},{10,... | collective-permute-start | bytes 442376 | tf_op jit(solution)/shard_map/ppermute | solution.py:331

commit v3 on v2

--- a/solution.py
+++ b/solution.py
@@ -84,26 +84,22 @@
     )(l_bucket, present, l_cores)
 
 
-def pack(own, twin, place):
-    pivots, columns, rows, width = own.shape
-    half = pivots // 2
+def pack(own, twin, place, chunks):
+    half, rows = own.shape[0] // 2, own.shape[2]
 
     def body(at, mine, other, *outs):
         core = at[0] % 2
-        for column in range(columns):
-            outs[column][core] = mine[:, column]
-            outs[column][1 - core] = other[:, column]
-
-    source = pl.BlockSpec((1, columns, rows, width), lambda k, at: (half * (at[0] % 2) + k, 0, 0, 0))
-    return pl.pallas_call(
-        body,
-        grid_spec=pltpu.PrefetchScalarGridSpec(
-            num_scalar_prefetch=1,
-            grid=(half,),
-            in_specs=[source, source],
-            out_specs=[pl.BlockSpec((2, 1, rows, width), lambda k, at: (0, k, 0, 0))] * columns,
-        ),
-        out_shape=[jax.ShapeDtypeStruct((2, half, rows, width), F32)] * columns,
+        for (column, lane, lanes), out in zip(chunks, outs):
+            for k in range(half):
+                out[core, k] = mine[half * core + k, column, :, lane : lane + lanes]
+                out[1 - core, k] = other[half * core + k, column, :, lane : lane + lanes]
+
+    vmem = pl.BlockSpec(memory_space=pltpu.VMEM)
+    return pl.pallas_call(
+        body,
+        in_specs=[pl.BlockSpec(memory_space=pltpu.SMEM), vmem, vmem],
+        out_specs=[vmem] * len(chunks),
+        out_shape=[jax.ShapeDtypeStruct((2, half, rows, lanes), F32) for _, _, lanes in chunks],
         compiler_params=pltpu.CompilerParams(vmem_limit_bytes=LIMIT),
         name="pack",
     )(place, own, twin)
@@ -124,7 +120,8 @@
             store(chip + core, part(core))
 
 
-def multiply(j, pieces, place, u_bucket, lower, own, twin, mine, theirs):
+def multiply(chunk, place, u_bucket, lower, own, twin, mine, theirs):
+    j, lane, lanes = chunk
     high, low = lower
     pairs, height, depth = high.shape
     rows, width = own.shape[-2:]
@@ -132,14 +129,13 @@
     step = width // 3
     half = pairs // 2
     share = width // 4
-    each = tiles // pieces
 
     def body(at, bucket, lhs_high, lhs_low, own_ref, twin_ref, *rest):
         parts, others = rest[:3], rest[3:6]
-        keep, send = rest[6 : 6 + pieces], rest[6 + pieces : 6 + 2 * pieces]
-        rhs_high, rhs_low, total = rest[6 + 2 * pieces :]
+        keep, send, (rhs_high, rhs_low, total) = rest[6:8], rest[8:10], rest[10:]
         core, z = at[0] % 2, at[1]
-        row = lax.broadcasted_iota(jnp.int32, (rows, width), 0)
+        row = lax.broadcasted_iota(jnp.int32, (rows, lanes), 0)
+        span = slice(lane, lane + lanes)
         for turn, (bundle, refs) in enumerate(((core, parts), (1 - core, others))):
             for local in range(half):
                 slot = turn * half + local
@@ -154,7 +150,7 @@
                         rhs_low[slot, pl.ds(k * width + start, rows)] = b
 
                     gather_tile(
-                        at, bundle, own_ref[2 * p + k, j], twin_ref[2 * p + k, j],
+                        at, bundle, own_ref[2 * p + k, j, :, span], twin_ref[2 * p + k, j, :, span],
                         [lambda s, r=r: r[s, 2 * local + k] for r in refs], store,
                     )
                 a, b = lhs_high[p], lhs_low[p]
@@ -170,23 +166,28 @@
         for slot, (target, block) in enumerate(((keep, z), (keep, z ^ 2), (send, z ^ 1), (send, z ^ 3))):
             for i in range(tiles):
                 start = pl.multiple_of(block * share, 8)
-                target[i // each][slot % 2, i % each] = total[pl.ds(i * width + start, share)]
-
-    shape = jax.ShapeDtypeStruct((2, each, share, width), F32)
+                target[slot % 2][i] = total[pl.ds(i * width + start, share)]
+
+    shape = jax.ShapeDtypeStruct((tiles, share, lanes), F32)
     vmem = pl.BlockSpec(memory_space=pltpu.VMEM)
     smem = pl.BlockSpec(memory_space=pltpu.SMEM)
     return pl.pallas_call(
         body,
         in_specs=[smem, smem] + [vmem] * 10,
-        out_specs=[vmem] * (2 * pieces),
+        out_specs=[vmem] * 4,
         scratch_shapes=[
-            pltpu.VMEM((pairs, depth, width), BF16),
-            pltpu.VMEM((pairs, depth, width), BF16),
-            pltpu.VMEM((height, width), F32),
+            pltpu.VMEM((pairs, depth, lanes), BF16),
+            pltpu.VMEM((pairs, depth, lanes), BF16),
+            pltpu.VMEM((height, lanes), F32),
         ],
-        out_shape=[shape] * (2 * pieces),
+        out_shape=[shape] * 4,
         compiler_params=pltpu.CompilerParams(vmem_limit_bytes=LIMIT),
     )(place, u_bucket, high, low, own, twin, *mine, *theirs)
+
+
+def joined(parts):
+    terms = [parts[n][...] + parts[n + 1][...] + parts[n + 2][...] for n in range(0, len(parts), 3)]
+    return terms[0] if len(terms) == 1 else jnp.concatenate(terms, axis=-1)
 
 
 def finish_early(place, columns, diag, sums, own, twin, mine, theirs):
@@ -194,11 +195,11 @@
     rows = own.shape[-2]
     half = own.shape[0] // 2
     height = tiles * share
+    count = sum(len(part) for part in sums)
 
     def body(at, *refs):
         diag_ref = refs[0]
-        parts = refs[1 : 1 + 3 * (columns - 1)]
-        refs = refs[1 + 3 * (columns - 1) :]
+        parts, refs = refs[1 : 1 + 3 * count], refs[1 + 3 * count :]
         own_ref, twin_ref, refs = refs[0], refs[1], refs[2:]
         pieces, others, refs = refs[:3], refs[3:6], refs[6:]
         done, linked_ref, last_high, last_low, mat_high, mat_low = refs
@@ -229,8 +230,9 @@
 
         linked = None
         for column in range(columns - 1):
-            keep, near, far = (parts[3 * column + n] for n in range(3))
-            reduced = (diag_ref[:, column] - (keep[0] + near[0] + far[...])).reshape(height, width)
+            first = 3 * sum(len(part) for part in sums[:column])
+            update = joined(parts[first : first + 3 * len(sums[column])])
+            reduced = (diag_ref[:, column] - update).reshape(height, width)
             if linked is not None:
                 reduced = reduced - linked
             previous = dot3(halves(reduced), mat_high[column], mat_low[column])
@@ -241,8 +243,8 @@
         last_low[...] = mat_low[columns - 1]
 
     operands = [diag]
-    for keep, near, far in sums:
-        operands += [keep, near, far]
+    for part in sums:
+        operands += [value for chunk in part for value in chunk]
     operands += [own, twin, *mine, *theirs]
     square = jax.ShapeDtypeStruct((width, width), BF16)
     vmem = pl.BlockSpec(memory_space=pltpu.VMEM)
@@ -264,20 +266,15 @@
 
 def finish_last(columns, diag, done, linked, last_high, last_low, parts):
     tiles, _, share, width = diag.shape
-    each = tiles // len(parts)
-    height = each * share
+    height = tiles * share
 
     def body(diag_ref, done_ref, linked_ref, high, low, *rest):
         out = rest[-1]
         for column in range(columns - 1):
             out[:, column] = done_ref[:, column]
-        for n in range(len(parts)):
-            keep, near, far = rest[3 * n : 3 * n + 3]
-            span = slice(n * each, (n + 1) * each)
-            update = keep[0] + near[0] + far[...]
-            reduced = diag_ref[span, columns - 1] - update - linked_ref[span]
-            value = dot3(halves(reduced.reshape(height, width)), high[...], low[...])
-            out[span, columns - 1] = value.reshape(each, share, width)
+        reduced = diag_ref[:, columns - 1] - joined(rest[:-1]) - linked_ref[...]
+        value = dot3(halves(reduced.reshape(height, width)), high[...], low[...])
+        out[:, columns - 1] = value.reshape(tiles, share, width)
 
     return pl.pallas_call(
         body,
@@ -293,8 +290,14 @@
     return [(d, d ^ first_of_core[d % 2]) for d in range(size)]
 
 
+def chunks_of(columns, width):
+    step = width // 3
+    last = columns - 1
+    return [(column, 0, width) for column in range(last)] + [(last, 0, 2 * step), (last, 2 * step, step)]
+
+
 def cube_device(l_cores, l_bucket, present, u_cores, u_bucket, diag_cores, pivot_inv, coupling):
-    columns, tiles = u_cores.shape[1], l_cores.shape[0]
+    columns = u_cores.shape[1]
     size = lax.axis_size("row")
     first = functools.partial(lax.ppermute, axis_name="row", perm=moves(size, (2, 4)))
     second = functools.partial(lax.ppermute, axis_name="row", perm=moves(size, (4, 2)))
@@ -307,9 +310,11 @@
     u_twin = twin_of(u_cores)
     small = jnp.concatenate([pivot_inv, coupling, pivot_inv[:1]], axis=0)[:, None]
     small_twin = twin_of(small)
-    bundles = pack(u_cores, u_twin, place)
+    width = u_cores.shape[-1]
+    chunks = chunks_of(columns, width)
+    bundles = pack(u_cores, u_twin, place, chunks)
     lower = split_lower(l_cores, l_bucket, present)
-    bundles += pack(small, small_twin, place)
+    bundles += pack(small, small_twin, place, [(0, 0, width)])
 
     gathered = []
     for bundle in bundles:
@@ -319,20 +324,14 @@
         twins = tuple(twin_of(v) for v in (a, b, c))
         gathered.append(((a, b, c), twins))
 
-    sums = []
+    sums = [[] for _ in range(columns)]
     bucket = u_bucket.T
-    for j in range(columns):
-        pieces = tiles if j == columns - 1 else 1
-        outs = multiply(j, pieces, place, bucket, lower, u_cores, u_twin, *gathered[j])
-        parts = []
-        for n in range(pieces):
-            keep, send = outs[n], outs[pieces + n]
-            near = near_of(send)
-            far = far_of(keep[1] + near[1])
-            parts.append((keep, near, far))
-        sums.append(parts)
+    for n, chunk in enumerate(chunks):
+        own, relayed, send, onward = multiply(chunk, place, bucket, lower, u_cores, u_twin, *gathered[n])
+        far = far_of(relayed + near_of(onward))
+        sums[chunk[0]].append((own, near_of(send), far))
     done, linked, last_high, last_low = finish_early(
-        place, columns, diag_cores, [p[0] for p in sums[:-1]], small, small_twin, *gathered[columns],
+        place, columns, diag_cores, sums[:-1], small, small_twin, *gathered[len(chunks)],
     )
     return finish_last(columns, diag_cores, done, linked, last_high, last_low, sums[-1])
 

time: 218 us -> 243 us (1.11)
  waiting for transfers between devices: 118 us -> 137 us
  starting transfers between devices: 40.7 us -> 46.2 us
    ppermute x5 -> x6, waiting for transfers between devices: 15.3 us -> 36.5 us  [cube_device(): c = second(a)]
    ppermute x5 -> x6, waiting for transfers between devices: 44.5 us -> 28.1 us  [cube_device(): a = first(bundle)]
    ppermute x5 -> x6, waiting for transfers between devices: 0.01 us -> 10.8 us  [cube_device(): b = second(bundle)]
    ppermute x5 -> x6, starting transfers between devices: 8.39 us -> 11.6 us  [cube_device(): a = first(bundle)]
    ppermute x10 -> x15, waiting for transfers between devices: 55.5 us -> 58.3 us  [the longest x10 35.4 us: cube_device(): far = far_of(relayed + near_of(onward))]
    ppermute x5 -> x6, starting transfers between devices: 9.47 us -> 6.84 us  [cube_device(): b = second(bundle)]
    ppermute x10 -> x15, starting transfers between devices: 12.9 us -> 15.2 us  [the longest x10 10.5 us: cube_device(): far = far_of(relayed + near_of(onward))]
    pallas_call x4 -> x5, Pallas kernels: 39.9 us -> 42.1 us  [multiply(): pl.pallas_call(body, in_specs=[smem, smem] + [vmem] * 10, out_specs=[vmem...]
  transfers between devices with their start and end apart: 42 -> 53, of which waited for: 16 -> 20; matrix products, arithmetic and copies ran while one was open for 1% -> 1% of each run, Pallas kernels for 23% -> 21%
where the time goes in v3:
time: 243 us; the launch traced here: 242 us
  waiting for transfers between devices  137 us (56%)
  Pallas kernels  53 us (22%)
  starting transfers between devices  46.2 us (19%)
  local copies, waits for them, and re-layouts  4.81 us (2%)
    pallas_call x5, Pallas kernels, multiply(): pl.pallas_call(body, in_specs=[smem, smem] + [vmem] * 10, out_specs=[vmem...  42.1 us
    ppermute x6, waiting for transfers between devices, cube_device(): c = second(a)  36.5 us
    ppermute x10, waiting for transfers between devices, cube_device(): far = far_of(relayed + near_of(onward))  35.4 us
    ppermute x6, waiting for transfers between devices, cube_device(): a = first(bundle)  28.1 us
    ppermute x5, waiting for transfers between devices, cube_device(): sums[chunk[0]].append((own, near_of(send), far))  22.9 us
    ppermute x6, starting transfers between devices, cube_device(): a = first(bundle)  11.6 us
    ppermute x6, waiting for transfers between devices, cube_device(): b = second(bundle)  10.8 us
    ppermute x10, starting transfers between devices, cube_device(): far = far_of(relayed + near_of(onward))  10.5 us
  transfers between devices with their start and end apart: 53, of which 20 were waited for; matrix products, arithmetic and copies ran while one was open for 1% of the time, Pallas kernels for 21%

profile of v3, /device:TPU:0, one launch (start us, length us, event | category | flops | bytes accessed | tf_op | source)
XLA Modules:
  0.0 242.2 jit_solution(12733096207811349721)
XLA Ops:
  0.5 1.1 slice.3
  1.6 1.1 maximum_bitcast_fusion.mine.refs_10_
  2.9 2.8 %collective-permute-done.28.other.refs_11_ = f32[8,1,48,384]{3,2,1,0:T(8,128)S(1)} collective-permute-done((f32[8,1,48,384]{3,2,1,0:T(8,128)S(1)}, f32[8,1,48,384]{3,2,1,0:T(8,128)S(1)}, u32[]{:S(2)}, u32[]{:S(2)}) %collective-permute-start.28) | collective-permute-done | bytes 589856 | tf_op jit(solution)/shard_map/ppermute | solution.py:312
  5.7 0.6 pack.3
  6.3 2.9 %collective-permute-start.29 = (f32[2,4,48,384]{3,2,1,0:T(8,128)S(1)}, f32[2,4,48,384]{3,2,1,0:T(8,128)S(1)}, u32[]{:S(2)}, u32[]{:S(2)}) collective-permute-start(f32[2,4,48,384]{3,2,1,0:T(8,128)S(1)} %pack.3), channel_id=1, source_target_pairs={{0,8},{4,20},{8,0},{12,28},{16,24},{20,4},{24,16},{28,12},{1,9},{5... | collective-permute-start | bytes 1769480 | tf_op jit(solution)/shard_map/ppermute | solution.py:321
  9.2 1.5 collective-permute-start.30
  10.8 11.8 %collective-permute-done.29.refs_12_ = f32[2,4,48,384]{3,2,1,0:T(8,128)S(1)} collective-permute-done((f32[2,4,48,384]{3,2,1,0:T(8,128)S(1)}, f32[2,4,48,384]{3,2,1,0:T(8,128)S(1)}, u32[]{:S(2)}, u32[]{:S(2)}) %collective-permute-start.29) | collective-permute-done | bytes 589856 | tf_op jit(solution)/shard_map/ppermute | solution.py:321
  22.6 2.2 collective-permute-start.31
  24.7 1.8 pack.2
  26.6 1.7 collective-permute-start.35
  29.1 1.6 collective-permute-start.45
  30.7 6.9 %collective-permute-done.31.refs_14_ = f32[2,4,48,384]{3,2,1,0:T(8,128)S(1)} collective-permute-done((f32[2,4,48,384]{3,2,1,0:T(8,128)S(1)}, f32[2,4,48,384]{3,2,1,0:T(8,128)S(1)}, u32[]{:S(2)}, u32[]{:S(2)}) %collective-permute-start.31) | collective-permute-done | bytes 589856 | tf_op jit(solution)/shard_map/ppermute | solution.py:323
  37.6 3.6 %collective-permute-start.19 = (f32[2,4,48,384]{3,2,1,0:T(8,128)S(1)}, f32[2,4,48,384]{3,2,1,0:T(8,128)S(1)}, u32[]{:S(2)}, u32[]{:S(2)}) collective-permute-start(f32[2,4,48,384]{3,2,1,0:T(8,128)S(1)} %get-tuple-element.48), channel_id=1, source_target_pairs={{0,8},{4,20},{8,0},{12,28},{16,24},{20,4},{24,16},{28,12},{1,9},{5... | collective-permute-start | bytes 1769480 | tf_op jit(solution)/shard_map/ppermute | solution.py:321
  41.2 1.6 collective-permute-done.44.rest_0_
  43.2 7.1 %collective-permute-done.45.rest_1_ = f32[2,4,48,128]{3,2,1,0:T(8,128)S(1)} collective-permute-done((f32[2,4,48,128]{3,2,1,0:T(8,128)S(1)}, f32[2,4,48,128]{3,2,1,0:T(8,128)S(1)}, u32[]{:S(2)}, u32[]{:S(2)}) %collective-permute-start.45) | collective-permute-done | bytes 196640 | tf_op jit(solution)/shard_map/ppermute | solution.py:322
  50.3 2.5 %collective-permute-start.46 = (f32[2,4,48,128]{3,2,1,0:T(8,128)S(1)}, f32[2,4,48,128]{3,2,1,0:T(8,128)S(1)}, u32[]{:S(2)}, u32[]{:S(2)}) collective-permute-start(f32[2,4,48,128]{3,2,1,0:T(8,128)S(1)} %collective-permute-done.44.rest_0_), channel_id=1, source_target_pairs={{0,16},{4,12},{8,24},{12,4},{16,0},{20,28},{24,8},{28,20},{1,17},{... | collective-permute-start | bytes 589832 | tf_op jit(solution)/shard_map/ppermute | solution.py:323
  52.8 0.5 collective-permute-start.48
  53.3 6.7 %collective-permute-done.46.rest_2_ = f32[2,4,48,128]{3,2,1,0:T(8,128)S(1)} collective-permute-done((f32[2,4,48,128]{3,2,1,0:T(8,128)S(1)}, f32[2,4,48,128]{3,2,1,0:T(8,128)S(1)}, u32[]{:S(2)}, u32[]{:S(2)}) %collective-permute-start.46) | collective-permute-done | bytes 196640 | tf_op jit(solution)/shard_map/ppermute | solution.py:323
  60.0 2.1 collective-permute-start.10
  62.0 1.1 collective-permute-start.11
  63.1 0.9 collective-permute-start.1
  64.2 1.9 collective-permute-start.2
  66.1 10.2 %collective-permute-done.10.rest_0_ = f32[2,4,48,384]{3,2,1,0:T(8,128)S(1)} collective-permute-done((f32[2,4,48,384]{3,2,1,0:T(8,128)S(1)}, f32[2,4,48,384]{3,2,1,0:T(8,128)S(1)}, u32[]{:S(2)}, u32[]{:S(2)}) %collective-permute-start.10) | collective-permute-done | bytes 589856 | tf_op jit(solution)/shard_map/ppermute | solution.py:321
  76.2 2.0 collective-permute-done.11.rest_1_
  78.2 6.0 %collective-permute-done.37.rest_2_ = f32[2,4,48,256]{3,2,1,0:T(8,128)S(1)} collective-permute-done((f32[2,4,48,256]{3,2,1,0:T(8,128)S(1)}, f32[2,4,48,256]{3,2,1,0:T(8,128)S(1)}, u32[]{:S(2)}, u32[]{:S(2)}) %collective-permute-start.37) | collective-permute-done | bytes 393248 | tf_op jit(solution)/shard_map/ppermute | solution.py:323
  84.3 4.6 %collective-permute-done.1.rest_0_ = f32[2,4,48,384]{3,2,1,0:T(8,128)S(1)} collective-permute-done((f32[2,4,48,384]{3,2,1,0:T(8,128)S(1)}, f32[2,4,48,384]{3,2,1,0:T(8,128)S(1)}, u32[]{:S(2)}, u32[]{:S(2)}) %collective-permute-start.1) | collective-permute-done | bytes 589856 | tf_op jit(solution)/shard_map/ppermute | solution.py:321
  88.9 1.7 collective-permute-done.2.rest_1_
  90.6 1.1 collective-permute-start.21
  91.6 1.0 collective-permute-start.22
  92.7 1.0 collective-permute-start.12
  93.7 6.8 %collective-permute-done.21.rest_2_ = f32[2,4,48,384]{3,2,1,0:T(8,128)S(1)} collective-permute-done((f32[2,4,48,384]{3,2,1,0:T(8,128)S(1)}, f32[2,4,48,384]{3,2,1,0:T(8,128)S(1)}, u32[]{:S(2)}, u32[]{:S(2)}) %collective-permute-start.21) | collective-permute-done | bytes 589856 | tf_op jit(solution)/shard_map/ppermute | solution.py:323
  100.5 1.1 collective-permute-start.3
  101.5 0.9 collective-permute-start.4
  102.4 4.3 %collective-permute-done.12.rest_2_ = f32[2,4,48,384]{3,2,1,0:T(8,128)S(1)} collective-permute-done((f32[2,4,48,384]{3,2,1,0:T(8,128)S(1)}, f32[2,4,48,384]{3,2,1,0:T(8,128)S(1)}, u32[]{:S(2)}, u32[]{:S(2)}) %collective-permute-start.12) | collective-permute-done | bytes 589856 | tf_op jit(solution)/shard_map/ppermute | solution.py:323
  106.8 0.5 collective-permute-start.24
  107.4 5.7 %collective-permute-done.3.rest_2_ = f32[2,4,48,384]{3,2,1,0:T(8,128)S(1)} collective-permute-done((f32[2,4,48,384]{3,2,1,0:T(8,128)S(1)}, f32[2,4,48,384]{3,2,1,0:T(8,128)S(1)}, u32[]{:S(2)}, u32[]{:S(2)}) %collective-permute-start.3) | collective-permute-done | bytes 589856 | tf_op jit(solution)/shard_map/ppermute | solution.py:323
  113.1 0.5 collective-permute-start.32
  114.1 3.7 %copy-done.1 = f32[2,8,384,384]{3,2,1,0:T(8,128)S(1)} copy-done((f32[2,8,384,384]{3,2,1,0:T(8,128)S(1)}, f32[2,8,384,384]{3,2,1,0:T(8,128)}, u32[]{:S(2)}) %copy-start.1) | copy-done | bytes 9437208
  117.8 2.8 %split_lower.1 = (bf16[4,768,768]{2,1,0:T(8,128)(2,1)S(1)}, bf16[4,768,768]{2,1,0:T(8,128)(2,1)S(1)}) custom-call(s32[2,8]{1,0:T(2,128)S(1)} %copy-done.4, s32[2,8]{1,0:T(2,128)S(1)} %copy-done.5, f32[2,8,384,384]{3,2,1,0:T(8,128)S(1)} %copy-done.1), custom_call_target="tpu_custom_call" | custom-call | tf_op jit(solution)/shard_map/split_lower/pallas_call | solution.py:73
  120.7 9.9 %shard_map.84 = (f32[2,96,384]{2,1,0:T(8,128)S(1)}, f32[2,96,384]{2,1,0:T(8,128)S(1)}, f32[2,96,384]{2,1,0:T(8,128)S(1)}, f32[2,96,384]{2,1,0:T(8,128)S(1)}) custom-call(s32[2]{0:T(128)S(1)} %pad_add_fusion.at, s32[4,8]{1,0:T(4,128)S(1)} %bitcast.5, bf16[4,768,768]{2,1,0:T(8,128)(2,1)S(1)} %get-tuple-element.36.lhs_high, ...), custom_call_target="tpu_custom_call" | custom-call | tf_op jit(solution)/shard_map/pallas_call | solution.py:174
  130.6 1.4 collective-permute-start.26
  132.0 5.8 %shard_map.86 = (f32[2,96,128]{2,1,0:T(8,128)S(1)}, f32[2,96,128]{2,1,0:T(8,128)S(1)}, f32[2,96,128]{2,1,0:T(8,128)S(1)}, f32[2,96,128]{2,1,0:T(8,128)S(1)}) custom-call(s32[2]{0:T(128)S(1)} %pad_add_fusion.at, s32[4,8]{1,0:T(4,128)S(1)} %bitcast.6, bf16[4,768,768]{2,1,0:T(8,128)(2,1)S(1)} %get-tuple-element.36.lhs_high, ...), custom_call_target="tpu_custom_call" | custom-call | tf_op jit(solution)/shard_map/pallas_call | solution.py:174
  137.8 6.3 %shard_map.85 = (f32[2,96,256]{2,1,0:T(8,128)S(1)}, f32[2,96,256]{2,1,0:T(8,128)S(1)}, f32[2,96,256]{2,1,0:T(8,128)S(1)}, f32[2,96,256]{2,1,0:T(8,128)S(1)}) custom-call(s32[2]{0:T(128)S(1)} %pad_add_fusion.at, s32[4,8]{1,0:T(4,128)S(1)} %bitcast.7, bf16[4,768,768]{2,1,0:T(8,128)(2,1)S(1)} %get-tuple-element.36.lhs_high, ...), custom_call_target="tpu_custom_call" | custom-call | tf_op jit(solution)/shard_map/pallas_call | solution.py:174
  144.1 10.1 %shard_map.83 = (f32[2,96,384]{2,1,0:T(8,128)S(1)}, f32[2,96,384]{2,1,0:T(8,128)S(1)}, f32[2,96,384]{2,1,0:T(8,128)S(1)}, f32[2,96,384]{2,1,0:T(8,128)S(1)}) custom-call(s32[2]{0:T(128)S(1)} %pad_add_fusion.at, s32[4,8]{1,0:T(4,128)S(1)} %bitcast.8, bf16[4,768,768]{2,1,0:T(8,128)(2,1)S(1)} %get-tuple-element.36.lhs_high, ...), custom_call_target="tpu_custom_call" | custom-call | tf_op jit(solution)/shard_map/pallas_call | solution.py:174
  154.3 0.8 collective-permute-start.51
  155.0 9.9 %shard_map.82 = (f32[2,96,384]{2,1,0:T(8,128)S(1)}, f32[2,96,384]{2,1,0:T(8,128)S(1)}, f32[2,96,384]{2,1,0:T(8,128)S(1)}, f32[2,96,384]{2,1,0:T(8,128)S(1)}) custom-call(s32[2]{0:T(128)S(1)} %pad_add_fusion.at, s32[4,8]{1,0:T(4,128)S(1)} %bitcast.9, bf16[4,768,768]{2,1,0:T(8,128)(2,1)S(1)} %get-tuple-element.36.lhs_high, ...), custom_call_target="tpu_custom_call" | custom-call | tf_op jit(solution)/shard_map/pallas_call | solution.py:174
  165.0 1.4 collective-permute-start.17
  166.4 0.7 collective-permute-start.42
  167.1 1.3 collective-permute-start.8
  168.4 0.7 collective-permute-start.25
  169.1 10.0 %collective-permute-done.42 = f32[2,96,256]{2,1,0:T(8,128)S(1)} collective-permute-done((f32[2,96,256]{2,1,0:T(8,128)S(1)}, f32[2,96,256]{2,1,0:T(8,128)S(1)}, u32[]{:S(2)}, u32[]{:S(2)}) %collective-permute-start.42) | collective-permute-done | bytes 196640 | tf_op jit(solution)/shard_map/ppermute | solution.py:331
  179.1 1.3 collective-permute-start.16
  180.5 0.7 collective-permute-start.7
  181.2 2.4 collective-permute-start.27
  183.6 11.3 %collective-permute-done.8 = f32[2,96,384]{2,1,0:T(8,128)S(1)} collective-permute-done((f32[2,96,384]{2,1,0:T(8,128)S(1)}, f32[2,96,384]{2,1,0:T(8,128)S(1)}, u32[]{:S(2)}, u32[]{:S(2)}) %collective-permute-start.8) | collective-permute-done | bytes 294944 | tf_op jit(solution)/shard_map/ppermute | solution.py:331
  194.9 1.4 collective-permute-start.18
  196.4 10.3 %collective-permute-done.25.refs_8_ = f32[2,96,384]{2,1,0:T(8,128)S(1)} collective-permute-done((f32[2,96,384]{2,1,0:T(8,128)S(1)}, f32[2,96,384]{2,1,0:T(8,128)S(1)}, u32[]{:S(2)}, u32[]{:S(2)}) %collective-permute-start.25) | collective-permute-done | bytes 294944 | tf_op jit(solution)/shard_map/ppermute | solution.py:332
  206.7 6.3 %collective-permute-done.16.refs_5_ = f32[2,96,384]{2,1,0:T(8,128)S(1)} collective-permute-done((f32[2,96,384]{2,1,0:T(8,128)S(1)}, f32[2,96,384]{2,1,0:T(8,128)S(1)}, u32[]{:S(2)}, u32[]{:S(2)}) %collective-permute-start.16) | collective-permute-done | bytes 294944 | tf_op jit(solution)/shard_map/ppermute | solution.py:332
  213.0 6.3 %collective-permute-done.7.refs_2_ = f32[2,96,384]{2,1,0:T(8,128)S(1)} collective-permute-done((f32[2,96,384]{2,1,0:T(8,128)S(1)}, f32[2,96,384]{2,1,0:T(8,128)S(1)}, u32[]{:S(2)}, u32[]{:S(2)}) %collective-permute-start.7) | collective-permute-done | bytes 294944 | tf_op jit(solution)/shard_map/ppermute | solution.py:332
  219.3 2.0 collective-permute-start.50
  221.3 1.1 collective-permute-start.52
  222.4 14.1 %collective-permute-done.9.refs_3_ = f32[2,96,384]{2,1,0:T(8,128)S(1)} collective-permute-done((f32[2,96,384]{2,1,0:T(8,128)S(1)}, f32[2,96,384]{2,1,0:T(8,128)S(1)}, u32[]{:S(2)}, u32[]{:S(2)}) %collective-permute-start.9) | collective-permute-done | bytes 294944 | tf_op jit(solution)/shard_map/ppermute | solution.py:331
  236.5 4.2 %finish_early.1 = (f32[2,3,96,384]{3,2,1,0:T(8,128)S(1)}, f32[2,96,384]{2,1,0:T(8,128)S(1)}, bf16[384,384]{1,0:T(8,128)(2,1)S(1)}, bf16[384,384]{1,0:T(8,128)(2,1)S(1)}) custom-call(s32[2]{0:T(128)S(1)} %pad_add_fusion.at, f32[2,4,96,384]{3,2,1,0:T(8,128)S(1)} %copy-done.2, f32[2,96,384]{2,1,0:T(8,128)S(1)} %get-tuple-element.39.refs_1_, ...), custom_call_target="tpu_custom_call" | custom-call | tf_op jit(solution)/shard_map/finish_early/pallas_call | solution.py:251
  240.8 1.5 finish_last.1
  (72 shorter events, 2.8 us)
Async XLA Ops:
  0.0 24.7 %copy-start = (f32[8,4,48,384]{3,2,1,0:T(8,128)S(1)}, f32[8,4,48,384]{3,2,1,0:T(8,128)}, u32[]{:S(2)}) copy-start(f32[8,4,48,384]{3,2,1,0:T(8,128)} %own_ref.9) | copy-start | bytes 7077892
  0.0 24.7 %collective-permute-start = (f32[8,4,48,384]{3,2,1,0:T(8,128)}, f32[8,4,48,384]{3,2,1,0:T(8,128)}, u32[]{:S(2)}, u32[]{:S(2)}) collective-permute-start(f32[8,4,48,384]{3,2,1,0:T(8,128)} %own_ref.9), channel_id=1, source_target_pairs={{0,4},{4,0},{8,12},{12,8},{16,20},{20,16},{24,28},{28,24},{1,5},{5... | collective-permute-start | bytes 7077896 | tf_op jit(solution)/shard_map/ppermute | solution.py:310
  2.7 3.0 %collective-permute-start.28 = (f32[8,1,48,384]{3,2,1,0:T(8,128)S(1)}, f32[8,1,48,384]{3,2,1,0:T(8,128)S(1)}, u32[]{:S(2)}, u32[]{:S(2)}) collective-permute-start(f32[8,1,48,384]{3,2,1,0:T(8,128)S(1)} %maximum_bitcast_fusion.mine.refs_10_), channel_id=1, source_target_pairs={{0,4},{4,0},{8,12},{12,8},{16,20},{20,16},{24,28},{28,24},{1,5},{5... | collective-permute-start | bytes 1769480 | tf_op jit(solution)/shard_map/ppermute | solution.py:312
  6.3 107.8 %copy-start.4 = (s32[2,8]{1,0:T(2,128)S(1)}, s32[2,8]{1,0:T(2,128)}, u32[]{:S(2)}) copy-start(s32[2,8]{1,0:T(2,128)} %bucket.1) | copy-start | bytes 196
  6.3 107.8 %copy-start.5 = (s32[2,8]{1,0:T(2,128)S(1)}, s32[2,8]{1,0:T(2,128)}, u32[]{:S(2)}) copy-start(s32[2,8]{1,0:T(2,128)} %flags.1) | copy-start | bytes 196
  6.3 16.2 %collective-permute-start.29 = (f32[2,4,48,384]{3,2,1,0:T(8,128)S(1)}, f32[2,4,48,384]{3,2,1,0:T(8,128)S(1)}, u32[]{:S(2)}, u32[]{:S(2)}) collective-permute-start(f32[2,4,48,384]{3,2,1,0:T(8,128)S(1)} %pack.3), channel_id=1, source_target_pairs={{0,8},{4,20},{8,0},{12,28},{16,24},{20,4},{24,16},{28,12},{1,9},{5... | collective-permute-start | bytes 1769480 | tf_op jit(solution)/shard_map/ppermute | solution.py:321
  9.2 19.8 %collective-permute-start.30 = (f32[2,4,48,384]{3,2,1,0:T(8,128)S(1)}, f32[2,4,48,384]{3,2,1,0:T(8,128)S(1)}, u32[]{:S(2)}, u32[]{:S(2)}) collective-permute-start(f32[2,4,48,384]{3,2,1,0:T(8,128)S(1)} %pack.3), channel_id=1, source_target_pairs={{0,16},{4,12},{8,24},{12,4},{16,0},{20,28},{24,8},{28,20},{1,17},{... | collective-permute-start | bytes 1769480 | tf_op jit(solution)/shard_map/ppermute | solution.py:322
  22.6 15.1 %collective-permute-start.31 = (f32[2,4,48,384]{3,2,1,0:T(8,128)S(1)}, f32[2,4,48,384]{3,2,1,0:T(8,128)S(1)}, u32[]{:S(2)}, u32[]{:S(2)}) collective-permute-start(f32[2,4,48,384]{3,2,1,0:T(8,128)S(1)} %collective-permute-done.29.refs_12_), channel_id=1, source_target_pairs={{0,16},{4,12},{8,24},{12,4},{16,0},{20,28},{24,8},{28,20},{1,17},{... | collective-permute-start | bytes 1769480 | tf_op jit(solution)/shard_map/ppermute | solution.py:323
  26.6 26.2 %collective-permute-start.35 = (f32[2,4,48,256]{3,2,1,0:T(8,128)S(1)}, f32[2,4,48,256]{3,2,1,0:T(8,128)S(1)}, u32[]{:S(2)}, u32[]{:S(2)}) collective-permute-start(f32[2,4,48,256]{3,2,1,0:T(8,128)S(1)} %get-tuple-element.57), channel_id=1, source_target_pairs={{0,8},{4,20},{8,0},{12,28},{16,24},{20,4},{24,16},{28,12},{1,9},{5... | collective-permute-start | bytes 1179656 | tf_op jit(solution)/shard_map/ppermute | solution.py:321
  28.3 14.6 %collective-permute-start.44 = (f32[2,4,48,128]{3,2,1,0:T(8,128)S(1)}, f32[2,4,48,128]{3,2,1,0:T(8,128)S(1)}, u32[]{:S(2)}, u32[]{:S(2)}) collective-permute-start(f32[2,4,48,128]{3,2,1,0:T(8,128)S(1)} %get-tuple-element.62), channel_id=1, source_target_pairs={{0,8},{4,20},{8,0},{12,28},{16,24},{20,4},{24,16},{28,12},{1,9},{5... | collective-permute-start | bytes 589832 | tf_op jit(solution)/shard_map/ppermute | solution.py:321
  28.7 24.1 %collective-permute-start.36 = (f32[2,4,48,256]{3,2,1,0:T(8,128)S(1)}, f32[2,4,48,256]{3,2,1,0:T(8,128)S(1)}, u32[]{:S(2)}, u32[]{:S(2)}) collective-permute-start(f32[2,4,48,256]{3,2,1,0:T(8,128)S(1)} %get-tuple-element.57), channel_id=1, source_target_pairs={{0,16},{4,12},{8,24},{12,4},{16,0},{20,28},{24,8},{28,20},{1,17},{... | collective-permute-start | bytes 1179656 | tf_op jit(solution)/shard_map/ppermute | solution.py:322
  29.1 21.2 %collective-permute-start.45 = (f32[2,4,48,128]{3,2,1,0:T(8,128)S(1)}, f32[2,4,48,128]{3,2,1,0:T(8,128)S(1)}, u32[]{:S(2)}, u32[]{:S(2)}) collective-permute-start(f32[2,4,48,128]{3,2,1,0:T(8,128)S(1)} %get-tuple-element.62), channel_id=1, source_target_pairs={{0,16},{4,12},{8,24},{12,4},{16,0},{20,28},{24,8},{28,20},{1,17},{... | collective-permute-start | bytes 589832 | tf_op jit(solution)/shard_map/ppermute | solution.py:322
  37.6 26.4 %collective-permute-start.19 = (f32[2,4,48,384]{3,2,1,0:T(8,128)S(1)}, f32[2,4,48,384]{3,2,1,0:T(8,128)S(1)}, u32[]{:S(2)}, u32[]{:S(2)}) collective-permute-start(f32[2,4,48,384]{3,2,1,0:T(8,128)S(1)} %get-tuple-element.48), channel_id=1, source_target_pairs={{0,8},{4,20},{8,0},{12,28},{16,24},{20,4},{24,16},{28,12},{1,9},{5... | collective-permute-start | bytes 1769480 | tf_op jit(solution)/shard_map/ppermute | solution.py:321
  42.8 21.3 %collective-permute-start.20 = (f32[2,4,48,384]{3,2,1,0:T(8,128)S(1)}, f32[2,4,48,384]{3,2,1,0:T(8,128)S(1)}, u32[]{:S(2)}, u32[]{:S(2)}) collective-permute-start(f32[2,4,48,384]{3,2,1,0:T(8,128)S(1)} %get-tuple-element.48), channel_id=1, source_target_pairs={{0,16},{4,12},{8,24},{12,4},{16,0},{20,28},{24,8},{28,20},{1,17},{... | collective-permute-start | bytes 1769480 | tf_op jit(solution)/shard_map/ppermute | solution.py:322
  50.3 9.7 %collective-permute-start.46 = (f32[2,4,48,128]{3,2,1,0:T(8,128)S(1)}, f32[2,4,48,128]{3,2,1,0:T(8,128)S(1)}, u32[]{:S(2)}, u32[]{:S(2)}) collective-permute-start(f32[2,4,48,128]{3,2,1,0:T(8,128)S(1)} %collective-permute-done.44.rest_0_), channel_id=1, source_target_pairs={{0,16},{4,12},{8,24},{12,4},{16,0},{20,28},{24,8},{28,20},{1,17},{... | collective-permute-start | bytes 589832 | tf_op jit(solution)/shard_map/ppermute | solution.py:323
  52.7 9.3 %collective-permute-start.47 = (f32[2,4,48,128]{3,2,1,0:T(8,128)S(1)}, f32[2,4,48,128]{3,2,1,0:T(8,128)S(1)}, u32[]{:S(2)}, u32[]{:S(2)}) collective-permute-start(f32[2,4,48,128]{3,2,1,0:T(8,128)S(1)} %collective-permute-done.44.rest_0_), channel_id=1, source_target_pairs={{0,4},{4,0},{8,12},{12,8},{16,20},{20,16},{24,28},{28,24},{1,5},{5... | collective-permute-start | bytes 589832 | tf_op jit(solution)/shard_map/ppermute | solution.py:324
  52.8 10.4 %collective-permute-start.48 = (f32[2,4,48,128]{3,2,1,0:T(8,128)S(1)}, f32[2,4,48,128]{3,2,1,0:T(8,128)S(1)}, u32[]{:S(2)}, u32[]{:S(2)}) collective-permute-start(f32[2,4,48,128]{3,2,1,0:T(8,128)S(1)} %collective-permute-done.45.rest_1_), channel_id=1, source_target_pairs={{0,4},{4,0},{8,12},{12,8},{16,20},{20,16},{24,28},{28,24},{1,5},{5... | collective-permute-start | bytes 589832 | tf_op jit(solution)/shard_map/ppermute | solution.py:324
  60.0 60.7 %copy-start.3 = (s32[8,4]{0,1:T(4,128)S(1)}, s32[8,4]{0,1:T(4,128)}, u32[]{:S(2)}) copy-start(s32[8,4]{0,1:T(4,128)} %param.12) | copy-start | bytes 388
  60.0 16.2 %collective-permute-start.10 = (f32[2,4,48,384]{3,2,1,0:T(8,128)S(1)}, f32[2,4,48,384]{3,2,1,0:T(8,128)S(1)}, u32[]{:S(2)}, u32[]{:S(2)}) collective-permute-start(f32[2,4,48,384]{3,2,1,0:T(8,128)S(1)} %get-tuple-element.43), channel_id=1, source_target_pairs={{0,8},{4,20},{8,0},{12,28},{16,24},{20,4},{24,16},{28,12},{1,9},{5... | collective-permute-start | bytes 1769480 | tf_op jit(solution)/shard_map/ppermute | solution.py:321
  62.0 16.2 %collective-permute-start.11 = (f32[2,4,48,384]{3,2,1,0:T(8,128)S(1)}, f32[2,4,48,384]{3,2,1,0:T(8,128)S(1)}, u32[]{:S(2)}, u32[]{:S(2)}) collective-permute-start(f32[2,4,48,384]{3,2,1,0:T(8,128)S(1)} %get-tuple-element.43), channel_id=1, source_target_pairs={{0,16},{4,12},{8,24},{12,4},{16,0},{20,28},{24,8},{28,20},{1,17},{... | collective-permute-start | bytes 1769480 | tf_op jit(solution)/shard_map/ppermute | solution.py:322
  63.1 25.7 %collective-permute-start.1 = (f32[2,4,48,384]{3,2,1,0:T(8,128)S(1)}, f32[2,4,48,384]{3,2,1,0:T(8,128)S(1)}, u32[]{:S(2)}, u32[]{:S(2)}) collective-permute-start(f32[2,4,48,384]{3,2,1,0:T(8,128)S(1)} %get-tuple-element.38), channel_id=1, source_target_pairs={{0,8},{4,20},{8,0},{12,28},{16,24},{20,4},{24,16},{28,12},{1,9},{5... | collective-permute-start | bytes 1769480 | tf_op jit(solution)/shard_map/ppermute | solution.py:321
  64.0 20.2 %collective-permute-start.37 = (f32[2,4,48,256]{3,2,1,0:T(8,128)S(1)}, f32[2,4,48,256]{3,2,1,0:T(8,128)S(1)}, u32[]{:S(2)}, u32[]{:S(2)}) collective-permute-start(f32[2,4,48,256]{3,2,1,0:T(8,128)S(1)} %collective-permute-done.35.rest_0_), channel_id=1, source_target_pairs={{0,16},{4,12},{8,24},{12,4},{16,0},{20,28},{24,8},{28,20},{1,17},{... | collective-permute-start | bytes 1179656 | tf_op jit(solution)/shard_map/ppermute | solution.py:323
  64.2 26.4 %collective-permute-start.2 = (f32[2,4,48,384]{3,2,1,0:T(8,128)S(1)}, f32[2,4,48,384]{3,2,1,0:T(8,128)S(1)}, u32[]{:S(2)}, u32[]{:S(2)}) collective-permute-start(f32[2,4,48,384]{3,2,1,0:T(8,128)S(1)} %get-tuple-element.38), channel_id=1, source_target_pairs={{0,16},{4,12},{8,24},{12,4},{16,0},{20,28},{24,8},{28,20},{1,17},{... | collective-permute-start | bytes 1769480 | tf_op jit(solution)/shard_map/ppermute | solution.py:322
  76.2 16.4 %collective-permute-start.38 = (f32[2,4,48,256]{3,2,1,0:T(8,128)S(1)}, f32[2,4,48,256]{3,2,1,0:T(8,128)S(1)}, u32[]{:S(2)}, u32[]{:S(2)}) collective-permute-start(f32[2,4,48,256]{3,2,1,0:T(8,128)S(1)} %collective-permute-done.35.rest_0_), channel_id=1, source_target_pairs={{0,4},{4,0},{8,12},{12,8},{16,20},{20,16},{24,28},{28,24},{1,5},{5... | collective-permute-start | bytes 1179656 | tf_op jit(solution)/shard_map/ppermute | solution.py:324
  78.2 14.5 %collective-permute-start.39 = (f32[2,4,48,256]{3,2,1,0:T(8,128)S(1)}, f32[2,4,48,256]{3,2,1,0:T(8,128)S(1)}, u32[]{:S(2)}, u32[]{:S(2)}) collective-permute-start(f32[2,4,48,256]{3,2,1,0:T(8,128)S(1)} %collective-permute-done.36.rest_1_), channel_id=1, source_target_pairs={{0,4},{4,0},{8,12},{12,8},{16,20},{20,16},{24,28},{28,24},{1,5},{5... | collective-permute-start | bytes 1179656 | tf_op jit(solution)/shard_map/ppermute | solution.py:324
  84.3 9.4 %collective-permute-start.40 = (f32[2,4,48,256]{3,2,1,0:T(8,128)S(1)}, f32[2,4,48,256]{3,2,1,0:T(8,128)S(1)}, u32[]{:S(2)}, u32[]{:S(2)}) collective-permute-start(f32[2,4,48,256]{3,2,1,0:T(8,128)S(1)} %collective-permute-done.37.rest_2_), channel_id=1, source_target_pairs={{0,4},{4,0},{8,12},{12,8},{16,20},{20,16},{24,28},{28,24},{1,5},{5... | collective-permute-start | bytes 1179656 | tf_op jit(solution)/shard_map/ppermute | solution.py:324
  88.9 2.8 %collective-permute-start.49 = (f32[2,4,48,128]{3,2,1,0:T(8,128)S(1)}, f32[2,4,48,128]{3,2,1,0:T(8,128)S(1)}, u32[]{:S(2)}, u32[]{:S(2)}) collective-permute-start(f32[2,4,48,128]{3,2,1,0:T(8,128)S(1)} %collective-permute-done.46.rest_2_), channel_id=1, source_target_pairs={{0,4},{4,0},{8,12},{12,8},{16,20},{20,16},{24,28},{28,24},{1,5},{5... | collective-permute-start | bytes 589832 | tf_op jit(solution)/shard_map/ppermute | solution.py:324
  90.6 9.9 %collective-permute-start.21 = (f32[2,4,48,384]{3,2,1,0:T(8,128)S(1)}, f32[2,4,48,384]{3,2,1,0:T(8,128)S(1)}, u32[]{:S(2)}, u32[]{:S(2)}) collective-permute-start(f32[2,4,48,384]{3,2,1,0:T(8,128)S(1)} %collective-permute-done.19.rest_0_), channel_id=1, source_target_pairs={{0,16},{4,12},{8,24},{12,4},{16,0},{20,28},{24,8},{28,20},{1,17},{... | collective-permute-start | bytes 1769480 | tf_op jit(solution)/shard_map/ppermute | solution.py:323
  91.6 8.8 %collective-permute-start.22 = (f32[2,4,48,384]{3,2,1,0:T(8,128)S(1)}, f32[2,4,48,384]{3,2,1,0:T(8,128)S(1)}, u32[]{:S(2)}, u32[]{:S(2)}) collective-permute-start(f32[2,4,48,384]{3,2,1,0:T(8,128)S(1)} %collective-permute-done.19.rest_0_), channel_id=1, source_target_pairs={{0,4},{4,0},{8,12},{12,8},{16,20},{20,16},{24,28},{28,24},{1,5},{5... | collective-permute-start | bytes 1769480 | tf_op jit(solution)/shard_map/ppermute | solution.py:324
  92.7 8.9 %collective-permute-start.23 = (f32[2,4,48,384]{3,2,1,0:T(8,128)S(1)}, f32[2,4,48,384]{3,2,1,0:T(8,128)S(1)}, u32[]{:S(2)}, u32[]{:S(2)}) collective-permute-start(f32[2,4,48,384]{3,2,1,0:T(8,128)S(1)} %collective-permute-done.20.rest_1_), channel_id=1, source_target_pairs={{0,4},{4,0},{8,12},{12,8},{16,20},{20,16},{24,28},{28,24},{1,5},{5... | collective-permute-start | bytes 1769480 | tf_op jit(solution)/shard_map/ppermute | solution.py:324
  92.7 14.1 %collective-permute-start.12 = (f32[2,4,48,384]{3,2,1,0:T(8,128)S(1)}, f32[2,4,48,384]{3,2,1,0:T(8,128)S(1)}, u32[]{:S(2)}, u32[]{:S(2)}) collective-permute-start(f32[2,4,48,384]{3,2,1,0:T(8,128)S(1)} %collective-permute-done.10.rest_0_), channel_id=1, source_target_pairs={{0,16},{4,12},{8,24},{12,4},{16,0},{20,28},{24,8},{28,20},{1,17},{... | collective-permute-start | bytes 1769480 | tf_op jit(solution)/shard_map/ppermute | solution.py:323
  93.7 13.1 %collective-permute-start.13 = (f32[2,4,48,384]{3,2,1,0:T(8,128)S(1)}, f32[2,4,48,384]{3,2,1,0:T(8,128)S(1)}, u32[]{:S(2)}, u32[]{:S(2)}) collective-permute-start(f32[2,4,48,384]{3,2,1,0:T(8,128)S(1)} %collective-permute-done.10.rest_0_), channel_id=1, source_target_pairs={{0,4},{4,0},{8,12},{12,8},{16,20},{20,16},{24,28},{28,24},{1,5},{5... | collective-permute-start | bytes 1769480 | tf_op jit(solution)/shard_map/ppermute | solution.py:324
  100.5 6.8 %collective-permute-start.14 = (f32[2,4,48,384]{3,2,1,0:T(8,128)S(1)}, f32[2,4,48,384]{3,2,1,0:T(8,128)S(1)}, u32[]{:S(2)}, u32[]{:S(2)}) collective-permute-start(f32[2,4,48,384]{3,2,1,0:T(8,128)S(1)} %collective-permute-done.11.rest_1_), channel_id=1, source_target_pairs={{0,4},{4,0},{8,12},{12,8},{16,20},{20,16},{24,28},{28,24},{1,5},{5... | collective-permute-start | bytes 1769480 | tf_op jit(solution)/shard_map/ppermute | solution.py:324
  100.5 12.6 %collective-permute-start.3 = (f32[2,4,48,384]{3,2,1,0:T(8,128)S(1)}, f32[2,4,48,384]{3,2,1,0:T(8,128)S(1)}, u32[]{:S(2)}, u32[]{:S(2)}) collective-permute-start(f32[2,4,48,384]{3,2,1,0:T(8,128)S(1)} %collective-permute-done.1.rest_0_), channel_id=1, source_target_pairs={{0,16},{4,12},{8,24},{12,4},{16,0},{20,28},{24,8},{28,20},{1,17},{... | collective-permute-start | bytes 1769480 | tf_op jit(solution)/shard_map/ppermute | solution.py:323
  101.5 11.6 %collective-permute-start.4 = (f32[2,4,48,384]{3,2,1,0:T(8,128)S(1)}, f32[2,4,48,384]{3,2,1,0:T(8,128)S(1)}, u32[]{:S(2)}, u32[]{:S(2)}) collective-permute-start(f32[2,4,48,384]{3,2,1,0:T(8,128)S(1)} %collective-permute-done.1.rest_0_), channel_id=1, source_target_pairs={{0,4},{4,0},{8,12},{12,8},{16,20},{20,16},{24,28},{28,24},{1,5},{5... | collective-permute-start | bytes 1769480 | tf_op jit(solution)/shard_map/ppermute | solution.py:324
  106.8 6.8 %collective-permute-start.5 = (f32[2,4,48,384]{3,2,1,0:T(8,128)S(1)}, f32[2,4,48,384]{3,2,1,0:T(8,128)S(1)}, u32[]{:S(2)}, u32[]{:S(2)}) collective-permute-start(f32[2,4,48,384]{3,2,1,0:T(8,128)S(1)} %collective-permute-done.2.rest_1_), channel_id=1, source_target_pairs={{0,4},{4,0},{8,12},{12,8},{16,20},{20,16},{24,28},{28,24},{1,5},{5... | collective-permute-start | bytes 1769480 | tf_op jit(solution)/shard_map/ppermute | solution.py:324
  106.8 6.9 %collective-permute-start.24 = (f32[2,4,48,384]{3,2,1,0:T(8,128)S(1)}, f32[2,4,48,384]{3,2,1,0:T(8,128)S(1)}, u32[]{:S(2)}, u32[]{:S(2)}) collective-permute-start(f32[2,4,48,384]{3,2,1,0:T(8,128)S(1)} %collective-permute-done.21.rest_2_), channel_id=1, source_target_pairs={{0,4},{4,0},{8,12},{12,8},{16,20},{20,16},{24,28},{28,24},{1,5},{5... | collective-permute-start | bytes 1769480 | tf_op jit(solution)/shard_map/ppermute | solution.py:324
  107.3 23.3 %collective-permute-start.15 = (f32[2,4,48,384]{3,2,1,0:T(8,128)S(1)}, f32[2,4,48,384]{3,2,1,0:T(8,128)S(1)}, u32[]{:S(2)}, u32[]{:S(2)}) collective-permute-start(f32[2,4,48,384]{3,2,1,0:T(8,128)S(1)} %collective-permute-done.12.rest_2_), channel_id=1, source_target_pairs={{0,4},{4,0},{8,12},{12,8},{16,20},{20,16},{24,28},{28,24},{1,5},{5... | collective-permute-start | bytes 1769480 | tf_op jit(solution)/shard_map/ppermute | solution.py:324
  113.1 41.1 %collective-permute-start.6 = (f32[2,4,48,384]{3,2,1,0:T(8,128)S(1)}, f32[2,4,48,384]{3,2,1,0:T(8,128)S(1)}, u32[]{:S(2)}, u32[]{:S(2)}) collective-permute-start(f32[2,4,48,384]{3,2,1,0:T(8,128)S(1)} %collective-permute-done.3.rest_2_), channel_id=1, source_target_pairs={{0,4},{4,0},{8,12},{12,8},{16,20},{20,16},{24,28},{28,24},{1,5},{5... | collective-permute-start | bytes 1769480 | tf_op jit(solution)/shard_map/ppermute | solution.py:324
  113.1 51.9 %collective-permute-start.32 = (f32[2,4,48,384]{3,2,1,0:T(8,128)S(1)}, f32[2,4,48,384]{3,2,1,0:T(8,128)S(1)}, u32[]{:S(2)}, u32[]{:S(2)}) collective-permute-start(f32[2,4,48,384]{3,2,1,0:T(8,128)S(1)} %collective-permute-done.29.refs_12_), channel_id=1, source_target_pairs={{0,4},{4,0},{8,12},{12,8},{16,20},{20,16},{24,28},{28,24},{1,5},{5... | collective-permute-start | bytes 1769480 | tf_op jit(solution)/shard_map/ppermute | solution.py:324
  113.6 52.7 %collective-permute-start.33 = (f32[2,4,48,384]{3,2,1,0:T(8,128)S(1)}, f32[2,4,48,384]{3,2,1,0:T(8,128)S(1)}, u32[]{:S(2)}, u32[]{:S(2)}) collective-permute-start(f32[2,4,48,384]{3,2,1,0:T(8,128)S(1)} %collective-permute-done.30.refs_13_), channel_id=1, source_target_pairs={{0,4},{4,0},{8,12},{12,8},{16,20},{20,16},{24,28},{28,24},{1,5},{5... | collective-permute-start | bytes 1769480 | tf_op jit(solution)/shard_map/ppermute | solution.py:324
  113.7 53.4 %collective-permute-start.34 = (f32[2,4,48,384]{3,2,1,0:T(8,128)S(1)}, f32[2,4,48,384]{3,2,1,0:T(8,128)S(1)}, u32[]{:S(2)}, u32[]{:S(2)}) collective-permute-start(f32[2,4,48,384]{3,2,1,0:T(8,128)S(1)} %collective-permute-done.31.refs_14_), channel_id=1, source_target_pairs={{0,4},{4,0},{8,12},{12,8},{16,20},{20,16},{24,28},{28,24},{1,5},{5... | collective-permute-start | bytes 1769480 | tf_op jit(solution)/shard_map/ppermute | solution.py:324
  114.1 3.7 %copy-start.1 = (f32[2,8,384,384]{3,2,1,0:T(8,128)S(1)}, f32[2,8,384,384]{3,2,1,0:T(8,128)}, u32[]{:S(2)}) copy-start(f32[2,8,384,384]{3,2,1,0:T(8,128)} %source.1) | copy-start | bytes 28311556
  130.6 49.8 %collective-permute-start.26 = (f32[2,96,384]{2,1,0:T(8,128)S(1)}, f32[2,96,384]{2,1,0:T(8,128)S(1)}, u32[]{:S(2)}, u32[]{:S(2)}) collective-permute-start(f32[2,96,384]{2,1,0:T(8,128)S(1)} %get-tuple-element.52), channel_id=1, source_target_pairs={{0,1},{1,0},{2,3},{3,2},{4,5},{5,4},{6,7},{7,6},{8,9},{9,8},{10,11... | collective-permute-start | bytes 884744 | tf_op jit(solution)/shard_map/ppermute | solution.py:331
  154.3 14.1 %collective-permute-start.51 = (f32[2,96,128]{2,1,0:T(8,128)S(1)}, f32[2,96,128]{2,1,0:T(8,128)S(1)}, u32[]{:S(2)}, u32[]{:S(2)}) collective-permute-start(f32[2,96,128]{2,1,0:T(8,128)S(1)} %get-tuple-element.66), channel_id=1, source_target_pairs={{0,1},{1,0},{2,3},{3,2},{4,5},{5,4},{6,7},{7,6},{8,9},{9,8},{10,11... | collective-permute-start | bytes 294920 | tf_op jit(solution)/shard_map/ppermute | solution.py:331
  165.0 71.5 %copy-start.2 = (f32[2,4,96,384]{3,2,1,0:T(8,128)S(1)}, f32[2,4,96,384]{3,2,1,0:T(8,128)}, u32[]{:S(2)}) copy-start(f32[2,4,96,384]{3,2,1,0:T(8,128)} %diag_ref.1) | copy-start | bytes 3538948
  165.0 16.2 %collective-permute-start.17 = (f32[2,96,384]{2,1,0:T(8,128)S(1)}, f32[2,96,384]{2,1,0:T(8,128)S(1)}, u32[]{:S(2)}, u32[]{:S(2)}) collective-permute-start(f32[2,96,384]{2,1,0:T(8,128)S(1)} %get-tuple-element.47), channel_id=1, source_target_pairs={{0,1},{1,0},{2,3},{3,2},{4,5},{5,4},{6,7},{7,6},{8,9},{9,8},{10,11... | collective-permute-start | bytes 884744 | tf_op jit(solution)/shard_map/ppermute | solution.py:331
  166.4 12.8 %collective-permute-start.42 = (f32[2,96,256]{2,1,0:T(8,128)S(1)}, f32[2,96,256]{2,1,0:T(8,128)S(1)}, u32[]{:S(2)}, u32[]{:S(2)}) collective-permute-start(f32[2,96,256]{2,1,0:T(8,128)S(1)} %get-tuple-element.61), channel_id=1, source_target_pairs={{0,1},{1,0},{2,3},{3,2},{4,5},{5,4},{6,7},{7,6},{8,9},{9,8},{10,11... | collective-permute-start | bytes 589832 | tf_op jit(solution)/shard_map/ppermute | solution.py:331
  167.1 27.9 %collective-permute-start.8 = (f32[2,96,384]{2,1,0:T(8,128)S(1)}, f32[2,96,384]{2,1,0:T(8,128)S(1)}, u32[]{:S(2)}, u32[]{:S(2)}) collective-permute-start(f32[2,96,384]{2,1,0:T(8,128)S(1)} %get-tuple-element.42), channel_id=1, source_target_pairs={{0,1},{1,0},{2,3},{3,2},{4,5},{5,4},{6,7},{7,6},{8,9},{9,8},{10,11... | collective-permute-start | bytes 884744 | tf_op jit(solution)/shard_map/ppermute | solution.py:331
  168.4 38.2 %collective-permute-start.25 = (f32[2,96,384]{2,1,0:T(8,128)S(1)}, f32[2,96,384]{2,1,0:T(8,128)S(1)}, u32[]{:S(2)}, u32[]{:S(2)}) collective-permute-start(f32[2,96,384]{2,1,0:T(8,128)S(1)} %get-tuple-element.50), channel_id=1, source_target_pairs={{0,1},{1,0},{2,3},{3,2},{4,5},{5,4},{6,7},{7,6},{8,9},{9,8},{10,11... | collective-permute-start | bytes 884744 | tf_op jit(solution)/shard_map/ppermute | solution.py:332
  179.1 33.8 %collective-permute-start.16 = (f32[2,96,384]{2,1,0:T(8,128)S(1)}, f32[2,96,384]{2,1,0:T(8,128)S(1)}, u32[]{:S(2)}, u32[]{:S(2)}) collective-permute-start(f32[2,96,384]{2,1,0:T(8,128)S(1)} %get-tuple-element.45), channel_id=1, source_target_pairs={{0,1},{1,0},{2,3},{3,2},{4,5},{5,4},{6,7},{7,6},{8,9},{9,8},{10,11... | collective-permute-start | bytes 884744 | tf_op jit(solution)/shard_map/ppermute | solution.py:332
  180.5 38.8 %collective-permute-start.7 = (f32[2,96,384]{2,1,0:T(8,128)S(1)}, f32[2,96,384]{2,1,0:T(8,128)S(1)}, u32[]{:S(2)}, u32[]{:S(2)}) collective-permute-start(f32[2,96,384]{2,1,0:T(8,128)S(1)} %get-tuple-element.40), channel_id=1, source_target_pairs={{0,1},{1,0},{2,3},{3,2},{4,5},{5,4},{6,7},{7,6},{8,9},{9,8},{10,11... | collective-permute-start | bytes 884744 | tf_op jit(solution)/shard_map/ppermute | solution.py:332
  181.2 38.1 %collective-permute-start.27 = (f32[2,96,384]{2,1,0:T(8,128)S(1)}, f32[2,96,384]{2,1,0:T(8,128)S(1)}, u32[]{:S(2)}, u32[]{:S(2)}) collective-permute-start(f32[2,96,384]{2,1,0:T(8,128)S(1)} %add.17), channel_id=1, source_target_pairs={{0,2},{1,3},{2,0},{3,1},{4,6},{5,7},{6,4},{7,5},{8,10},{9,11},{10,... | collective-permute-start | bytes 884744 | tf_op jit(solution)/shard_map/ppermute | solution.py:331
  194.9 26.4 %collective-permute-start.18 = (f32[2,96,384]{2,1,0:T(8,128)S(1)}, f32[2,96,384]{2,1,0:T(8,128)S(1)}, u32[]{:S(2)}, u32[]{:S(2)}) collective-permute-start(f32[2,96,384]{2,1,0:T(8,128)S(1)} %add.16), channel_id=1, source_target_pairs={{0,2},{1,3},{2,0},{3,1},{4,6},{5,7},{6,4},{7,5},{8,10},{9,11},{10,... | collective-permute-start | bytes 884744 | tf_op jit(solution)/shard_map/ppermute | solution.py:331
  206.6 29.8 %collective-permute-start.9 = (f32[2,96,384]{2,1,0:T(8,128)S(1)}, f32[2,96,384]{2,1,0:T(8,128)S(1)}, u32[]{:S(2)}, u32[]{:S(2)}) collective-permute-start(f32[2,96,384]{2,1,0:T(8,128)S(1)} %add.15), channel_id=1, source_target_pairs={{0,2},{1,3},{2,0},{3,1},{4,6},{5,7},{6,4},{7,5},{8,10},{9,11},{10,... | collective-permute-start | bytes 884744 | tf_op jit(solution)/shard_map/ppermute | solution.py:331
  213.0 27.8 %collective-permute-start.41 = (f32[2,96,256]{2,1,0:T(8,128)S(1)}, f32[2,96,256]{2,1,0:T(8,128)S(1)}, u32[]{:S(2)}, u32[]{:S(2)}) collective-permute-start(f32[2,96,256]{2,1,0:T(8,128)S(1)} %get-tuple-element.59), channel_id=1, source_target_pairs={{0,1},{1,0},{2,3},{3,2},{4,5},{5,4},{6,7},{7,6},{8,9},{9,8},{10,11... | collective-permute-start | bytes 589832 | tf_op jit(solution)/shard_map/ppermute | solution.py:332
  219.3 21.5 %collective-permute-start.43 = (f32[2,96,256]{2,1,0:T(8,128)S(1)}, f32[2,96,256]{2,1,0:T(8,128)S(1)}, u32[]{:S(2)}, u32[]{:S(2)}) collective-permute-start(f32[2,96,256]{2,1,0:T(8,128)S(1)} %add.18), channel_id=1, source_target_pairs={{0,2},{1,3},{2,0},{3,1},{4,6},{5,7},{6,4},{7,5},{8,10},{9,11},{10,... | collective-permute-start | bytes 589832 | tf_op jit(solution)/shard_map/ppermute | solution.py:331
  219.3 21.4 %collective-permute-start.50 = (f32[2,96,128]{2,1,0:T(8,128)S(1)}, f32[2,96,128]{2,1,0:T(8,128)S(1)}, u32[]{:S(2)}, u32[]{:S(2)}) collective-permute-start(f32[2,96,128]{2,1,0:T(8,128)S(1)} %get-tuple-element.64), channel_id=1, source_target_pairs={{0,1},{1,0},{2,3},{3,2},{4,5},{5,4},{6,7},{7,6},{8,9},{9,8},{10,11... | collective-permute-start | bytes 294920 | tf_op jit(solution)/shard_map/ppermute | solution.py:332
  221.3 19.4 %collective-permute-start.52 = (f32[2,96,128]{2,1,0:T(8,128)S(1)}, f32[2,96,128]{2,1,0:T(8,128)S(1)}, u32[]{:S(2)}, u32[]{:S(2)}) collective-permute-start(f32[2,96,128]{2,1,0:T(8,128)S(1)} %add.19), channel_id=1, source_target_pairs={{0,2},{1,3},{2,0},{3,1},{4,6},{5,7},{6,4},{7,5},{8,10},{9,11},{10,... | collective-permute-start | bytes 294920 | tf_op jit(solution)/shard_map/ppermute | solution.py:331
